TPU v7x, 256 devices: a whole 4x4x8 slice. The times are simulated.
256 devices in a mesh: rep: 1, dp: 256 (over x, y, z, core).
Axes of the slice: x: 4, y: 4, z: 8, core: 2. Of those that a mesh axis runs over, the one named last changes fastest.
Arguments:
- x: bfloat16 [256, 1024, 1024], P(('rep', 'dp'))
- dy: bfloat16 [256, 1024, 1024], P(('rep', 'dp'))
- w_gate: bfloat16 [2, 1024, 3328], replicated
- w_up: bfloat16 [2, 1024, 3328], replicated
- w_down: bfloat16 [2, 3328, 1024], replicated
- m_w_gate: float32 [2, 1024, 3328], P(None, 'dp')
- m_w_up: float32 [2, 1024, 3328], P(None, 'dp')
- m_w_down: float32 [2, 3328, 1024], P(None, 'dp')
- v_w_gate: float32 [2, 1024, 3328], P(None, 'dp')
- v_w_up: float32 [2, 1024, 3328], P(None, 'dp')
- v_w_down: float32 [2, 3328, 1024], P(None, 'dp')
Outputs:
- output 1: bfloat16 [2, 1024, 3328], P('rep')
- output 2: bfloat16 [2, 1024, 3328], P('rep')
- output 3: bfloat16 [2, 3328, 1024], P('rep')
- output 4: float32 [2, 1024, 3328], P('rep', 'dp')
- output 5: float32 [2, 1024, 3328], P('rep', 'dp')
- output 6: float32 [2, 3328, 1024], P('rep', 'dp')
- output 7: float32 [2, 1024, 3328], P('rep', 'dp')
- output 8: float32 [2, 1024, 3328], P('rep', 'dp')
- output 9: float32 [2, 3328, 1024], P('rep', 'dp')
All inputs are finite; a program needn't handle non-finite values.
Results may differ from a plain program's by a relative error of at most 0.022.
Values are sent between devices in bfloat16 or wider.
A program may use at most 768 MiB of HBM per device.

v0:
```python
import jax
import jax.numpy as jnp
from jax import lax

NAMES = ("w_gate", "w_up", "w_down")


def matmul(a, w):
    return jnp.dot(a, w, preferred_element_type=jnp.float32).astype(jnp.bfloat16)


def normed(h):
    wide = h.astype(jnp.float32)
    scale = lax.rsqrt(jnp.mean(wide**2, -1, keepdims=True) + 1e-6)
    return (wide * scale).astype(jnp.bfloat16)


def layer(h, w):
    a = normed(h)
    gate = jnp.dot(a, w["w_gate"], preferred_element_type=jnp.float32)
    up = jnp.dot(a, w["w_up"], preferred_element_type=jnp.float32)
    return h + matmul((jax.nn.silu(gate) * up).astype(jnp.bfloat16), w["w_down"])


def adamw(w, m, v, g):
    m = 0.9 * m + 0.1 * g
    v = 0.95 * v + 0.05 * g * g
    step = m * lax.rsqrt(v + 1e-8) + 0.1 * w
    return (w - 0.02 * step).astype(jnp.bfloat16), m, v


def clipped(gradients, sum_of_squares, count):
    factor = jnp.minimum(1.0, 0.5 * lax.rsqrt(sum_of_squares / count + 1e-30))
    return [g * factor for g in gradients]


def stack(weights, h):
    for number in range(weights["w_gate"].shape[0]):
        h = layer(h, {name: w[number] for name, w in weights.items()})
    return h


def solution(mesh):
    groups = mesh.shape["rep"]

    def step(x, dy, *arrays):
        weights, m, v = (arrays[i : i + 3] for i in (0, 3, 6))
        x, dy = (t.reshape(groups, -1, *t.shape[1:]) for t in (x, dy))

        def of_a_group(x, dy):
            _, back = jax.vjp(lambda w: stack(w, x), dict(zip(NAMES, weights, strict=True)))
            by_weights = back(dy)[0]
            gradients = [by_weights[name].astype(jnp.float32) for name in NAMES]
            gradients = clipped(gradients, sum(jnp.sum(g * g) for g in gradients), sum(g.size for g in gradients))
            new = [adamw(w.astype(jnp.float32), m, v, g) for w, m, v, g in zip(weights, m, v, gradients, strict=True)]
            return tuple(one[which] for which in range(3) for one in new)

        return tuple(t.reshape(-1, *t.shape[2:]) for t in jax.vmap(of_a_group)(x, dy))

    return step
```

profile of v0, /device:TPU:1, one launch (start us, length us, event | category | flops | bytes accessed | tf_op | source)
XLA Modules:
  0.0 2521.8 jit_solution(6437946965204211006)
XLA Ops:
  23.2 17.9 fusion.46
  60.3 14.1 fusion.38
  74.4 13.5 fusion.41
  102.9 14.8 fusion.26
  117.7 14.9 fusion.8
  132.5 15.8 fusion.30
  163.5 13.3 fusion.134
  176.8 729.8 %fusion.131 = (f32[1024,16]{0,1:T(8,128)S(1)}, f32[16,1024]{1,0:T(8,128)S(1)}) fusion(f32[1024,3328]{0,1:T(8,128)} %fusion.134, f32[3328,1024]{1,0:T(8,128)} %fusion.30), kind=kCustom, calls=%all-reduce-scatter.2 | all-reduce-scatter fusion | flops 8388609 | bytes 27394048
  923.9 13.1 collective-permute-start.10
  937.1 13.1 collective-permute-start.11
  955.8 14.4 collective-permute-start.12
  1169.8 13.2 collective-permute-start.7
  1209.4 13.1 collective-permute-start.48
  1222.5 13.7 collective-permute-start.49
  1248.9 13.7 collective-permute-start.51
  1262.6 13.2 collective-permute-start.52
  1275.8 13.2 collective-permute-start.53
  1288.9 13.1 collective-permute-start.54
  1380.9 18.3 fusion.12
  1399.2 13.3 collective-permute-start.60
  1429.4 15.4 fusion.4
  1464.8 15.0 fusion.24
  1529.2 415.0 %all-reduce.22 = (bf16[3328,1024]{0,1:T(8,128)(2,1)}, bf16[3328,1024]{0,1:T(8,128)(2,1)}, bf16[3328,1024]{0,1:T(8,128)(2,1)}, bf16[3328,1024]{0,1:T(8,128)(2,1)}) all-reduce(f32[3328,1024]{0,1:T(8,128)} %fusion.12, f32[3328,1024]{0,1:T(8,128)} %fusion.79, f32[3328,1024]{0,1:T(8,128)} %fusion.4, ...), channel_id=17, replica_groups=mesh['axis_0'=256] {'axis_0'}, use_global_device_ids=true, to_apply=%add.1.clone.clone | all-reduce | flops 13631488 | bytes 81788928
  1991.7 19.9 concatenate
  2019.8 37.4 %concatenate.1 = bf16[1024,781]{0,1:T(8,128)(2,1)S(1)} concatenate(bf16[1024,13]{0,1:T(8,128)(2,1)S(1)} %collective-permute-done.95, bf16[1024,16]{0,1:T(8,128)(2,1)S(1)} %collective-permute-done.94, bf16[1024,16]{0,1:T(8,128)(2,1)S(1)} %collective-permute-done.93, bf16[1024,16]{0,1:T(8,128)(2,1)S(1)} %collective-permute-done.92, bf16[1024,16]{0,1:T(8,128)(2,1)S(1)} %collective-permute-done.91, ...), dimensions={1} | concatenate | bytes 3231744
  2058.6 76.1 %all-reduce.10 = f32[]{:T(128)} all-reduce(f32[]{:T(128)S(6)} %add.102), channel_id=3, replica_groups=mesh['rep'=1,'dp'=256] {'dp'}, use_global_device_ids=true, to_apply=%region_3.4.clone | all-reduce | flops 1 | bytes 8 | tf_op jit(solution)/vmap()/reduce_sum | solution.py:54
  2143.6 112.1 %all-gather.14.cloned.1.call-done = bf16[1,2,3328,1024]{3,1,0,2:T(2,128)(2,1)} async-done(((bf16[1,2,13,1024]{3,1,0,2:T(2,128)(2,1)}), bf16[1,2,3328,1024]{3,1,0,2:T(2,128)(2,1)}) %all-gather.14.cloned.1.call-update) | async-done | bytes 13631504 | tf_op jit(solution)/reshape | solution.py:58
  2255.7 14.7 copy.15
  2270.4 108.0 %all-gather.12.cloned.1.call-done = bf16[1,2,1024,3328]{3,1,0,2:T(2,128)(2,1)} async-done(((bf16[1,2,4,3328]{3,1,0,2:T(2,128)(2,1)}), bf16[1,2,1024,3328]{3,1,0,2:T(2,128)(2,1)}) %all-gather.12.cloned.1.call-update) | async-done | bytes 13631504 | tf_op jit(solution)/reshape | solution.py:58
  2378.5 13.6 copy.14
  2392.0 109.2 %all-gather.10.cloned.1.call-done = bf16[1,2,1024,3328]{3,1,0,2:T(2,128)(2,1)} async-done(((bf16[1,2,4,3328]{3,1,0,2:T(2,128)(2,1)}), bf16[1,2,1024,3328]{3,1,0,2:T(2,128)(2,1)}) %all-gather.10.cloned.1.call-update) | async-done | bytes 13631504 | tf_op jit(solution)/reshape | solution.py:58
  2501.2 13.6 copy.13
  (369 shorter events, 553.1 us)
Async XLA Ops:
  7.2 2248.5 %all-gather.14.cloned.1.call-start = ((), (), s32[]{:S(2)}) async-start(), calls=%async_computation.2 | async-start | bytes 13684736 | tf_op jit(solution)/reshape | solution.py:58
  906.7 43.5 %collective-permute-start.47 = (bf16[13,1024]{1,0:T(8,128)(2,1)S(1)}, bf16[13,1024]{1,0:T(8,128)(2,1)S(1)}, u32[]{:S(2)}, u32[]{:S(2)}) collective-permute-start(bf16[13,1024]{1,0:T(8,128)(2,1)S(1)} %slice.24), channel_id=1, source_target_pairs={{0,48},{1,49},{2,50},{3,51},{4,52},{5,53},{6,54},{7,55},{8,56},{9,... | collective-permute-start | bytes 79880
  908.0 62.1 %collective-permute-start = (bf16[16,1024]{1,0:T(8,128)(2,1)S(1)}, bf16[16,1024]{1,0:T(8,128)(2,1)S(1)}, u32[]{:S(2)}, u32[]{:S(2)}) collective-permute-start(bf16[16,1024]{1,0:T(8,128)(2,1)S(1)} %convert.221), channel_id=1, source_target_pairs={{0,1},{1,2},{2,3},{3,4},{4,5},{5,6},{6,7},{7,8},{8,9},{9,10},{10,1... | collective-permute-start | bytes 98312
  910.8 65.6 %collective-permute-start.1 = (bf16[16,1024]{1,0:T(8,128)(2,1)S(1)}, bf16[16,1024]{1,0:T(8,128)(2,1)S(1)}, u32[]{:S(2)}, u32[]{:S(2)}) collective-permute-start(bf16[16,1024]{1,0:T(8,128)(2,1)S(1)} %convert.221), channel_id=1, source_target_pairs={{0,2},{1,3},{2,4},{3,5},{4,6},{5,7},{6,8},{7,9},{8,10},{9,11},{10,... | collective-permute-start | bytes 98312
  923.9 56.2 %collective-permute-start.10 = (bf16[16,1024]{1,0:T(8,128)(2,1)S(1)}, bf16[16,1024]{1,0:T(8,128)(2,1)S(1)}, u32[]{:S(2)}, u32[]{:S(2)}) collective-permute-start(bf16[16,1024]{1,0:T(8,128)(2,1)S(1)} %convert.221), channel_id=1, source_target_pairs={{0,11},{1,12},{2,13},{3,14},{4,15},{5,16},{6,17},{7,18},{8,19},{9,... | collective-permute-start | bytes 98312
  937.1 46.2 %collective-permute-start.11 = (bf16[16,1024]{1,0:T(8,128)(2,1)S(1)}, bf16[16,1024]{1,0:T(8,128)(2,1)S(1)}, u32[]{:S(2)}, u32[]{:S(2)}) collective-permute-start(bf16[16,1024]{1,0:T(8,128)(2,1)S(1)} %convert.221), channel_id=1, source_target_pairs={{0,12},{1,13},{2,14},{3,15},{4,16},{5,17},{6,18},{7,19},{8,20},{9,... | collective-permute-start | bytes 98312
  1148.6 47.6 %collective-permute-start.46 = (bf16[16,1024]{1,0:T(8,128)(2,1)S(1)}, bf16[16,1024]{1,0:T(8,128)(2,1)S(1)}, u32[]{:S(2)}, u32[]{:S(2)}) collective-permute-start(bf16[16,1024]{1,0:T(8,128)(2,1)S(1)} %convert.221), channel_id=1, source_target_pairs={{0,47},{1,48},{2,49},{3,50},{4,51},{5,52},{6,53},{7,54},{8,55},{9,... | collective-permute-start | bytes 98312
  1150.8 58.5 %collective-permute-start.5 = (bf16[16,1024]{1,0:T(8,128)(2,1)S(1)}, bf16[16,1024]{1,0:T(8,128)(2,1)S(1)}, u32[]{:S(2)}, u32[]{:S(2)}) collective-permute-start(bf16[16,1024]{1,0:T(8,128)(2,1)S(1)} %convert.221), channel_id=1, source_target_pairs={{0,6},{1,7},{2,8},{3,9},{4,10},{5,11},{6,12},{7,13},{8,14},{9,15},... | collective-permute-start | bytes 98312
  1156.0 66.5 %collective-permute-start.6 = (bf16[16,1024]{1,0:T(8,128)(2,1)S(1)}, bf16[16,1024]{1,0:T(8,128)(2,1)S(1)}, u32[]{:S(2)}, u32[]{:S(2)}) collective-permute-start(bf16[16,1024]{1,0:T(8,128)(2,1)S(1)} %convert.221), channel_id=1, source_target_pairs={{0,7},{1,8},{2,9},{3,10},{4,11},{5,12},{6,13},{7,14},{8,15},{9,16}... | collective-permute-start | bytes 98312
  1169.8 66.4 %collective-permute-start.7 = (bf16[16,1024]{1,0:T(8,128)(2,1)S(1)}, bf16[16,1024]{1,0:T(8,128)(2,1)S(1)}, u32[]{:S(2)}, u32[]{:S(2)}) collective-permute-start(bf16[16,1024]{1,0:T(8,128)(2,1)S(1)} %convert.221), channel_id=1, source_target_pairs={{0,8},{1,9},{2,10},{3,11},{4,12},{5,13},{6,14},{7,15},{8,16},{9,17... | collective-permute-start | bytes 98312
  1183.1 65.8 %collective-permute-start.8 = (bf16[16,1024]{1,0:T(8,128)(2,1)S(1)}, bf16[16,1024]{1,0:T(8,128)(2,1)S(1)}, u32[]{:S(2)}, u32[]{:S(2)}) collective-permute-start(bf16[16,1024]{1,0:T(8,128)(2,1)S(1)} %convert.221), channel_id=1, source_target_pairs={{0,9},{1,10},{2,11},{3,12},{4,13},{5,14},{6,15},{7,16},{8,17},{9,1... | collective-permute-start | bytes 98312
  1196.2 66.4 %collective-permute-start.9 = (bf16[16,1024]{1,0:T(8,128)(2,1)S(1)}, bf16[16,1024]{1,0:T(8,128)(2,1)S(1)}, u32[]{:S(2)}, u32[]{:S(2)}) collective-permute-start(bf16[16,1024]{1,0:T(8,128)(2,1)S(1)} %convert.221), channel_id=1, source_target_pairs={{0,10},{1,11},{2,12},{3,13},{4,14},{5,15},{6,16},{7,17},{8,18},{9,... | collective-permute-start | bytes 98312
  1209.4 66.4 %collective-permute-start.48 = (bf16[1024,16]{0,1:T(8,128)(2,1)}, bf16[1024,16]{0,1:T(8,128)(2,1)}, u32[]{:S(2)}, u32[]{:S(2)}) collective-permute-start(bf16[1024,16]{0,1:T(8,128)(2,1)} %convert.222), channel_id=1, source_target_pairs={{0,1},{1,2},{2,3},{3,4},{4,5},{5,6},{6,7},{7,8},{8,9},{9,10},{10,1... | collective-permute-start | bytes 98312
  1222.5 66.4 %collective-permute-start.49 = (bf16[1024,16]{0,1:T(8,128)(2,1)}, bf16[1024,16]{0,1:T(8,128)(2,1)}, u32[]{:S(2)}, u32[]{:S(2)}) collective-permute-start(bf16[1024,16]{0,1:T(8,128)(2,1)} %convert.222), channel_id=1, source_target_pairs={{0,2},{1,3},{2,4},{3,5},{4,6},{5,7},{6,8},{7,9},{8,10},{9,11},{10,... | collective-permute-start | bytes 98312
  1236.3 78.9 %collective-permute-start.50 = (bf16[1024,16]{0,1:T(8,128)(2,1)}, bf16[1024,16]{0,1:T(8,128)(2,1)S(1)}, u32[]{:S(2)}, u32[]{:S(2)}) collective-permute-start(bf16[1024,16]{0,1:T(8,128)(2,1)} %convert.222), channel_id=1, source_target_pairs={{0,3},{1,4},{2,5},{3,6},{4,7},{5,8},{6,9},{7,10},{8,11},{9,12},{10... | collective-permute-start | bytes 98312
  1248.9 79.4 %collective-permute-start.51 = (bf16[1024,16]{0,1:T(8,128)(2,1)}, bf16[1024,16]{0,1:T(8,128)(2,1)}, u32[]{:S(2)}, u32[]{:S(2)}) collective-permute-start(bf16[1024,16]{0,1:T(8,128)(2,1)} %convert.222), channel_id=1, source_target_pairs={{0,4},{1,5},{2,6},{3,7},{4,8},{5,9},{6,10},{7,11},{8,12},{9,13},{1... | collective-permute-start | bytes 98312
  1262.6 78.8 %collective-permute-start.52 = (bf16[1024,16]{0,1:T(8,128)(2,1)}, bf16[1024,16]{0,1:T(8,128)(2,1)}, u32[]{:S(2)}, u32[]{:S(2)}) collective-permute-start(bf16[1024,16]{0,1:T(8,128)(2,1)} %convert.222), channel_id=1, source_target_pairs={{0,5},{1,6},{2,7},{3,8},{4,9},{5,10},{6,11},{7,12},{8,13},{9,14},{... | collective-permute-start | bytes 98312
  1275.8 78.8 %collective-permute-start.53 = (bf16[1024,16]{0,1:T(8,128)(2,1)}, bf16[1024,16]{0,1:T(8,128)(2,1)}, u32[]{:S(2)}, u32[]{:S(2)}) collective-permute-start(bf16[1024,16]{0,1:T(8,128)(2,1)} %convert.222), channel_id=1, source_target_pairs={{0,6},{1,7},{2,8},{3,9},{4,10},{5,11},{6,12},{7,13},{8,14},{9,15},... | collective-permute-start | bytes 98312
  1288.9 78.8 %collective-permute-start.54 = (bf16[1024,16]{0,1:T(8,128)(2,1)}, bf16[1024,16]{0,1:T(8,128)(2,1)}, u32[]{:S(2)}, u32[]{:S(2)}) collective-permute-start(bf16[1024,16]{0,1:T(8,128)(2,1)} %convert.222), channel_id=1, source_target_pairs={{0,7},{1,8},{2,9},{3,10},{4,11},{5,12},{6,13},{7,14},{8,15},{9,16}... | collective-permute-start | bytes 98312
  1315.8 83.4 %collective-permute-start.55 = (bf16[1024,16]{0,1:T(8,128)(2,1)}, bf16[1024,16]{0,1:T(8,128)(2,1)S(1)}, u32[]{:S(2)}, u32[]{:S(2)}) collective-permute-start(bf16[1024,16]{0,1:T(8,128)(2,1)} %convert.222), channel_id=1, source_target_pairs={{0,8},{1,9},{2,10},{3,11},{4,12},{5,13},{6,14},{7,15},{8,16},{9,17... | collective-permute-start | bytes 98312
  1328.3 84.1 %collective-permute-start.56 = (bf16[1024,16]{0,1:T(8,128)(2,1)}, bf16[1024,16]{0,1:T(8,128)(2,1)S(1)}, u32[]{:S(2)}, u32[]{:S(2)}) collective-permute-start(bf16[1024,16]{0,1:T(8,128)(2,1)} %convert.222), channel_id=1, source_target_pairs={{0,9},{1,10},{2,11},{3,12},{4,13},{5,14},{6,15},{7,16},{8,17},{9,1... | collective-permute-start | bytes 98312
  1341.5 77.2 %collective-permute-start.57 = (bf16[1024,16]{0,1:T(8,128)(2,1)}, bf16[1024,16]{0,1:T(8,128)(2,1)S(1)}, u32[]{:S(2)}, u32[]{:S(2)}) collective-permute-start(bf16[1024,16]{0,1:T(8,128)(2,1)} %convert.222), channel_id=1, source_target_pairs={{0,10},{1,11},{2,12},{3,13},{4,14},{5,15},{6,16},{7,17},{8,18},{9,... | collective-permute-start | bytes 98312
  1354.6 67.8 %collective-permute-start.58 = (bf16[1024,16]{0,1:T(8,128)(2,1)}, bf16[1024,16]{0,1:T(8,128)(2,1)S(1)}, u32[]{:S(2)}, u32[]{:S(2)}) collective-permute-start(bf16[1024,16]{0,1:T(8,128)(2,1)} %convert.222), channel_id=1, source_target_pairs={{0,11},{1,12},{2,13},{3,14},{4,15},{5,16},{6,17},{7,18},{8,19},{9,... | collective-permute-start | bytes 98312
  1367.7 57.9 %collective-permute-start.59 = (bf16[1024,16]{0,1:T(8,128)(2,1)}, bf16[1024,16]{0,1:T(8,128)(2,1)S(1)}, u32[]{:S(2)}, u32[]{:S(2)}) collective-permute-start(bf16[1024,16]{0,1:T(8,128)(2,1)} %convert.222), channel_id=1, source_target_pairs={{0,12},{1,13},{2,14},{3,15},{4,16},{5,17},{6,18},{7,19},{8,20},{9,... | collective-permute-start | bytes 98312
  1399.2 45.7 %collective-permute-start.60 = (bf16[1024,16]{0,1:T(8,128)(2,1)}, bf16[1024,16]{0,1:T(8,128)(2,1)S(1)}, u32[]{:S(2)}, u32[]{:S(2)}) collective-permute-start(bf16[1024,16]{0,1:T(8,128)(2,1)} %convert.222), channel_id=1, source_target_pairs={{0,13},{1,14},{2,15},{3,16},{4,17},{5,18},{6,19},{7,20},{8,21},{9,... | collective-permute-start | bytes 98312
  1521.9 422.3 %collective-permute-start.75 = (bf16[1024,16]{0,1:T(8,128)(2,1)}, bf16[1024,16]{0,1:T(8,128)(2,1)S(1)}, u32[]{:S(2)}, u32[]{:S(2)}) collective-permute-start(bf16[1024,16]{0,1:T(8,128)(2,1)} %convert.222), channel_id=1, source_target_pairs={{0,28},{1,29},{2,30},{3,31},{4,32},{5,33},{6,34},{7,35},{8,36},{9,... | collective-permute-start | bytes 98312
  1523.4 427.6 %collective-permute-start.76 = (bf16[1024,16]{0,1:T(8,128)(2,1)}, bf16[1024,16]{0,1:T(8,128)(2,1)S(1)}, u32[]{:S(2)}, u32[]{:S(2)}) collective-permute-start(bf16[1024,16]{0,1:T(8,128)(2,1)} %convert.222), channel_id=1, source_target_pairs={{0,29},{1,30},{2,31},{3,32},{4,33},{5,34},{6,35},{7,36},{8,37},{9,... | collective-permute-start | bytes 98312
  1524.7 429.9 %collective-permute-start.77 = (bf16[1024,16]{0,1:T(8,128)(2,1)}, bf16[1024,16]{0,1:T(8,128)(2,1)S(1)}, u32[]{:S(2)}, u32[]{:S(2)}) collective-permute-start(bf16[1024,16]{0,1:T(8,128)(2,1)} %convert.222), channel_id=1, source_target_pairs={{0,30},{1,31},{2,32},{3,33},{4,34},{5,35},{6,36},{7,37},{8,38},{9,... | collective-permute-start | bytes 98312
  1526.0 431.7 %collective-permute-start.78 = (bf16[1024,16]{0,1:T(8,128)(2,1)}, bf16[1024,16]{0,1:T(8,128)(2,1)S(1)}, u32[]{:S(2)}, u32[]{:S(2)}) collective-permute-start(bf16[1024,16]{0,1:T(8,128)(2,1)} %convert.222), channel_id=1, source_target_pairs={{0,31},{1,32},{2,33},{3,34},{4,35},{5,36},{6,37},{7,38},{8,39},{9,... | collective-permute-start | bytes 98312
  1527.7 434.8 %collective-permute-start.79 = (bf16[1024,16]{0,1:T(8,128)(2,1)}, bf16[1024,16]{0,1:T(8,128)(2,1)S(1)}, u32[]{:S(2)}, u32[]{:S(2)}) collective-permute-start(bf16[1024,16]{0,1:T(8,128)(2,1)} %convert.222), channel_id=1, source_target_pairs={{0,32},{1,33},{2,34},{3,35},{4,36},{5,37},{6,38},{7,39},{8,40},{9,... | collective-permute-start | bytes 98312
  2137.2 241.3 %all-gather.12.cloned.1.call-start = ((), (), s32[]{:S(2)}) async-start(), calls=%async_computation.1 | async-start | bytes 13684736 | tf_op jit(solution)/reshape | solution.py:58
  2139.7 361.6 %all-gather.10.cloned.1.call-start = ((), (), s32[]{:S(2)}) async-start(), calls=%async_computation | async-start | bytes 13684736 | tf_op jit(solution)/reshape | solution.py:58
  (141 other events, 9198.8 us)
Sparse Core Ops, SparseCore 0:
  2137.3 118.3 all-gather.13
  2259.9 118.5 all-gather.11
  2382.6 118.5 all-gather.9
where the time goes:
time: 2540 us; the launch traced here: 2520 us
  blocking collectives  1220 us (48%)
  starting transfers between devices  593 us (23%)
  waiting for transfers between devices  332 us (13%)
  matrix products  211 us (8%)
  local copies, waits for them, and re-layouts  112 us (4%)
  other arithmetic  32.8 us (1%)
    unnamed x2, blocking collectives  1140 us
    unnamed x96, starting transfers between devices  593 us
    reshape x3, waiting for transfers between devices, step(): t.reshape(-1, *t.shape[2:])  329 us
    unnamed x159, local copies, waits for them, and re-layouts  109 us
    dot_general x5, matrix products, layer(): up = jnp.dot(a, w['w_up'], preferred_element_type=jnp.float32)  76.5 us
    reduce_sum x1, blocking collectives, of_a_group(): jnp.sum(g * g)  76.1 us
    dot_general x5, matrix products, layer(): gate = jnp.dot(a, w['w_gate'], preferred_element_type=jnp.float32)  68.5 us
    dot_general x5, matrix products, matmul(): jnp.dot(a, w, preferred_element_type=jnp.float32).astype(jnp.bfloat16)  66.3 us
  transfers between devices with their start and end apart: 99, of which 5 were waited for; matrix products, arithmetic and copies ran while one was open for 5% of the time, Pallas kernels for 0%

commit v1 on v0

v1 whole, which is shorter than its diff:
```python
import functools
import heapq
import math

import jax, jax.numpy as jnp
from jax import lax
from jax.experimental import pallas as pl
from jax.experimental.pallas import tpu as pltpu
from jax.sharding import PartitionSpec as P
MESH = pl.DeviceIdType.MESH
BF, F32 = jnp.bfloat16, jnp.float32
SIZE = {"x": 4, "y": 4, "z": 8}


def coords():
    i = lax.axis_index("dp")
    return {"x": i // 64, "y": (i // 16) % 4, "z": (i // 2) % 8, "c": i % 2}


def device(at):
    return {"dp": ((at["x"] * 4 + at["y"]) * 8 + at["z"]) * 2 + at["c"]}


def moved(at, dim, by):
    n = SIZE[dim]
    return {**at, dim: lax.rem(at[dim] + by + n, n)}


UNITS = [
    ("u", 0, 1664, "zxy"), ("g", 0, 896, "xyz"), ("g", 1664, 896, "yxz"), ("d", 0, 256, "xyz"), ("d", 512, 256, "yxz"),
    ("u", 1664, 1664, "zxy"), ("g", 896, 768, "xyz"), ("g", 2560, 768, "yxz"), ("d", 256, 256, "xyz"), ("d", 768, 256, "yxz"),
]
DEPTH = {"u": 4, "g": 8, "d": 26}
WIDTH = {"u": 3328, "g": 3328, "d": 1024}
TALL = {"u": 1, "g": 1, "d": 4}
ROWS = {"u": 4, "g": 4, "d": 16}
COUNT = 2 * 3 * 1024 * 3328
LASTDIM = {"u": "y", "g": "z", "d": "z"}
NB = 3


def sub(a, v):
    return pl.ds(13 * (v // 4) + 3 * lax.rem(v, 4), 4) if a == "d" else pl.ds(v, 1)


def view(a, order, at, level, v):
    al = slice(None)
    if level == 0:
        return {"z": (al, al, v), "x": (v,), "y": (al, v)}[order[0]]
    if level == 1:
        return {"zxy": (v, al, at["z"]), "xyz": (at["x"], v), "yxz": (v, at["y"])}[order]
    return (at["x"], sub(a, v), at["z"]) if a == "u" else (at["x"], at["y"], sub(a, v))


def plan():
    RATE, LAT, DRATE, DLAT = 46.0e3, 2.6, 550.0e3, 1.5
    block = {i: 4 * DEPTH[u[0]] * 8 * u[2] * 2 for i, u in enumerate(UNITS)}
    jobs = []
    for i, u in enumerate(UNITS):
        n = SIZE[u[3][0]]
        h = n // 2
        offs = [h] + [s * (h - k) for k in range(1, h) for s in (1, -1)] + [0]
        jobs += [(i, o) for o in offs]
    rank = {}
    for i, o in jobs:
        nth = sum(k[0] == i for k in rank)
        rank[i, o] = (i // 5) + 0.9 * nth / SIZE[UNITS[i][3][0]]
    jobs.sort(key=rank.get)
    t, arrive = 1.0, {}
    for j in jobs:
        t += block[j[0]] / DRATE
        arrive[j] = t + DLAT
    free = {}
    now = 3.0
    heap = []
    order = []
    def send(t0, link, nbytes):
        s = max(free.get(link, 0.0), t0)
        free[link] = s + nbytes / RATE
        return s + nbytes / RATE + LAT
    ring = {}
    for i, u in enumerate(UNITS):
        ring[0, i] = (u[3][0], block[i])
        ring[1, i] = (u[3][1], block[i] // 4)
    for a in "ugd":
        ring[2, a] = (LASTDIM[a], TALL[a] * 8 * WIDTH[a] * 2)
    done = {}
    seqno = [0]
    def push(t0, ev):
        seqno[0] += 1
        heapq.heappush(heap, (t0, seqno[0], ev))
    for i, u in enumerate(UNITS):
        push(arrive[i, SIZE[u[3][0]] // 2], ("start", 0, i, 0, 0))
    finished = {}
    end = None
    while heap:
        t0, _, ev = heapq.heappop(heap)
        kind, level, key, s, k = ev
        dim, nbytes = ring[level, key]
        n = SIZE[dim]
        h = n // 2
        if level == 0 and kind == "step":
            o = s * (h - k)
            if k < h and arrive[key, o] > t0 + 1e-9:
                push(arrive[key, o], ev)
                continue
        now = max(now, t0)
        order.append(ev)
        cost = 0.1 + nbytes * (4 + 2 * level) / 9.0e6
        if kind == "start":
            now += cost
            for s in (1, -1):
                push(send(now, (dim, s), nbytes // 2), ("step", level, key, s, 1))
        elif k < h:
            now += cost
            push(send(now, (dim, s), nbytes), ("step", level, key, s, k + 1))
        else:
            finished[level, key] = finished.get((level, key), 0) + 1
            if finished[level, key] == 2:
                if level == 0:
                    push(max(now, arrive[key, 0]), ("start", 1, key, 0, 0))
                elif level == 1:
                    a = UNITS[key][0]
                    done[a] = done.get(a, 0) + 1
                    if done[a] == sum(u[0] == a for u in UNITS):
                        push(now, ("start", 2, a, 0, 0))
    return jobs, order, now, free


def addsum(dst, srcs):
    def add(*at):
        acc = srcs[0][at].astype(F32)
        for s in srcs[1:]:
            acc = acc + s[at].astype(F32)
        dst[at] = acc.astype(BF)

    if len(dst.shape) == 4:

        def body(i, _):
            add(i)
            return 0
        lax.fori_loop(0, dst.shape[0], body, 0)
    else:
        add(...)


def block_shape(i, level):
    a, _, cols, _ = UNITS[i]
    return ((4, DEPTH[a], 8, cols), (DEPTH[a], 8, cols))[level]


def rs_scratch():
    sh = {}
    for a, n in (("u", 8), ("g", 8), ("d", 26)):
        sh["loc_" + a] = pltpu.VMEM((4, 4, n, 8, WIDTH[a]), BF)
        sh["stage_" + a] = pltpu.VMEM((NB, 4, DEPTH[a], 8, max(u[2] for u in UNITS if u[0] == a)), BF)
        sh["stsem_" + a] = pltpu.SemaphoreType.DMA((NB,))
        h = SIZE[LASTDIM[a]] // 2
        sh["slot2_" + a] = pltpu.VMEM((2, h, TALL[a], 8, WIDTH[a]), BF)
        sh["r2_" + a] = pltpu.SemaphoreType.DMA((2, h + 1))
        sh["s2_" + a] = pltpu.SemaphoreType.DMA((2, h + 1))
        sh["first_" + a] = pltpu.VMEM((TALL[a], 8, WIDTH[a]), BF)
        sh["red_" + a] = pltpu.VMEM((TALL[a], 8, WIDTH[a]), BF)
    for i, u in enumerate(UNITS):
        h = SIZE[u[3][0]] // 2
        sh["own_%d" % i] = pltpu.VMEM(block_shape(i, 0), BF)
        sh["slot0_%d" % i] = pltpu.VMEM((2, h) + block_shape(i, 0), BF)
        sh["slot1_%d" % i] = pltpu.VMEM((2, 2) + block_shape(i, 1), BF)
        for lv, hh in ((0, h), (1, 2)):
            sh["r%d_%d" % (lv, i)] = pltpu.SemaphoreType.DMA((2, hh + 1))
            sh["s%d_%d" % (lv, i)] = pltpu.SemaphoreType.DMA((2, hh + 1))
    sh["ownsem"] = pltpu.SemaphoreType.DMA((len(UNITS),))
    sh["dr"] = pltpu.SemaphoreType.DMA((48,))
    sh["ds"] = pltpu.SemaphoreType.DMA((48,))
    sh["ar_z"] = pltpu.VMEM((16, 8, 128), F32)
    sh["ar_p"] = pltpu.VMEM((16, 8, 128), F32)
    sh["arsem"] = pltpu.SemaphoreType.DMA((4, 16))
    for a in "ugd":
        sh["mv_" + a] = pltpu.VMEM((2, 2, ROWS[a], WIDTH[a]), F32)
        sh["w_" + a] = pltpu.VMEM((TALL[a], 8, WIDTH[a]), BF)
    sh["new_u"] = pltpu.VMEM((8, 3328), BF)
    sh["new_g"] = pltpu.VMEM((8, 3328), BF)
    sh["new_d"] = pltpu.VMEM((2, 16, 1024), BF)
    sh["mv_r"] = pltpu.SemaphoreType.DMA((3, 2, 2))
    sh["mv_s"] = pltpu.SemaphoreType.DMA((3, 2, 2))
    sh["w_s"] = pltpu.SemaphoreType.DMA((3,))
    sh["fin_r"] = pltpu.SemaphoreType.DMA((3, 2))
    sh["fin_s"] = pltpu.SemaphoreType.DMA((3, 5))
    return sh


def rs_kernel(names, *refs):
    g = {(a, l): refs[2 * j + l] for j, a in enumerate("ugd") for l in (0, 1)}
    weights = {a: refs[6 + j] for j, a in enumerate("ugd")}
    moments = {a: (refs[9 + j], refs[12 + j]) for j, a in enumerate("ugd")}
    new = {a: refs[15 + j] for j, a in enumerate("ugd")}
    new_moments = {a: (refs[18 + j], refs[21 + j]) for j, a in enumerate("ugd")}
    S = dict(zip(names, refs[24:], strict=True))
    at = coords()
    c = at["c"]
    sib = device({**at, "c": 1 - c})
    jobs, order, _, _ = plan()

    peers = [device({**at, "z": lax.rem(at["z"] + dz, 8), "c": lax.rem(c + dc, 2)}) for dz in range(8) for dc in range(2)][1:]
    peers += [device({**at, "x": lax.rem(at["x"] + dx, 4), "y": lax.rem(at["y"] + dy, 4)}) for dx in range(4) for dy in range(4)][1:]
    bar = pltpu.get_barrier_semaphore()
    for p in peers:
        pl.semaphore_signal(bar, inc=1, device_id=p, device_id_type=MESH)
    pl.semaphore_wait(bar, len(peers))

    pend = []

    def remote(src, dst, ss, rs, to):
        cp = pltpu.make_async_remote_copy(src_ref=src, dst_ref=dst, send_sem=ss, recv_sem=rs, device_id=to, device_id_type=MESH)
        cp.start()
        pend.append(cp)
        return cp

    def cols(i):
        return pl.ds(UNITS[i][1], UNITS[i][2])

    def region(ref, i, level, v):
        a, _, _, o = UNITS[i]
        idx = view(a, o, at, level, v)
        return ref.at[(*idx, *([slice(None)] * (4 - len(idx))), cols(i))]

    def pos(i, level, off):
        dim = UNITS[i][3][level] if level < 2 else LASTDIM[UNITS[i][0]]
        return lax.rem(at[dim] + off + SIZE[dim], SIZE[dim])

    moment_copies = []
    for j, a in enumerate("ugd"):
        for q in (0, 1):
            ref = moments[a][q]
            moment_copies.append(remote(ref.at[1 - c], S["mv_" + a].at[q, c], S["mv_s"].at[j, q, 0], S["mv_r"].at[j, q, 0], sib))
            cp = pltpu.make_async_copy(ref.at[c], S["mv_" + a].at[q, c], S["mv_r"].at[j, q, 1])
            cp.start()
            moment_copies.append(cp)
        w = weights[a]
        ref = w.at[c, at["x"], at["y"], sub("d", at["z"])] if a == "d" else w.at[c, at["x"], at["y"], pl.ds(at["z"], 1)]
        cp = pltpu.make_async_copy(ref, S["w_" + a], S["w_s"].at[j])
        cp.start()
        moment_copies.append(cp)

    dcopy = {}
    for j, (i, off) in enumerate(jobs):
        a = UNITS[i][0]
        dst = region(S["loc_" + a], i, 0, pos(i, 0, off))
        for cc in (0, 1):
            src = region(g[a, 1 - cc], i, 0, pos(i, 0, off))
            cp = pltpu.make_async_remote_copy(src_ref=src, dst_ref=dst, send_sem=S["ds"].at[j], recv_sem=S["dr"].at[j], device_id=sib, device_id_type=MESH)
            pl.when(c == cc)(cp.start)
        pend.append(cp)
        dcopy[i, off] = cp

    uses = {a: [] for a in "ugd"}
    for kind, level, key, s, k in order:
        if level == 0:
            h = SIZE[UNITS[key][3][0]] // 2
            if kind == "start":
                uses[UNITS[key][0]].append((key, h))
            elif k < h:
                uses[UNITS[key][0]].append((key, s * (h - k)))
    nth = {a: 0 for a in "ugd"}

    def fetch(a, n, start):
        if n >= len(uses[a]):
            return None
        i, off = uses[a][n]
        buf = S["stage_" + a].at[n % NB, :, :, :, pl.ds(0, UNITS[i][2])]
        for cc in (0, 1):
            cp = pltpu.make_async_copy(region(g[a, cc], i, 0, pos(i, 0, off)), buf, S["stsem_" + a].at[n % NB])
            if start:
                pl.when(c == cc)(cp.start)
        if not start:
            cp.wait()
        return buf
    for n in range(NB):
        for a in "ugd":
            fetch(a, n, True)

    def fetch_own(i, start):
        a = UNITS[i][0]
        for cc in (0, 1):
            cp = pltpu.make_async_copy(region(g[a, cc], i, 0, pos(i, 0, 0)), S["own_%d" % i], S["ownsem"].at[i])
            if start:
                pl.when(c == cc)(cp.start)
        if not start:
            cp.wait()

    waited = set()

    def sibling_block(i, off):
        if (i, off) not in waited:
            waited.add((i, off))
            dcopy[i, off].wait_recv()

    def operands(level, i, off):
        a, _, _, o = UNITS[i]
        v = pos(i, level, off)
        l = region(S["loc_" + a], i, level, v)
        if level == 0:
            sibling_block(i, off)
            buf = fetch(a, nth[a], False)
            assert uses[a][nth[a]] == (i, off)
            nth[a] += 1
            return [buf, l]
        h = SIZE[o[0]] // 2
        first = [S["own_%d" % i]] + [S["slot0_%d" % i].at[d, h - 1] for d in (0, 1)]
        if level == 1:
            return [l] + [f.at[v] for f in first]
        w = pos(i, 1, 0)
        return [l] + [f.at[w, sub(a, v)] for f in first] + [S["slot1_%d" % i].at[d, 1, sub(a, v)] for d in (0, 1)]

    def half(ref, which, level, a):
        if level == 2 and TALL[a] == 1:
            n = ref.shape[-1] // 2
            return ref.at[..., pl.ds(n * which, n)]
        n = ref.shape[0] // 2
        return ref.at[pl.ds(n * which, n)]

    def parts(level, key):
        if level < 2:
            return [(key, None)]
        return [(i, cols(i)) for i, u in enumerate(UNITS) if u[0] == key]

    def cut(ref, cs):
        return ref if cs is None else ref.at[..., cs]

    for kind, level, key, s, k in order:
        a = UNITS[key][0] if level < 2 else key
        dim = UNITS[key][3][level] if level < 2 else LASTDIM[a]
        h = SIZE[dim] // 2
        slot, rsem, ssem = (S["%s%d_%s" % (n, level, key)] for n in ("slot", "r", "s"))
        d = 0 if s > 0 else 1

        def send(src, dst, d, k, dim=dim, rsem=rsem, ssem=ssem):
            remote(src, dst, ssem.at[d, k], rsem.at[d, k], device(moved(at, dim, 1 - 2 * d)))

        if kind == "start":
            if level == 0:
                fetch_own(key, True)
            if level == 1:
                sibling_block(key, 0)
                fetch_own(key, False)
            if level == 2:
                dst = S["first_" + a]
            else:
                dst = region(S["loc_" + a], key, level, pos(key, level, h))
            for i, cs in parts(level, key):
                addsum(cut(dst, cs), operands(level, i, h))
            for d in (0, 1):
                send(half(dst, d, level, a), half(slot.at[d, 0], d, level, a), d, 0)
            if level == 0:
                fetch(a, nth[a] - 1 + NB, True)
            continue
        block = slot.at[d, k - 1]
        got = half(block, d, level, a) if k == 1 else block
        pltpu.make_async_remote_copy(src_ref=got, dst_ref=got, send_sem=ssem.at[d, k - 1], recv_sem=rsem.at[d, k - 1], device_id=sib, device_id_type=MESH).wait_recv()
        if k == h:
            continue
        off = s * (h - k)
        for i, cs in parts(level, key):
            ops = operands(level, i, off)
            mine = cut(block, cs)
            if k > 1:
                addsum(mine, [mine] + ops)
            elif level == 2 and TALL[a] == 1:
                inside = (UNITS[i][1] >= WIDTH[a] // 2) == (d == 1)
                addsum(mine, ([mine] if inside else []) + ops)
            else:
                for w in (0, 1):
                    hops = [half(r, w, level, a) for r in ops]
                    hm = half(mine, w, level, a)
                    addsum(hm, ([hm] if w == d else []) + hops)
        send(block, slot.at[d, k], d, k)
        if level == 0:
            fetch(a, nth[a] - 1 + NB, True)

    total = jnp.zeros((8, 128), F32)
    zz = lax.rem(at["z"], 4)
    for j, a in enumerate("ugd"):
        h = SIZE[LASTDIM[a]] // 2
        for i, cs in parts(2, a):
            ops = operands(2, i, 0) + [S["slot2_" + a].at[d, h - 1, :, :, cs] for d in (0, 1)]
            for t in range(TALL[a]):
                for q in range(UNITS[i][2] // 128):
                    acc = ops[0][t, :, q * 128:q * 128 + 128].astype(F32)
                    for o in ops[1:]:
                        acc = acc + o[t, :, q * 128:q * 128 + 128].astype(F32)
                    acc = acc.astype(BF)
                    S["red_" + a][t, :, pl.ds(UNITS[i][1] + q * 128, 128)] = acc
                    acc = acc.astype(F32)
                    if a == "d":
                        row = lax.broadcasted_iota(jnp.int32, (8, 128), 0) + 8 * t
                        acc = jnp.where((row >= 2 * zz) & (row < 2 * zz + 26), acc, 0.0)
                    total = total + acc * acc
    for r, (buf, ds) in enumerate(((S["ar_z"], [(0, 0, q // 2, q % 2) for q in range(16)]), (S["ar_p"], [(q // 4, q % 4, 0, 0) for q in range(16)]))):
        buf[0] = total
        cps = []
        for q in range(1, 16):
            dx, dy, dz, dc = ds[q]
            to = device({"x": lax.rem(at["x"] + dx, 4), "y": lax.rem(at["y"] + dy, 4), "z": lax.rem(at["z"] + dz, 8), "c": lax.rem(c + dc, 2)})
            cps.append(remote(buf.at[0], buf.at[q], S["arsem"].at[2 * r, q], S["arsem"].at[2 * r + 1, q], to))
        for cp in cps:
            cp.wait_recv()
        total = buf[0]
        for q in range(1, 16):
            total = total + buf[q]
    mean = jnp.sum(jnp.sum(total, axis=1, keepdims=True), axis=0, keepdims=True) / COUNT
    factor = jnp.minimum(1.0, 0.5 * lax.rsqrt(mean + 1e-30))
    for cp in moment_copies:
        cp.wait_recv() if cp.is_remote else cp.wait()

    def adamw(w, m, v, g):
        g = g * factor
        m = 0.9 * m + 0.1 * g
        v = 0.95 * v + 0.05 * g * g
        step = m * lax.rsqrt(v + 1e-8) + 0.1 * w
        return (w - 0.02 * step).astype(BF), m, v

    for a in "ug":
        mv, red, wv = S["mv_" + a], S["red_" + a], S["w_" + a]

        def body(q, _, mv=mv, red=red, wv=wv, a=a):
            cs = pl.ds(pl.multiple_of(q * 256, 256), 256)
            m, v = (jnp.concatenate([mv[e, 0, :, cs], mv[e, 1, :, cs]], axis=0) for e in (0, 1))
            n, m, v = adamw(wv[0, :, cs].astype(F32), m, v, red[0, :, cs].astype(F32))
            S["new_" + a][:, cs] = n
            for e, t in enumerate((m, v)):
                for s in (0, 1):
                    mv[e, s, :, cs] = t[4 * s:4 * s + 4]
            return 0
        lax.fori_loop(0, 3328 // 256, body, 0)
    row = lax.broadcasted_iota(jnp.int32, (32, 32), 0)
    column = lax.broadcasted_iota(jnp.int32, (32, 32), 1)
    pick = (column == 2 * zz + 13 * (row >> 4) + (row & 15)) & ((row & 15) < 13)
    pick = jnp.where(pick, 1.0, 0.0).astype(BF)
    gd, wd = (jnp.dot(pick, S[n][...].reshape(32, 1024), preferred_element_type=F32) for n in ("red_d", "w_d"))
    for s in (0, 1):
        rows = slice(16 * s, 16 * s + 16)
        n, m, v = adamw(wd[rows], S["mv_d"][0, s], S["mv_d"][1, s], gd[rows])
        S["new_d"][s] = n
        S["mv_d"][0, s] = m
        S["mv_d"][1, s] = v
    ends = []
    for j, a in enumerate("ugd"):
        cp = pltpu.make_async_copy(S["new_" + a], new[a], S["fin_s"].at[j, 4])
        cp.start()
        pend.append(cp)
        for q in (0, 1):
            ends.append(remote(S["mv_" + a].at[q, 1 - c], new_moments[a][q].at[c], S["fin_s"].at[j, q], S["fin_r"].at[j, q], sib))
            cp = pltpu.make_async_copy(S["mv_" + a].at[q, c], new_moments[a][q].at[c], S["fin_s"].at[j, 2 + q])
            cp.start()
            pend.append(cp)
    for cp in ends:
        cp.wait_recv()
    for cp in pend:
        cp.wait_send() if cp.is_remote else cp.wait()


def reduce_scatter(u, g, d, weights, m, v):
    args = [t.reshape(4, 4, 8, 8, 3328) for t in (*u, *g)] + [t.reshape(4, 4, 26, 8, 1024) for t in d]
    args += [w.reshape(2, 4, 4, -1, 8, w.shape[-1]) for w in weights]
    args += [*m, *v]
    sh = rs_scratch()
    any_ = pl.BlockSpec(memory_space=pl.ANY)
    outs = [jax.ShapeDtypeStruct(s, BF) for s in ((8, 3328), (8, 3328), (2, 16, 1024))] + [jax.ShapeDtypeStruct(t.shape, F32) for t in (*m, *v)]
    outs = pl.pallas_call(
        functools.partial(rs_kernel, list(sh)), out_shape=outs, in_specs=[any_] * 15, out_specs=[any_] * 9, scratch_shapes=list(sh.values()), name="reduce_scatter",
        compiler_params=pltpu.CompilerParams(collective_id=0, has_side_effects=True, vmem_limit_bytes=67043328))(*args)
    return outs[:3], outs[3:6], outs[6:]


def plan_ag():
    RATE, LAT = 46.0e3, 2.9
    free, heap, order, n_ = {}, [], [], [0]

    def push(t0, ev):
        n_[0] += 1
        heapq.heappush(heap, (t0, n_[0], ev))

    def send(t0, link, nbytes):
        s = max(free.get(link, 0.0), t0)
        free[link] = s + nbytes / RATE
        return free[link] + LAT
    ring = {(2, a): (LASTDIM[a], {"u": 8 * 3328, "g": 8 * 3328, "d": 32 * 1024}[a] * 2) for a in "ugd"}
    for i, (a, _, cols, o) in enumerate(UNITS):
        ring[1, i] = (o[1], DEPTH[a] * 8 * cols * 2)
        ring[0, i] = (o[0], 4 * DEPTH[a] * 8 * cols * 2)
    got = {}
    for a in "gdu":
        push(1.0, ("start", 2, a, 0, 0))
    now = 1.0
    while heap:
        t0, _, ev = heapq.heappop(heap)
        kind, level, key, s, k = ev
        dim, nbytes = ring[level, key]
        h = SIZE[dim] // 2
        now = max(now, t0) + 0.1
        order.append(ev)
        if kind == "start":
            for s in (1, -1):
                push(send(now, (dim, s), nbytes), ("step", level, key, s, 1))
            continue
        if k < h:
            push(send(now, (dim, s), nbytes if k < h - 1 else nbytes // 2), ("step", level, key, s, k + 1))
            continue
        got[level, key] = got.get((level, key), 0) + 1
        if got[level, key] < 2:
            continue
        if level == 2:
            for i, u in enumerate(UNITS):
                if u[0] == key:
                    push(now + (1.0 if key == "d" else 0), ("start", 1, i, 0, 0))
        elif level == 1:
            push(now, ("start", 0, key, 0, 0))
    return order, now, free


def ag_scratch():
    sh = {"pc": pltpu.VMEM((8, 2, 16, 1024), BF), "asm": pltpu.VMEM((26, 8, 1024), BF), "loc": pltpu.SemaphoreType.DMA((4,)),
          "sr": pltpu.SemaphoreType.DMA((128,)), "ss": pltpu.SemaphoreType.DMA((128,))}
    for a in "ugd":
        h = SIZE[LASTDIM[a]] // 2
        for n in "rs":
            sh["%s2_%s" % (n, a)] = pltpu.SemaphoreType.DMA((2, h))
    for i, u in enumerate(UNITS):
        for lv in (0, 1):
            for n in "rs":
                sh["%s%d_%d" % (n, lv, i)] = pltpu.SemaphoreType.DMA((2, SIZE[u[3][lv]] // 2))
    return sh


def ag_kernel(names, *refs):
    own = {a: refs[j] for j, a in enumerate("ugd")}
    outs = {a: refs[3 + j] for j, a in enumerate("ugd")}
    S = dict(zip(names, refs[6:], strict=True))
    at = coords()
    c = at["c"]
    sib = device({**at, "c": 1 - c})
    out = {a: r.at[c] for a, r in outs.items()}
    order, _, _ = plan_ag()
    peers = [sib] + [device(moved(at, d, s)) for d in "xyz" for s in (1, -1)]
    bar = pltpu.get_barrier_semaphore()
    for p in peers:
        pl.semaphore_signal(bar, inc=1, device_id=p, device_id_type=MESH)
    x, y, z = at["x"], at["y"], at["z"]
    locals_ = [pltpu.make_async_copy(own["u"], out["u"].at[x, y, z], S["loc"].at[0]), pltpu.make_async_copy(own["g"], out["g"].at[x, y, z], S["loc"].at[1]),
               pltpu.make_async_copy(own["d"], S["pc"].at[z], S["loc"].at[2])]
    for cp in locals_:
        cp.start()
    pl.semaphore_wait(bar, len(peers))
    for cp in locals_:
        cp.wait()
    pend, twin = [], []

    def remote(src, dst, ss, rs, to):
        cp = pltpu.make_async_remote_copy(src_ref=src, dst_ref=dst, send_sem=ss, recv_sem=rs, device_id=to, device_id_type=MESH)
        cp.start()
        pend.append(cp)

    def to_sibling(ref):
        n = len(twin)
        remote(ref, ref, S["ss"].at[n], S["sr"].at[n], sib)
        twin.append(ref)

    def region(level, key, v):
        if level == 2:
            return {"u": lambda: out["u"].at[x, v, z], "g": lambda: out["g"].at[x, y, v], "d": lambda: S["pc"].at[v]}[key]()
        a, col, n, o = UNITS[key]
        idx = view(a, o, at, level, v)
        return out[a].at[(*idx, *([slice(None)] * (4 - len(idx))), pl.ds(col, n))]

    def half(ref, which, level, key):
        if level == 2 and key != "d":
            return ref.at[:, pl.ds(1664 * which, 1664)]
        n = ref.shape[0] // 2
        return ref.at[pl.ds(n * which, n)]

    got = {}
    for kind, level, key, s, k in order:
        dim = UNITS[key][3][level] if level < 2 else LASTDIM[key]
        n = SIZE[dim]
        h = n // 2
        rsem, ssem = S["r%d_%s" % (level, key)], S["s%d_%s" % (level, key)]

        def send(src, d, k, dim=dim, rsem=rsem, ssem=ssem):
            remote(src, src, ssem.at[d, k], rsem.at[d, k], device(moved(at, dim, 1 - 2 * d)))

        if kind == "start":
            for d in (0, 1):
                send(region(level, key, at[dim]), d, 0)
            continue
        d = 0 if s > 0 else 1
        block = region(level, key, lax.rem(at[dim] - s * k + n, n))
        if k == h:
            block = half(block, d, level, key)
        pltpu.make_async_remote_copy(src_ref=block, dst_ref=block, send_sem=ssem.at[d, k - 1], recv_sem=rsem.at[d, k - 1], device_id=sib, device_id_type=MESH).wait_recv()
        if k < h - 1:
            send(block, d, k)
        elif k == h - 1:
            send(half(block, d, level, key), d, k)
        if level < 2:
            to_sibling(block)
        if k == h:
            got[level, key] = got.get((level, key), 0) + 1
            if level == 2 and got[level, key] == 2:
                if key == "d":
                    q = lax.broadcasted_iota(jnp.int32, (208, 256), 1)
                    r = lax.broadcasted_iota(jnp.int32, (208, 256), 0)
                    e = q & 15
                    pick = (r == 26 * (q >> 5) + 13 * ((q >> 4) & 1) + e) & (e < 13)
                    got_rows = jnp.dot(jnp.where(pick, 1.0, 0.0).astype(BF), S["pc"][...].reshape(256, 1024), preferred_element_type=F32)
                    S["asm"][...] = got_rows.reshape(26, 8, 1024).astype(BF)
                    cp = pltpu.make_async_copy(S["asm"], out["d"].at[x, y], S["loc"].at[3])
                    cp.start()
                    cp.wait()
                to_sibling({"u": lambda: out["u"].at[x, :, z], "g": lambda: out["g"].at[x, y], "d": lambda: out["d"].at[x, y]}[key]())
    for n, ref in enumerate(twin):
        other = ref
        pltpu.make_async_remote_copy(src_ref=other, dst_ref=other, send_sem=S["ss"].at[n], recv_sem=S["sr"].at[n], device_id=sib, device_id_type=MESH).wait_recv()
    for cp in pend:
        cp.wait_send()


def all_gather(u, g, d):
    sh = ag_scratch()
    any_ = pl.BlockSpec(memory_space=pl.ANY)
    outs = [jax.ShapeDtypeStruct((2, 4, 4, n, 8, w), BF) for n, w in ((8, 3328), (8, 3328), (26, 1024))]
    return pl.pallas_call(
        functools.partial(ag_kernel, list(sh)), out_shape=outs, in_specs=[any_] * 3, out_specs=[any_] * 3, scratch_shapes=list(sh.values()), name="all_gather",
        compiler_params=pltpu.CompilerParams(collective_id=1, has_side_effects=True, vmem_limit_bytes=67043328))(u, g, d)


NAMES = ("w_gate", "w_up", "w_down")


def matmul(a, w):
    return jnp.dot(a, w, preferred_element_type=F32).astype(BF)


def normed(h):
    wide = h.astype(F32)
    scale = lax.rsqrt(jnp.mean(wide**2, -1, keepdims=True) + 1e-6)
    return (wide * scale).astype(BF)


def layer(h, w):
    a = normed(h)
    gate = jnp.dot(a, w["w_gate"], preferred_element_type=F32)
    up = jnp.dot(a, w["w_up"], preferred_element_type=F32)
    return h + matmul((jax.nn.silu(gate) * up).astype(BF), w["w_down"])


def solution(mesh):
    def step(x, dy, w_gate, w_up, w_down, *moments):
        weights = [{n: w[i] for n, w in zip(NAMES, (w_gate, w_up, w_down), strict=True)} for i in (0, 1)]

        def stack(weights):
            h = x[0]
            for w in weights:
                h = layer(h, w)
            return h

        _, back = jax.vjp(stack, weights)
        grads = back(dy[0])[0]
        gate, up, down = ([grads[i][n] for i in (0, 1)] for n in NAMES)
        m, v = moments[:3], moments[3:]
        order = lambda t: (t[1], t[0], t[2])
        pad = lambda t: (*t[:2], jnp.pad(t[2], ((0, 0), (0, 3), (0, 0))))
        new, m, v = reduce_scatter(up, gate, down, order((w_gate, w_up, w_down)), pad(order(m)), pad(order(v)))
        u, g, d = all_gather(*new)
        w = (g.reshape(w_gate.shape), u.reshape(w_up.shape), d.reshape(w_down.shape))
        cut = lambda t: (t[1], t[0], t[2][:, :13])
        return (*w, *cut(m), *cut(v))

    data, whole, rows = P(("rep", "dp"), None, None), P(), P(None, "dp", None)
    out = P("rep", None, None)
    return jax.shard_map(step, mesh=mesh, in_specs=(data, data) + (whole,) * 3 + (rows,) * 6, out_specs=(out,) * 3 + (P("rep", "dp", None),) * 6, check_vma=False)
```

time: 2540 us -> 479 us (0.19)
  blocking collectives: 1220 us -> 0 us
  starting transfers between devices: 593 us -> 0 us
  waiting for transfers between devices: 332 us -> 0 us
  Pallas kernels: 0 us -> 218 us
  local copies, waits for them, and re-layouts: 112 us -> 40.4 us
  other arithmetic: 32.8 us -> 4.43 us
    unnamed x2 -> x0, blocking collectives: 1140 us -> none
    unnamed x96 -> x0, starting transfers between devices: 593 us -> none
    reshape x3 -> x0, waiting for transfers between devices: 329 us -> none  [step(): t.reshape(-1, *t.shape[2:])]
    pallas_call x0 -> x2, Pallas kernels: none -> 218 us  [the longest x1 123 us: reduce_scatter(): pl.pallas_call(functools.partial(rs_kernel, list(sh)), out_shape=outs, in...]
    reduce_sum x1 -> x0, blocking collectives: 76.1 us -> none  [of_a_group(): jnp.sum(g * g)]
    unnamed x159 -> x75, local copies, waits for them, and re-layouts: 109 us -> 39 us
  transfers between devices with their start and end apart: 99 -> 0, of which waited for: 5 -> 0; matrix products, arithmetic and copies ran while one was open for 5% -> 0% of each run, Pallas kernels for 0% -> 0%
where the time goes in v1:
time: 479 us; the launch traced here: 471 us
  Pallas kernels  218 us (46%)
  matrix products  207 us (43%)
  local copies, waits for them, and re-layouts  40.4 us (8%)
    pallas_call x1, Pallas kernels, reduce_scatter(): pl.pallas_call(functools.partial(rs_kernel, list(sh)), out_shape=outs, in...  123 us
    pallas_call x1, Pallas kernels, all_gather(): pl.pallas_call(functools.partial(ag_kernel, list(sh)), out_shape=outs, in...  95.1 us
    dot_general x5, matrix products, layer(): gate = jnp.dot(a, w['w_gate'], preferred_element_type=F32)  76.3 us
    dot_general x5, matrix products, layer(): up = jnp.dot(a, w['w_up'], preferred_element_type=F32)  73.3 us
    dot_general x5, matrix products, matmul(): return jnp.dot(a, w, preferred_element_type=F32).astype(BF)  57.7 us
    unnamed x75, local copies, waits for them, and re-layouts  39 us

profile of v1, /device:TPU:1, one launch (start us, length us, event | category | flops | bytes accessed | tf_op | source)
XLA Modules:
  0.0 471.3 jit_solution(4119340393014354984)
XLA Ops:
  0.6 2.9 copy.20
  4.0 14.0 %fusion.31 = f32[1024,3328]{1,0:T(8,128)} fusion(bf16[2,1024,3328]{2,1,0:T(8,128)(2,1)} %param.13, bf16[1,1024,1024]{2,1,0:T(8,128)(2,1)} %param.11, f32[1024]{0:T(1024)S(1)} %add_rsqrt_fusion), kind=kOutput, calls=%fused_computation.47 | convolution fusion | flops 6982467584 | bytes 22548480 | tf_op jit(solution)/shard_map/jvp()/dot_general | solution.py:651
  18.1 16.5 %multiply_convert_fusion.1 = (bf16[1024,3328]{1,0:T(8,128)(2,1)}, f32[1024,3328]{1,0:T(8,128)}) fusion(f32[1024,3328]{1,0:T(8,128)} %fusion.31, bf16[2,1024,3328]{2,1,0:T(8,128)(2,1)} %param.14, bf16[1,1024,1024]{2,1,0:T(8,128)(2,1)S(1)} %copy-done.6, f32[1024]{0:T(1024)S(1)} %add_rsqrt_fusion), kind=kOutput, calls=%fused_computation.17 | convolution fusion | flops 7002914816 | bytes 42995712 | tf_op jit(solution)/shard_map/jvp()/dot_general | solution.py:652
  34.6 11.8 %fusion.47 = (f32[1024]{0:T(1024)S(1)}, bf16[1024,1024]{0,1:T(8,128)(2,1)S(1)}) fusion(bf16[1024,3328]{1,0:T(8,128)(2,1)} %get-tuple-element.42, bf16[2,3328,1024]{2,1,0:T(8,128)(2,1)} %param.15, bf16[1,1024,1024]{1,2,0:T(8,128)(2,1)S(1)} %copy.20), kind=kOutput, calls=%fused_computation.66 | convolution fusion | flops 6984563712 | bytes 17829888 | tf_op jit(solution)/shard_map/jvp()/dot_general | solution.py:640
  46.4 14.4 %fusion.18 = f32[1024,3328]{1,0:T(8,128)} fusion(bf16[2,1024,3328]{2,1,0:T(8,128)(2,1)} %param.14, bf16[1024,1024]{0,1:T(8,128)(2,1)S(1)} %get-tuple-element.45, f32[1024]{0:T(1024)S(1)} %fusion.67), kind=kOutput, calls=%fused_computation.34 | convolution fusion | flops 6982467584 | bytes 22548480 | tf_op jit(solution)/shard_map/jvp()/dot_general | solution.py:652
  60.9 9.3 %convolution_convert_fusion.4 = bf16[1024,3328]{1,0:T(8,128)(2,1)} fusion(bf16[2,3328,1024]{2,1,0:T(8,128)(2,1)S(1)} %bitcast.80, bf16[1,1024,1024]{2,1,0:T(8,128)(2,1)S(1)} %copy-done.7), kind=kOutput, calls=%fused_computation.29 | convolution fusion | flops 6982729728 | bytes 15728640 | tf_op jit(solution)/shard_map/transpose(jvp())/dot_general | solution.py:640
  70.2 23.5 %fusion.2 = (bf16[1024,3328]{1,0:T(8,128)(2,1)}, f32[1024,3328]{1,0:T(8,128)}) fusion(f32[1024,3328]{1,0:T(8,128)} %fusion.18, bf16[1024,3328]{1,0:T(8,128)(2,1)} %convolution_convert_fusion.4, bf16[2,1024,3328]{2,1,0:T(8,128)(2,1)} %param.13, bf16[1024,1024]{0,1:T(8,128)(2,1)} %copy-done.3, f32[1024]{0:T(1024)S(1)} %fusion.67), kind=kOutput, calls=%fused_computation.8 | convolution fusion | flops 7023362048 | bytes 49811456 | tf_op jit(solution)/shard_map/jvp()/dot_general | solution.py:651
  93.7 14.7 %convolution_convert_fusion = bf16[3328,1024]{1,0:T(8,128)(2,1)} fusion(f32[1024,3328]{1,0:T(8,128)} %fusion.18, bf16[1,1024,1024]{2,1,0:T(8,128)(2,1)S(1)} %copy-done.7, f32[1024,3328]{1,0:T(8,128)} %get-tuple-element.47), kind=kOutput, calls=%fused_computation.25 | convolution fusion | flops 7003176960 | bytes 36175872 | tf_op jit(solution)/shard_map/transpose(jvp())/dot_general | solution.py:640
  108.4 14.1 %fusion.12 = bf16[1024,1024]{0,1:T(8,128)(2,1)S(1)} fusion(bf16[1024,3328]{1,0:T(8,128)(2,1)} %convolution_convert_fusion.4, bf16[2,1024,3328]{2,1,0:T(8,128)(2,1)} %param.14, f32[1024,3328]{1,0:T(8,128)} %get-tuple-element.47), kind=kOutput, calls=%fused_computation.21 | convolution fusion | flops 6999769088 | bytes 29360128 | tf_op jit(solution)/shard_map/transpose(jvp())/dot_general | solution.py:652
  122.5 12.6 %fusion.49 = (f32[1024]{0:T(1024)S(1)}, bf16[1024,1024]{0,1:T(8,128)(2,1)}) fusion(bf16[1024,1024]{0,1:T(8,128)(2,1)S(1)} %copy-done.4, bf16[1024,1024]{0,1:T(8,128)(2,1)S(1)} %fusion.12, bf16[1024,3328]{1,0:T(8,128)(2,1)} %get-tuple-element.46, bf16[2,1024,3328]{2,1,0:T(8,128)(2,1)} %param.13), kind=kOutput, calls=%fused_computation.68 | convolution fusion | flops 6984563712 | bytes 19927040 | tf_op jit(solution)/shard_map/transpose(jvp())/dot_general | solution.py:651
  135.2 2.9 copy.21
  138.0 3.9 fusion.52
  142.0 12.5 %convolution_convert_fusion.1 = bf16[3328,1024]{1,0:T(8,128)(2,1)} fusion(bf16[1024,3328]{1,0:T(8,128)(2,1)} %get-tuple-element.42, bf16[1024,1024]{0,1:T(8,128)(2,1)S(1)} %fusion.52), kind=kOutput, calls=%fused_computation.26 | convolution fusion | flops 6982729728 | bytes 15728640 | tf_op jit(solution)/shard_map/transpose(jvp())/dot_general | solution.py:640
  154.6 9.3 %convolution_convert_fusion.2 = bf16[1024,3328]{1,0:T(8,128)(2,1)} fusion(bf16[1024,3328]{1,0:T(8,128)(2,1)S(1)} %bitcast.97, bf16[1024,1024]{0,1:T(8,128)(2,1)S(1)} %copy-done.5, f32[1024]{0:T(1024)S(1)} %fusion.67), kind=kOutput, calls=%fused_computation.27 | convolution fusion | flops 6982467584 | bytes 15732736 | tf_op jit(solution)/shard_map/transpose(jvp())/dot_general | solution.py:651
  163.9 9.4 %convolution_convert_fusion.3 = bf16[1024,3328]{1,0:T(8,128)(2,1)} fusion(bf16[1024,1024]{0,1:T(8,128)(2,1)S(1)} %fusion.52, bf16[2,3328,1024]{2,1,0:T(8,128)(2,1)S(1)} %bitcast.82), kind=kOutput, calls=%fused_computation.28 | convolution fusion | flops 6982729728 | bytes 15728640 | tf_op jit(solution)/shard_map/transpose(jvp())/dot_general | solution.py:640
  173.3 16.9 %fusion.14 = bf16[1024,3328]{1,0:T(8,128)(2,1)} fusion(f32[1024,3328]{1,0:T(8,128)} %fusion.31, f32[1024,3328]{1,0:T(8,128)} %get-tuple-element.43, bf16[1024,3328]{1,0:T(8,128)(2,1)} %convolution_convert_fusion.3, bf16[1,1024,1024]{1,2,0:T(8,128)(2,1)S(1)} %copy-done.2, f32[1024]{0:T(1024)S(1)} %copy-done.15), kind=kOutput, calls=%fused_computation.23 | convolution fusion | flops 7023362048 | bytes 42995712 | tf_op jit(solution)/shard_map/transpose(jvp())/dot_general | solution.py:651
  190.2 15.1 %fusion.13 = bf16[1024,3328]{1,0:T(8,128)(2,1)} fusion(bf16[1024,3328]{1,0:T(8,128)(2,1)} %convolution_convert_fusion.4, bf16[1024,1024]{0,1:T(8,128)(2,1)} %copy-done.3, f32[1024]{0:T(1024)S(1)} %fusion.67, f32[1024,3328]{1,0:T(8,128)} %get-tuple-element.47), kind=kOutput, calls=%fused_computation.22 | convolution fusion | flops 7006322688 | bytes 29364224 | tf_op jit(solution)/shard_map/transpose(jvp())/dot_general | solution.py:652
  205.4 13.2 %fusion.17 = bf16[1024,3328]{1,0:T(8,128)(2,1)} fusion(bf16[1024,3328]{1,0:T(8,128)(2,1)S(1)} %copy-done.16, f32[1024,3328]{1,0:T(8,128)} %fusion.31, bf16[1,1024,1024]{1,2,0:T(8,128)(2,1)S(1)} %copy-done.2, f32[1024]{0:T(1024)S(1)} %copy-done.15), kind=kOutput, calls=%fused_computation.24 | convolution fusion | flops 7006322688 | bytes 29364224 | tf_op jit(solution)/shard_map/transpose(jvp())/dot_general | solution.py:652
  218.6 0.7 pad.7.refs_11_
  219.3 0.7 pad.8.refs_14_
  220.0 122.7 %reduce_scatter.1 = (bf16[8,3328]{1,0:T(8,128)(2,1)}, bf16[8,3328]{1,0:T(8,128)(2,1)}, bf16[2,16,1024]{2,1,0:T(8,128)(2,1)}, f32[2,4,3328]{2,1,0:T(4,128)}, f32[...) custom-call(bf16[4,4,8,8,3328]{4,3,2,1,0:T(8,128)(2,1)} %bitcast.93,, ...), custom_call_target="tpu_custom_call" | custom-call | tf_op jit(solution)/shard_map/reduce_scatter/pallas_call | solution.py:469
  342.6 95.1 %all_gather.1 = (bf16[2,4,4,8,8,3328]{5,4,3,2,1,0:T(8,128)(2,1)}, bf16[2,4,4,8,8,3328]{5,4,3,2,1,0:T(8,128)(2,1)}, bf16[2,4,4,26,8,1024]{5,4,3,2,1,0:T(8,128)(2,1)}) custom-call(bf16[8,3328]{1,0:T(8,128)(2,1)} %get-tuple-element.21.refs_0_, bf16[8,3328]{1,0:T(8,128)(2,1)} %get-tuple-element.22.refs_1_, bf16[2,16,1024]{2,1,0:T(8,128)(2,1)} %get-tuple-element.23.refs_2_), custom_call_target="tpu_custom_call" | custom-call | tf_op jit(solution)/shard_map/all_gather/pallas_call | solution.py:631
  437.7 1.6 copy.24
  439.4 1.6 copy.25
  441.0 15.1 %copy.33 = bf16[2,1024,3328]{2,1,0:T(8,128)(2,1)} copy(bf16[2,1024,3328]{2,1,0:T(8,128)(2,1)} %bitcast.87) | data formatting | bytes 27262976
  456.1 6.6 %copy.34 = bf16[2,1024,3328]{2,1,0:T(8,128)(2,1)} copy(bf16[2,1024,3328]{2,1,0:T(8,128)(2,1)S(1)} %bitcast.86) | data formatting | bytes 27262976
  462.7 0.5 slice-done.11
  463.2 5.1 %copy.35 = bf16[2,3328,1024]{2,1,0:T(8,128)(2,1)} copy(bf16[2,3328,1024]{2,1,0:T(8,128)(2,1)S(1)} %bitcast.85) | data formatting | bytes 27262976
  468.3 0.6 copy.36
  468.9 0.6 copy.37
  469.6 0.6 copy.38
  470.2 0.6 copy.39
  (71 shorter events, 0.7 us)
Async XLA Ops:
  3.5 31.1 %copy-start.1 = (bf16[1,1024,1024]{1,2,0:T(8,128)(2,1)}, bf16[1,1024,1024]{1,2,0:T(8,128)(2,1)S(1)}, u32[]{:S(2)}) copy-start(bf16[1,1024,1024]{1,2,0:T(8,128)(2,1)S(1)} %copy.20) | copy-start | bytes 6291460
  4.0 14.0 %copy-start.14 = (f32[1024]{0:T(1024)}, f32[1024]{0:T(1024)S(1)}, u32[]{:S(2)}) copy-start(f32[1024]{0:T(1024)S(1)} %add_rsqrt_fusion) | copy-start | bytes 12292
  4.0 14.0 %copy-start.6 = (bf16[1,1024,1024]{2,1,0:T(8,128)(2,1)S(1)}, bf16[1,1024,1024]{2,1,0:T(8,128)(2,1)}, u32[]{:S(2)}) copy-start(bf16[1,1024,1024]{2,1,0:T(8,128)(2,1)} %param.11) | copy-start | bytes 6291460
  34.6 26.3 %slice-start = ((s8[13631488]{0:T(1024)(128)(4,1)}), s8[4194304]{0:T(1024)(128)(4,1)S(1)}, s32[]{:S(2)}) async-start(s8[13631488]{0:T(1024)(128)(4,1)} %bitcast.79), calls=%async_computation | async-start | bytes 8388608
  34.6 26.3 %slice-start.1 = ((s8[13631488]{0:T(1024)(128)(4,1)}), s8[4194304]{0:T(1024)(128)(4,1)S(1)}, s32[]{:S(2)}) async-start(s8[13631488]{0:T(1024)(128)(4,1)} %bitcast.79), calls=%async_computation.1 | async-start | bytes 8388608
  34.6 26.3 %slice-start.2 = ((s8[13631488]{0:T(1024)(128)(4,1)}), s8[1048576]{0:T(1024)(128)(4,1)S(1)}, s32[]{:S(2)}) async-start(s8[13631488]{0:T(1024)(128)(4,1)} %bitcast.79), calls=%async_computation.2 | async-start | bytes 2097152
  46.4 14.5 %copy-start.3 = (bf16[1024,1024]{0,1:T(8,128)(2,1)}, bf16[1024,1024]{0,1:T(8,128)(2,1)S(1)}, u32[]{:S(2)}) copy-start(bf16[1024,1024]{0,1:T(8,128)(2,1)S(1)} %get-tuple-element.45) | copy-start | bytes 6291460
  46.4 14.5 %slice-start.3 = ((s8[13631488]{0:T(1024)(128)(4,1)}), s8[4194304]{0:T(1024)(128)(4,1)S(1)}, s32[]{:S(2)}) async-start(s8[13631488]{0:T(1024)(128)(4,1)} %bitcast.79), calls=%async_computation.3 | async-start | bytes 8388608
  46.4 14.5 %copy-start.7 = (bf16[1,1024,1024]{2,1,0:T(8,128)(2,1)S(1)}, bf16[1,1024,1024]{2,1,0:T(8,128)(2,1)}, u32[]{:S(2)}) copy-start(bf16[1,1024,1024]{2,1,0:T(8,128)(2,1)} %param.12) | copy-start | bytes 6291460
  108.4 14.1 %copy-start.4 = (bf16[1024,1024]{0,1:T(8,128)(2,1)S(1)}, bf16[1024,1024]{0,1:T(8,128)(2,1)}, u32[]{:S(2)}) copy-start(bf16[1024,1024]{0,1:T(8,128)(2,1)} %copy-done.3) | copy-start | bytes 6291460
  138.0 16.5 %slice-start.12 = ((s8[6815744]{0:T(1024)(128)(4,1)}), s8[4194304]{0:T(1024)(128)(4,1)S(1)}, s32[]{:S(2)}) async-start(s8[6815744]{0:T(1024)(128)(4,1)} %bitcast.96), calls=%async_computation.12 | async-start | bytes 8388608
  142.0 12.5 %copy-start.5 = (bf16[1024,1024]{0,1:T(8,128)(2,1)S(1)}, bf16[1024,1024]{0,1:T(8,128)(2,1)}, u32[]{:S(2)}) copy-start(bf16[1024,1024]{0,1:T(8,128)(2,1)} %copy-done.3) | copy-start | bytes 6291460
  142.0 12.5 %slice-start.13 = ((s8[6815744]{0:T(1024)(128)(4,1)}), s8[2621440]{0:T(1024)(128)(4,1)S(1)}, s32[]{:S(2)}) async-start(s8[6815744]{0:T(1024)(128)(4,1)} %bitcast.96), calls=%async_computation.13 | async-start | bytes 5242880
  142.0 21.9 %slice-start.4 = ((s8[13631488]{0:T(1024)(128)(4,1)}), s8[4194304]{0:T(1024)(128)(4,1)S(1)}, s32[]{:S(2)}) async-start(s8[13631488]{0:T(1024)(128)(4,1)} %bitcast.81), calls=%async_computation.4 | async-start | bytes 8388608
  142.0 21.9 %slice-start.5 = ((s8[13631488]{0:T(1024)(128)(4,1)}), s8[4194304]{0:T(1024)(128)(4,1)S(1)}, s32[]{:S(2)}) async-start(s8[13631488]{0:T(1024)(128)(4,1)} %bitcast.81), calls=%async_computation.5 | async-start | bytes 8388608
  154.5 9.4 %slice-start.6 = ((s8[13631488]{0:T(1024)(128)(4,1)}), s8[4194304]{0:T(1024)(128)(4,1)S(1)}, s32[]{:S(2)}) async-start(s8[13631488]{0:T(1024)(128)(4,1)} %bitcast.81), calls=%async_computation.6 | async-start | bytes 8388608
  154.5 9.4 %slice-start.7 = ((s8[13631488]{0:T(1024)(128)(4,1)}), s8[1048576]{0:T(1024)(128)(4,1)S(1)}, s32[]{:S(2)}) async-start(s8[13631488]{0:T(1024)(128)(4,1)} %bitcast.81), calls=%async_computation.7 | async-start | bytes 2097152
  163.9 9.4 %copy-start.2 = (bf16[1,1024,1024]{1,2,0:T(8,128)(2,1)S(1)}, bf16[1,1024,1024]{1,2,0:T(8,128)(2,1)}, u32[]{:S(2)}) copy-start(bf16[1,1024,1024]{1,2,0:T(8,128)(2,1)} %copy-done.1) | copy-start | bytes 6291460
  163.9 9.4 %copy-start.15 = (f32[1024]{0:T(1024)S(1)}, f32[1024]{0:T(1024)}, u32[]{:S(2)}) copy-start(f32[1024]{0:T(1024)} %copy-done.14) | copy-start | bytes 12292
  190.2 15.1 %copy-start.16 = (bf16[1024,3328]{1,0:T(8,128)(2,1)S(1)}, bf16[1024,3328]{1,0:T(8,128)(2,1)}, u32[]{:S(2)}) copy-start(bf16[1024,3328]{1,0:T(8,128)(2,1)} %convolution_convert_fusion.3) | copy-start | bytes 20447236
  205.4 13.2 %copy-start.8 = (f32[2,13,1024]{2,0,1:T(2,128)S(1)}, f32[2,13,1024]{2,0,1:T(2,128)}, u32[]{:S(2)}) copy-start(f32[2,13,1024]{2,0,1:T(2,128)} %param.18) | copy-start | bytes 319492
  205.4 13.9 %copy-start.9 = (f32[2,13,1024]{2,0,1:T(2,128)S(1)}, f32[2,13,1024]{2,0,1:T(2,128)}, u32[]{:S(2)}) copy-start(f32[2,13,1024]{2,0,1:T(2,128)} %param.21) | copy-start | bytes 319492
  441.0 15.1 %copy-start = (bf16[2,4,4,8,8,3328]{5,4,3,2,1,0:T(8,128)(2,1)S(1)}, bf16[2,4,4,8,8,3328]{5,4,3,2,1,0:T(8,128)(2,1)}, u32[]{:S(2)}) copy-start(bf16[2,4,4,8,8,3328]{5,4,3,2,1,0:T(8,128)(2,1)} %get-tuple-element.25) | copy-start | bytes 40894468
  441.0 21.6 %slice-start.8 = ((s8[13631488]{0:T(1024)(128)(4,1)}), s8[4194304]{0:T(1024)(128)(4,1)S(1)}, s32[]{:S(2)}) async-start(s8[13631488]{0:T(1024)(128)(4,1)} %bitcast.83), calls=%async_computation.8 | async-start | bytes 8388608
  441.0 21.6 %slice-start.9 = ((s8[13631488]{0:T(1024)(128)(4,1)}), s8[4194304]{0:T(1024)(128)(4,1)S(1)}, s32[]{:S(2)}) async-start(s8[13631488]{0:T(1024)(128)(4,1)} %bitcast.83), calls=%async_computation.9 | async-start | bytes 8388608
  456.1 6.6 %slice-start.10 = ((s8[13631488]{0:T(1024)(128)(4,1)}), s8[4194304]{0:T(1024)(128)(4,1)S(1)}, s32[]{:S(2)}) async-start(s8[13631488]{0:T(1024)(128)(4,1)} %bitcast.83), calls=%async_computation.10 | async-start | bytes 8388608
  456.1 7.1 %slice-start.11 = ((s8[13631488]{0:T(1024)(128)(4,1)}), s8[1048576]{0:T(1024)(128)(4,1)S(1)}, s32[]{:S(2)}) async-start(s8[13631488]{0:T(1024)(128)(4,1)} %bitcast.83), calls=%async_computation.11 | async-start | bytes 2097152
  463.2 5.1 %copy-start.13 = (f32[2,4,3328]{2,1,0:T(4,128)S(1)}, f32[2,4,3328]{2,1,0:T(4,128)}, u32[]{:S(2)}) copy-start(f32[2,4,3328]{2,1,0:T(4,128)} %get-tuple-element.62) | copy-start | bytes 319492
  463.2 5.8 %copy-start.12 = (f32[2,4,3328]{2,1,0:T(4,128)S(1)}, f32[2,4,3328]{2,1,0:T(4,128)}, u32[]{:S(2)}) copy-start(f32[2,4,3328]{2,1,0:T(4,128)} %get-tuple-element.63) | copy-start | bytes 319492
  463.2 6.4 %copy-start.11 = (f32[2,4,3328]{2,1,0:T(4,128)S(1)}, f32[2,4,3328]{2,1,0:T(4,128)}, u32[]{:S(2)}) copy-start(f32[2,4,3328]{2,1,0:T(4,128)} %get-tuple-element.65) | copy-start | bytes 319492
  463.2 7.1 %copy-start.10 = (f32[2,4,3328]{2,1,0:T(4,128)S(1)}, f32[2,4,3328]{2,1,0:T(4,128)}, u32[]{:S(2)}) copy-start(f32[2,4,3328]{2,1,0:T(4,128)} %get-tuple-element.66) | copy-start | bytes 319492

commit v2 on v0

v2 whole, which is shorter than its diff:
```python
import functools
import heapq

import jax
import jax.numpy as jnp
from jax import lax
from jax.experimental import pallas as pl
from jax.experimental.pallas import tpu as pltpu
from jax.sharding import PartitionSpec as P

MESH = pl.DeviceIdType.MESH
BF, F32 = jnp.bfloat16, jnp.float32
SIZE = {"x": 4, "y": 4, "z": 8}
VMEM_BYTES = 67043328
ALL = slice(None)


def coords():
    i = lax.axis_index("dp")
    return {"x": i // 64, "y": lax.rem(i // 16, 4), "z": lax.rem(i // 2, 8), "c": lax.rem(i, 2)}


def device(at):
    return {"dp": ((at["x"] * 4 + at["y"]) * 8 + at["z"]) * 2 + at["c"]}


def places(at):
    spots = {d: [at[d]] + [lax.rem(at[d] + k, n) for k in range(1, n)] for d, n in SIZE.items()}
    return spots, {(d, s): device({**at, d: spots[d][s]}) for d in SIZE for s in (1, -1)}


UNITS = [
    (1, "d", 0, 256, "xyz"), (1, "d", 256, 256, "yxz"), (1, "u", 0, 896, "zxy"), (1, "u", 896, 768, "zxy"), (1, "g", 0, 896, "xyz"), (1, "g", 896, 768, "yxz"),
    (0, "d", 0, 256, "xyz"), (0, "d", 256, 256, "yxz"), (0, "u", 0, 896, "zxy"), (0, "u", 896, 768, "zxy"), (0, "g", 0, 896, "yxz"), (0, "g", 896, 768, "xyz"),
]
DEPTH = {"u": 4, "g": 8, "d": 26}
TILES = {"u": 8, "g": 8, "d": 26}
WIDTH = {"u": 1664, "g": 1664, "d": 512}
TALL = {"u": 1, "g": 1, "d": 4}
LASTDIM = {"u": "y", "g": "z", "d": "z"}
ROWS = {"u": 4, "g": 4, "d": 16}
COUNT = 2 * 3 * 1024 * 3328
NB = 2


def view(a, order, at, level, v):
    if level == 0:
        return {"z": (ALL, ALL, v), "x": (v,), "y": (ALL, v)}[order[0]]
    if level == 1:
        return {"zxy": (v, ALL, at["z"]), "xyz": (at["x"], v), "yxz": (v, at["y"])}[order]
    return (at["x"], v, at["z"]) if a == "u" else (at["x"], at["y"], v)


def block_shape(i, level):
    _, a, _, cols, _ = UNITS[i]
    return ((4, DEPTH[a], 8, cols), (DEPTH[a], 8, cols))[level]


def remote_copy(src, dst, ss, rs, to):
    return pltpu.make_async_remote_copy(src_ref=src, dst_ref=dst, send_sem=ss, recv_sem=rs, device_id=to, device_id_type=MESH)


GROUPS = [(1, "d"), (1, "u"), (1, "g"), (0, "u"), (0, "d"), (0, "g")]
OFFSETS = (2, 1, 3, 0)


def plan():
    RATE, LAT, TASK, DRATE, DLAT = 46.0e3, 2.6, 1.15, 550.0e3, 1.7
    free, heap, seq = {}, [], [0]

    def send(t, link, nbytes):
        free[link] = max(free.get(link, 0.0), t) + nbytes / RATE
        return free[link] + LAT

    def push(t, ev):
        seq[0] += 1
        heapq.heappush(heap, (t, seq[0], ev))
    ring = {}
    for i, (l, a, _, cols, o) in enumerate(UNITS):
        ring[0, i] = (o[0], 4 * DEPTH[a] * 8 * cols * 2)
        ring[1, i] = (o[1], DEPTH[a] * 8 * cols * 2)
        ring[2, (l, a)] = (LASTDIM[a], TALL[a] * 8 * WIDTH[a] * 2)
    have = {}
    got, steps, now = {}, [], 4.0

    def ready(i, off):
        l, a, _, _, o = UNITS[i]
        need = [(l, a, off % 4)] if o[0] == "x" else [(l, a, b) for b in range(4)]
        return max(have[n] for n in need) if all(n in have for n in need) else None

    def run(until):
        nonlocal now
        taken = []
        while heap and heap[0][0] <= until:
            t, _, ev = heapq.heappop(heap)
            kind, level, key, s, k = ev
            dim, nbytes = ring[level, key]
            h = SIZE[dim] // 2
            if level == 0 and kind == "step" and k < h:
                when = ready(key, s * (h - k))
                if when is None or when > t:
                    push(t + 0.5 if when is None else when, ev)
                    continue
            now = max(now, t)
            taken.append(ev)
            cost = 0.15 + nbytes * (4 + 2 * level) / 7.0e6
            if kind == "end":
                continue
            if kind == "start":
                now += cost
                for s in (1, -1):
                    push(send(now, (dim, s), nbytes // 2), ("step", level, key, s, 1))
            elif k < h:
                now += cost
                push(send(now, (dim, s), nbytes), ("step", level, key, s, k + 1))
            else:
                got[level, key] = got.get((level, key), 0) + 1
                if got[level, key] < 2:
                    continue
                if level == 0:
                    push(now, ("start", 1, key, 0, 0))
                elif level == 1:
                    ka = UNITS[key][:2]
                    if all(got.get((1, i)) == 2 for i, u in enumerate(UNITS) if u[:2] == ka):
                        push(now, ("start", 2, ka, 0, 0))
                else:
                    push(now, ("end", 2, key, 0, 0))
        return taken
    dfree = 0.0
    for l, a in GROUPS:
        own = {}
        steps.append(((l, a), run(now)))
        for s in range(8):
            now += TASK
            block, half = (s // 2, s % 2) if a == "d" else (s % 4, s // 4)
            off = OFFSETS[block]
            if half == 0:
                dfree = max(dfree, now) + 4 * TILES[a] * 8 * WIDTH[a] * 2 / DRATE
                own[off] = dfree + DLAT
            else:
                have[l, a, off] = max(now + 2.0, own[off])
            if a == "d" and half == 1 and block == 0:
                push(have[l, a, off], ("start", 0, next(i for i, u in enumerate(UNITS) if u[:2] == (l, a) and u[4][0] == "x"), 0, 0))
        for i, u in enumerate(UNITS):
            if u[:2] == (l, a) and not (a == "d" and u[4][0] == "x"):
                push(ready(i, SIZE[u[4][0]] // 2), ("start", 0, i, 0, 0))
    steps.append((None, run(float("inf"))))
    return steps, now, free


def addsum(dst, srcs):
    def add(*at):
        acc = srcs[0][at].astype(F32)
        for s in srcs[1:]:
            acc = acc + s[at].astype(F32)
        dst[at] = acc.astype(BF)

    if len(dst.shape) == 4:

        def body(i, _):
            add(i)
            return 0
        lax.fori_loop(0, dst.shape[0], body, 0)
    else:
        add(...)


def rs_scratch():
    sh = {}
    sem = pltpu.SemaphoreType.DMA
    for a in "ugd":
        sh["loc_" + a] = pltpu.VMEM((2, 4, 4, TILES[a], 8, WIDTH[a]), BF)
        sh["stage_" + a] = pltpu.VMEM((NB, 4, DEPTH[a], 8, max(u[3] for u in UNITS if u[1] == a)), BF)
        sh["stsem_" + a] = sem((NB,))
        sh["red_" + a] = pltpu.VMEM((2, TALL[a], 8, WIDTH[a]), BF)
        sh["mv_" + a] = pltpu.VMEM((2, 2, 2, ROWS[a], WIDTH[a]), F32)
        sh["w_" + a] = pltpu.VMEM((2, TALL[a], 8, WIDTH[a]), BF)
        h = SIZE[LASTDIM[a]] // 2
        for l in (0, 1):
            sh["slot2_%d%s" % (l, a)] = pltpu.VMEM((2, h, TALL[a], 8, WIDTH[a]), BF)
            sh["first_%d%s" % (l, a)] = pltpu.VMEM((TALL[a], 8, WIDTH[a]), BF)
            for n in "rs":
                sh["%s2_%d%s" % (n, l, a)] = sem((2, h))
    sh["new_d"] = pltpu.VMEM((2, 2, 16, 512), BF)
    for i, u in enumerate(UNITS):
        h = SIZE[u[4][0]] // 2
        if not u[0]:
            sh["own_%d" % i] = pltpu.VMEM(block_shape(i, 0), BF)
        sh["slot0_%d" % i] = pltpu.VMEM((2, h) + block_shape(i, 0), BF)
        sh["slot1_%d" % i] = pltpu.VMEM((2, 2) + block_shape(i, 1), BF)
        for n in "rs":
            sh["%s0_%d" % (n, i)] = sem((2, h))
            sh["%s1_%d" % (n, i)] = sem((2, 2))
    sh["ownsem"] = sem((len(UNITS),))
    sh["left"] = pltpu.VMEM((1024, 1024), BF)
    sh["leftsem"] = sem((1,))
    sh["right"] = pltpu.VMEM((2, 1024, 1664), BF)
    sh["rightsem"] = sem((2,))
    sh["res_u"] = pltpu.VMEM((2, 4, 8, 8, 1664), BF)
    sh["res_d"] = pltpu.VMEM((2, 4, 26, 8, 512), BF)
    sh["dr"] = sem((6, 4))
    sh["ds"] = sem((6, 4))
    sh["os"] = sem((6, 4))
    sh["ar_z"] = pltpu.VMEM((16, 1, 128), F32)
    sh["ar_p"] = pltpu.VMEM((16, 1, 128), F32)
    sh["arsem"] = sem((4, 16))
    sh["mvsem"] = sem((3, 2, 3))
    sh["wsem"] = sem((3,))
    sh["finsem"] = sem((3, 2, 3))
    sh["newsem"] = sem((3,))
    return sh


def rs_kernel(names, *refs):
    act = {(n, l): refs[2 * j + l] for j, n in enumerate(("a", "h", "u", "g", "y")) for l in (0, 1)}
    weights = {a: refs[10 + j] for j, a in enumerate("ugd")}
    moments = {a: (refs[13 + j], refs[16 + j]) for j, a in enumerate("ugd")}
    new = {a: refs[19 + j] for j, a in enumerate("ugd")}
    new_moments = {a: (refs[22 + j], refs[25 + j]) for j, a in enumerate("ugd")}
    mine = {a: refs[28 + j] for j, a in enumerate("ugd")}
    S = dict(zip(names, refs[31:], strict=True))
    at = coords()
    c, x = at["c"], at["x"]
    sib = device({**at, "c": 1 - c})
    steps, _, _ = plan()
    spots, near = places(at)
    windows = [pl.ds(13 * lax.div(v, 4) + 3 * lax.rem(v, 4), 4) for v in spots["z"]]
    zz = lax.rem(at["z"], 4)

    peers = [device({**at, "z": lax.rem(at["z"] + dz, 8), "c": lax.rem(c + dc, 2)}) for dz in range(8) for dc in range(2)][1:]
    peers += [device({**at, "x": lax.rem(at["x"] + dx, 4), "y": lax.rem(at["y"] + dy, 4)}) for dx in range(4) for dy in range(4)][1:]
    bar = pltpu.get_barrier_semaphore()
    for p in peers:
        pl.semaphore_signal(bar, inc=1, device_id=p, device_id_type=MESH)

    def halfcols(a, which):
        w = WIDTH[a]
        return pl.ds(pl.multiple_of((c if which else 1 - c) * w, 128), w)

    def left(l, a):
        return pltpu.make_async_copy(act["y" if a == "d" else "a", l], S["left"], S["leftsem"].at[0])
    loads = []
    for l, a in GROUPS:
        loads += [(l, a, n) for n in range(4 if a == "d" else 2)]

    def right(n):
        l, a, k = loads[n]
        if a == "d":
            b = spots["x"][OFFSETS[k]]
            src = act["h", l].at[pl.ds(pl.multiple_of(832 * b, 832), 832)]
            dst = S["right"].at[n % 2, pl.ds(0, 832), pl.ds(0, 1024)]
        else:
            src = act[a, l].at[:, halfcols(a, k)]
            dst = S["right"].at[n % 2]
        return pltpu.make_async_copy(src, dst, S["rightsem"].at[n % 2])
    left(*GROUPS[0]).start()
    right(0).start()
    right(1).start()

    moment_copies = []
    for j, a in enumerate("ugd"):
        for q in (0, 1):
            ref = moments[a][q]
            moment_copies.append(pltpu.make_async_copy(ref.at[:, :, halfcols(a, 1)], S["mv_" + a].at[q, c], S["mvsem"].at[j, q, 2]))
        tile = windows[0] if a == "d" else pl.ds(at["z"], 1)
        moment_copies.append(pltpu.make_async_copy(weights[a].at[:, at["x"], at["y"], tile, :, halfcols(a, 1)], S["w_" + a], S["wsem"].at[j]))
    for cp in moment_copies:
        cp.start()
    pl.semaphore_wait(bar, len(peers))
    pend = []

    def remote(make):
        cp = make()
        cp.start()
        pend.append(make)
        return cp
    for j, a in enumerate("ugd"):
        for q in (0, 1):
            moment_copies.append(remote(lambda j=j, a=a, q=q: remote_copy(
                moments[a][q].at[:, :, halfcols(a, 0)], S["mv_" + a].at[q, c], S["mvsem"].at[j, q, 0], S["mvsem"].at[j, q, 1], sib)))

    def region(ref, i, level, v):
        l, a, col, n, o = UNITS[i]
        idx = view(a, o, at, level, v)
        return ref.at[(l, *idx, *([ALL] * (4 - len(idx))), pl.ds(col, n))]

    def pos(i, level, off):
        a = UNITS[i][1]
        dim = UNITS[i][4][level] if level < 2 else LASTDIM[a]
        off %= SIZE[dim]
        if level < 2:
            return spots[dim][off]
        return windows[off] if a == "d" else pl.ds(spots[dim][off], 1)

    def result(gi, block, half):
        l, a = GROUPS[gi]
        b = spots["x"][OFFSETS[block]]
        task = 2 * block + half if a == "d" else 4 * half + block
        buf = S["res_d" if a == "d" else "res_u"].at[task % 2]
        if half == 0:
            return lambda: remote_copy(buf, S["loc_" + a].at[l, b], S["ds"].at[gi, block], S["dr"].at[gi, block], sib)
        return lambda: pltpu.make_async_copy(buf, mine[a].at[l, b], S["os"].at[gi, block])

    def offset_of(block):
        return lax.select(block == 0, 2, lax.select(block == 1, 1, lax.select(block == 2, 3, 0)))

    def task_of(a, s):
        return (s // 2, s % 2) if a == "d" else (s % 4, s // 4)

    out_waited, sib_waited = set(), set()

    def wait_out(gi, block, half):
        if (gi, block, half) not in out_waited:
            out_waited.add((gi, block, half))
            cp = result(gi, block, half)()
            cp.wait() if half else cp.wait_send()

    def wait_terms(i, off):
        l, a, _, _, o = UNITS[i]
        gi = GROUPS.index((l, a))
        for block, b in enumerate(OFFSETS):
            if o[0] == "x" and b != off % 4:
                continue
            wait_out(gi, block, 1)
            if (gi, block) not in sib_waited:
                sib_waited.add((gi, block))
                result(gi, block, 0)().wait_recv()

    uses = {a: [] for a in "ugd"}
    for _, events in steps:
        for kind, level, key, s, k in events:
            if level == 0:
                h = SIZE[UNITS[key][4][0]] // 2
                if kind == "start" or k < h:
                    uses[UNITS[key][1]].append((key, h if kind == "start" else s * (h - k)))
    nth = {a: 0 for a in "ugd"}
    fetched = {a: 0 for a in "ugd"}

    def stage(a, n):
        i, off = uses[a][n]
        buf = S["stage_" + a].at[n % NB, :, :, :, pl.ds(0, UNITS[i][3])]
        return pltpu.make_async_copy(region(mine[a], i, 0, pos(i, 0, off)), buf, S["stsem_" + a].at[n % NB]), buf

    complete = set()

    def fetch_ahead(a):
        while fetched[a] < min(len(uses[a]), nth[a] + NB):
            i, off = uses[a][fetched[a]]
            if UNITS[i][:2] not in complete:
                return
            wait_terms(i, off)
            stage(a, fetched[a])[0].start()
            fetched[a] += 1

    def fetch_now(a, n):
        if fetched[a] == n:
            wait_terms(*uses[a][n])
            stage(a, n)[0].start()
            fetched[a] += 1

    own_fetched = set()

    sent = {}

    def own_buffer(i):
        return S["slot0_%d" % i].at[0, 0] if UNITS[i][0] else S["own_%d" % i]

    def own(i):
        return pltpu.make_async_copy(region(mine[UNITS[i][1]], i, 0, pos(i, 0, 0)), own_buffer(i), S["ownsem"].at[i])

    def fetch_own(i):
        if i in own_fetched or (UNITS[i][0] and i not in sent):
            return
        if UNITS[i][0]:
            sent[i]().wait_send()
        own_fetched.add(i)
        wait_terms(i, 0)
        own(i).start()

    def operands(level, i, off):
        _, a, _, _, o = UNITS[i]
        v = pos(i, level, off)
        here = region(S["loc_" + a], i, level, v)
        if level == 0:
            wait_terms(i, off)
            n = nth[a]
            assert uses[a][n] == (i, off)
            fetch_now(a, n)
            cp, buf = stage(a, n)
            cp.wait()
            nth[a] += 1
            return [buf, here]
        h = SIZE[o[0]] // 2
        first = [own_buffer(i)] + [S["slot0_%d" % i].at[d, h - 1] for d in (0, 1)]
        if level == 1:
            return [here] + [f.at[v] for f in first]
        w = pos(i, 1, 0)
        return [here] + [f.at[w, v] for f in first] + [S["slot1_%d" % i].at[d, 1, v] for d in (0, 1)]

    def half(ref, which, level, a):
        if level == 2 and TALL[a] == 1:
            return ref.at[..., pl.ds(896, 768) if which else pl.ds(0, 896)]
        n = ref.shape[0] // 2
        return ref.at[pl.ds(n * which, n)]

    def parts(key):
        r = []
        for i, u in enumerate(UNITS):
            if u[:2] == key:
                for lo, hi in ((0, 896), (896, 1664)):
                    a, b = max(lo, u[2]), min(hi, u[2] + u[3])
                    if a < b:
                        r.append((i, pl.ds(a - u[2], b - a), pl.ds(a, b - a), lo > 0))
        return r

    def cut(ref, cs):
        return ref.at[..., cs]

    def event(ev):
        kind, level, key, s, k = ev
        l, a = UNITS[key][:2] if level < 2 else key
        tag = "%d" % key if level < 2 else "%d%s" % key
        dim = UNITS[key][4][level] if level < 2 else LASTDIM[a]
        h = SIZE[dim] // 2
        if kind == "end":
            finish(l, a)
            return
        slot, rsem, ssem = (S["%s%d_%s" % (n, level, tag)] for n in ("slot", "r", "s"))

        def send(src, d, k):
            dst = lambda: slot.at[d, k] if k else half(slot.at[d, 0], d, level, a)
            remote(lambda: remote_copy(src(), dst(), ssem.at[d, k], rsem.at[d, k], near[dim, 1 - 2 * d]))

        if kind == "start":
            if level == 1:
                wait_terms(key, 0)
                fetch_own(key)
                assert key in own_fetched
                own(key).wait()
            dst = (lambda: S["first_" + tag]) if level == 2 else (lambda: region(S["loc_" + a], key, level, pos(key, level, h)))
            if level < 2:
                addsum(dst(), operands(level, key, h))
            else:
                for i, uc, sc, _ in parts(key):
                    addsum(cut(dst(), sc), [cut(o, uc) for o in operands(level, i, h)])
            for d in (0, 1):
                send(lambda d=d: half(dst(), d, level, a), d, 0)
            if level == 0:
                fetch_own(key)
                fetch_ahead(a)
            return
        d = 0 if s > 0 else 1
        block = slot.at[d, k - 1]
        got = half(block, d, level, a) if k == 1 else block
        remote_copy(got, got, ssem.at[d, k - 1], rsem.at[d, k - 1], sib).wait_recv()
        if k == h:
            if level == 0:
                fetch_own(key)
            return
        off = s * (h - k)
        if level < 2:
            ops = operands(level, key, off)
            if k > 1:
                addsum(block, [block] + ops)
            else:
                for w in (0, 1):
                    hm = half(block, w, level, a)
                    addsum(hm, ([hm] if w == d else []) + [half(r, w, level, a) for r in ops])
        else:
            for i, uc, sc, w in parts(key):
                ops = [cut(o, uc) for o in operands(level, i, off)]
                m = cut(block, sc)
                if k > 1:
                    addsum(m, [m] + ops)
                elif TALL[a] == 1:
                    addsum(m, ([m] if w == (d == 1) else []) + ops)
                else:
                    for w in (0, 1):
                        hm = half(m, w, level, a)
                        addsum(hm, ([hm] if w == d else []) + [half(r, w, level, a) for r in ops])
        send(lambda: slot.at[d, k - 1], d, k)
        if (level, d, k) == (0, 0, 1) and l:
            sent[key] = pend.pop()
        if level == 0:
            fetch_ahead(a)

    def finish(l, a):
        h = SIZE[LASTDIM[a]] // 2
        for i, uc, sc, _ in parts((l, a)):
            ops = [cut(o, uc) for o in operands(2, i, 0)] + [cut(S["slot2_%d%s" % (l, a)].at[d, h - 1], sc) for d in (0, 1)]
            addsum(cut(S["red_" + a].at[l], sc), ops)

    filled = {}
    holds = ("y", 1)
    left(*GROUPS[0]).wait()
    for gi, (l, a) in enumerate(GROUPS):
        wants = ("y" if a == "d" else "a", l)
        if wants != holds:
            left(l, a).start()
            left(l, a).wait()
            holds = wants
        first_load = sum(4 if g[1] == "d" else 2 for g in GROUPS[:gi])

        for k in (0, 1):
            if (a == "d", k) in filled:
                wait_out(*filled[a == "d", k])
        for ev in steps[gi][1]:
            event(ev)
        res = S["res_d" if a == "d" else "res_u"]

        def away(s, block, half_, gi=gi, l=l, a=a, res=res):
            b = lax.rem(x + offset_of(block), 4)
            buf = res.at[lax.rem(s, 2)]
            return (remote_copy(buf, S["loc_" + a].at[l, b], S["ds"].at[gi, block], S["dr"].at[gi, block], sib),
                    pltpu.make_async_copy(buf, mine[a].at[l, b], S["os"].at[gi, block]))

        def loop(s, _, l=l, a=a, first_load=first_load, res=res, away=away):
            block, half_ = (lax.div(s, 2), lax.rem(s, 2)) if a == "d" else (lax.rem(s, 4), lax.div(s, 4))
            n = lax.rem(block, 2) if a == "d" else half_

            @pl.when((half_ if a == "d" else block) == 0)
            def _():
                src, buf = (act["h", l].at[pl.ds(0, 832)], S["right"].at[n, pl.ds(0, 832), pl.ds(0, 1024)]) if a == "d" else (act[a, l].at[:, pl.ds(0, 1664)], S["right"].at[n])
                pltpu.make_async_copy(src, buf, S["rightsem"].at[n]).wait()
            before = (lax.div(s - 2, 2), half_) if a == "d" else (lax.rem(s - 2, 4), lax.div(s - 2, 4))
            send, keep = away(s, *before)

            @pl.when((s >= 2) & (before[1] == 0))
            def _():
                send.wait_send()

            @pl.when((s >= 2) & (before[1] == 1))
            def _():
                keep.wait()
            if a == "d":
                cols = pl.ds(pl.multiple_of(lax.select(half_ == 0, 1 - c, c) * 512, 512), 512)
                t = jnp.dot(S["right"][n, pl.ds(0, 832), pl.ds(0, 1024)], S["left"][:, cols], preferred_element_type=F32)
                res[lax.rem(s, 2)] = t.reshape(4, 26, 8, 512).astype(BF)
            else:
                rows = pl.ds(pl.multiple_of(lax.rem(x + offset_of(block), 4) * 256, 256), 256)
                t = jnp.dot(S["left"][rows], S["right"][half_], preferred_element_type=F32)
                res[lax.rem(s, 2)] = t.reshape(4, 8, 8, 1664).astype(BF)
            send, keep = away(s, block, half_)
            pl.when(half_ == 0)(send.start)
            pl.when(half_ == 1)(keep.start)
            for k in range(4 if a == "d" else 2):
                if first_load + k + 2 < len(loads):
                    pl.when(s == (2 * k + 1 if a == "d" else 4 * k + 3))(right(first_load + k + 2).start)
            return 0
        lax.fori_loop(0, 8, loop, 0)
        for k in range(6):
            out_waited.add((gi, *task_of(a, k)))
        for k in (0, 1):
            filled[a == "d", k] = gi, *task_of(a, 6 + k)
        complete.add((l, a))
        fetch_ahead(a)
    for ev in steps[-1][1]:
        event(ev)
    for gi, (l, a) in enumerate(GROUPS):
        for k in range(8):
            wait_out(gi, *task_of(a, k))

    total = jnp.zeros((8, 128), F32)
    for a in "ugd":
        for l in (0, 1):
            for t in range(TALL[a]):
                for q in range(WIDTH[a] // 128):
                    g = S["red_" + a][l, t, :, q * 128:q * 128 + 128].astype(F32)
                    if a == "d":
                        row = lax.broadcasted_iota(jnp.int32, (8, 128), 0) + 8 * t
                        g = jnp.where((row >= 2 * zz) & (row < 2 * zz + 26), g, 0.0)
                    total = total + g * g
    total = jnp.sum(total, axis=0, keepdims=True)
    for r, (buf, ds) in enumerate(((S["ar_z"], [(0, 0, q // 2, q % 2) for q in range(16)]), (S["ar_p"], [(q // 4, q % 4, 0, 0) for q in range(16)]))):
        buf[0] = total
        cps = []
        for q in range(1, 16):
            dx, dy, dz, dc = ds[q]
            to = device({"x": lax.rem(at["x"] + dx, 4), "y": lax.rem(at["y"] + dy, 4), "z": lax.rem(at["z"] + dz, 8), "c": lax.rem(c + dc, 2)})
            cps.append(remote(lambda q=q, to=to: remote_copy(buf.at[0], buf.at[q], S["arsem"].at[2 * r, q], S["arsem"].at[2 * r + 1, q], to)))
        for cp in cps:
            cp.wait_recv()
            cp.wait_send()
            pend.pop()
        total = buf[0]
        for q in range(1, 16):
            total = total + buf[q]
    mean = jnp.sum(total, axis=1, keepdims=True) / COUNT
    factor = jnp.minimum(1.0, 0.5 * lax.rsqrt(mean + 1e-30))
    for cp in moment_copies:
        cp.wait_recv() if cp.is_remote else cp.wait()

    def adamw(w, m, v, g):
        g = g * factor
        m = 0.9 * m + 0.1 * g
        v = 0.95 * v + 0.05 * g * g
        step = m * lax.rsqrt(v + 1e-8) + 0.1 * w
        return (w - 0.02 * step).astype(BF), m, v

    for a in "ug":
        mv, red, wv = S["mv_" + a], S["red_" + a], S["w_" + a]

        def body(q, _, mv=mv, red=red, wv=wv, a=a):
            cs = pl.ds(pl.multiple_of(q * 128, 128), 128)
            for l in (0, 1):
                m, v = (jnp.concatenate([mv[e, 0, l, :, cs], mv[e, 1, l, :, cs]], axis=0) for e in (0, 1))
                n, m, v = adamw(wv[l, 0, :, cs].astype(F32), m, v, red[l, 0, :, cs].astype(F32))
                wv[l, 0, :, cs] = n
                for e, t in enumerate((m, v)):
                    for s in (0, 1):
                        mv[e, s, l, :, cs] = t[4 * s:4 * s + 4]
            return 0
        lax.fori_loop(0, 13, body, 0)
    row = lax.broadcasted_iota(jnp.int32, (32, 32), 0)
    column = lax.broadcasted_iota(jnp.int32, (32, 32), 1)
    pick = (column == 2 * zz + 13 * (row >> 4) + (row & 15)) & ((row & 15) < 13)
    pick = jnp.where(pick, 1.0, 0.0).astype(BF)
    for l in (0, 1):
        gd, wd = (jnp.dot(pick, S[n][l].reshape(32, 512), preferred_element_type=F32) for n in ("red_d", "w_d"))
        for s in (0, 1):
            rows = slice(16 * s, 16 * s + 16)
            n, m, v = adamw(wd[rows], S["mv_d"][0, s, l], S["mv_d"][1, s, l], gd[rows])
            S["new_d"][l, s] = n
            S["mv_d"][0, s, l] = m
            S["mv_d"][1, s, l] = v
    ends = []
    for j, a in enumerate("ugd"):
        cp = pltpu.make_async_copy(S["new_d"] if a == "d" else S["w_" + a].at[:, 0], new[a], S["newsem"].at[j])
        cp.start()
        ends.append(cp.wait)
        for q in (0, 1):
            out = new_moments[a][q].at[:, :, halfcols(a, 1)]
            cp = remote_copy(S["mv_" + a].at[q, 1 - c], out, S["finsem"].at[j, q, 0], S["finsem"].at[j, q, 1], sib)
            cp.start()
            back = remote_copy(S["mv_" + a].at[q, 1 - c], new_moments[a][q].at[:, :, halfcols(a, 0)], S["finsem"].at[j, q, 0], S["finsem"].at[j, q, 1], sib)
            ends += [cp.wait_send, back.wait_recv]
            cp = pltpu.make_async_copy(S["mv_" + a].at[q, c], out, S["finsem"].at[j, q, 2])
            cp.start()
            ends.append(cp.wait)
    for wait in ends:
        wait()
    for make in pend:
        make().wait_send()


def reduce_scatter(acts, weights, m, v):
    args = list(acts) + [w.reshape(2, 4, 4, -1, 8, w.shape[-1]) for w in weights] + [*m, *v]
    sh = rs_scratch()
    any_ = pl.BlockSpec(memory_space=pl.ANY)
    outs = [jax.ShapeDtypeStruct(s, BF) for s in ((2, 8, 1664), (2, 8, 1664), (2, 2, 16, 512))] + [jax.ShapeDtypeStruct(t.shape, F32) for t in (*m, *v)]
    outs += [jax.ShapeDtypeStruct((2, 4, 4, TILES[a], 8, WIDTH[a]), BF) for a in "ugd"]
    outs = pl.pallas_call(
        functools.partial(rs_kernel, list(sh)), out_shape=outs, in_specs=[any_] * 19, out_specs=[any_] * 12, scratch_shapes=list(sh.values()), name="reduce_scatter",
        compiler_params=pltpu.CompilerParams(collective_id=0, has_side_effects=True, vmem_limit_bytes=VMEM_BYTES))(*args)
    return outs[:3], outs[3:6], outs[6:9]


def plan_ag():
    RATE, LAT = 46.0e3, 2.9
    free, heap, order, seq, got, now = {}, [], [], [0], {}, 1.0

    def push(t, ev):
        seq[0] += 1
        heapq.heappush(heap, (t, seq[0], ev))

    def send(t, link, nbytes):
        free[link] = max(free.get(link, 0.0), t) + nbytes / RATE
        return free[link] + LAT
    ring = {(2, a): (LASTDIM[a], {"u": 8 * 1664, "g": 8 * 1664, "d": 32 * 512}[a] * 4) for a in "ugd"}
    for i, (_, a, _, cols, o) in enumerate(UNITS):
        ring[1, i] = (o[1], DEPTH[a] * 8 * cols * 2)
        ring[0, i] = (o[0], 4 * DEPTH[a] * 8 * cols * 2)
    for a in "gdu":
        push(1.0, ("start", 2, a, 0, 0))
    while heap:
        t, _, ev = heapq.heappop(heap)
        kind, level, key, s, k = ev
        dim, nbytes = ring[level, key]
        h = SIZE[dim] // 2
        now = max(now, t) + 0.1
        order.append(ev)
        if kind == "start":
            for s in (1, -1):
                push(send(now, (dim, s), nbytes), ("step", level, key, s, 1))
            continue
        if k < h:
            push(send(now, (dim, s), nbytes if k < h - 1 else nbytes // 2), ("step", level, key, s, k + 1))
            continue
        got[level, key] = got.get((level, key), 0) + 1
        if got[level, key] < 2:
            continue
        if level == 2:
            for i, u in enumerate(UNITS):
                if u[1] == key:
                    push(now + (1.0 if key == "d" else 0), ("start", 1, i, 0, 0))
        elif level == 1:
            push(now, ("start", 0, key, 0, 0))
    return order, now, free


def ag_scratch():
    sem = pltpu.SemaphoreType.DMA
    sh = {"pc": pltpu.VMEM((8, 2, 2, 16, 512), BF), "asm": pltpu.VMEM((2, 26, 8, 512), BF), "loc": sem((4,)), "sr": sem((128,)), "ss": sem((128,))}
    for n in "rs":
        for a in "ugd":
            sh["%s2_%s" % (n, a)] = sem((2, SIZE[LASTDIM[a]] // 2))
        for i, u in enumerate(UNITS):
            for lv in (0, 1):
                sh["%s%d_%d" % (n, lv, i)] = sem((2, SIZE[u[4][lv]] // 2))
    return sh


def ag_kernel(names, *refs):
    own = {a: refs[j] for j, a in enumerate("ugd")}
    out = {a: refs[3 + j] for j, a in enumerate("ugd")}
    S = dict(zip(names, refs[6:], strict=True))
    at = coords()
    c, x, y, z = at["c"], at["x"], at["y"], at["z"]
    sib = device({**at, "c": 1 - c})
    order, _, _ = plan_ag()
    spots, near = places(at)
    peers = [sib, *near.values()]
    bar = pltpu.get_barrier_semaphore()
    for p in peers:
        pl.semaphore_signal(bar, inc=1, device_id=p, device_id_type=MESH)

    def hc(a, col=0, n=None):
        return pl.ds(pl.multiple_of(c * WIDTH[a] + col, 128), WIDTH[a] if n is None else n)
    local = [pltpu.make_async_copy(own["u"], out["u"].at[:, x, y, z, :, hc("u")], S["loc"].at[0]),
             pltpu.make_async_copy(own["g"], out["g"].at[:, x, y, z, :, hc("g")], S["loc"].at[1]),
             pltpu.make_async_copy(own["d"], S["pc"].at[z], S["loc"].at[2])]
    for cp in local:
        cp.start()
    pl.semaphore_wait(bar, len(peers))
    for cp in local:
        cp.wait()
    pend, twin = [], []

    def remote(src, ss, rs, to):
        cp = remote_copy(src, src, ss, rs, to)
        cp.start()
        pend.append(cp)

    def to_sibling(ref):
        n = len(twin)
        remote(ref, S["ss"].at[n], S["sr"].at[n], sib)
        twin.append(ref)

    def region(level, key, v):
        if level == 2:
            if key == "d":
                return S["pc"].at[v]
            return out["u"].at[:, x, v, z, :, hc("u")] if key == "u" else out["g"].at[:, x, y, v, :, hc("g")]
        l, a, col, n, o = UNITS[key]
        idx = view(a, o, at, level, v)
        return out[a].at[(l, *idx, *([ALL] * (4 - len(idx))), hc(a, col, n))]

    def half(ref, which):
        n = ref.shape[0] // 2
        return ref.at[pl.ds(n * which, n)]

    got = {}
    for kind, level, key, s, k in order:
        dim = UNITS[key][4][level] if level < 2 else LASTDIM[key]
        n = SIZE[dim]
        h = n // 2
        rsem, ssem = S["r%d_%s" % (level, key)], S["s%d_%s" % (level, key)]

        def send(src, d, k, dim=dim, rsem=rsem, ssem=ssem):
            remote(src, ssem.at[d, k], rsem.at[d, k], near[dim, 1 - 2 * d])

        if kind == "start":
            for d in (0, 1):
                send(region(level, key, at[dim]), d, 0)
            continue
        d = 0 if s > 0 else 1
        block = region(level, key, spots[dim][-s * k % n])
        if k == h:
            block = half(block, d)
        remote_copy(block, block, ssem.at[d, k - 1], rsem.at[d, k - 1], sib).wait_recv()
        if k < h - 1:
            send(block, d, k)
        elif k == h - 1:
            send(half(block, d), d, k)
        if level < 2:
            to_sibling(block)
        if k == h:
            got[level, key] = got.get((level, key), 0) + 1
            if level == 2 and got[level, key] == 2:
                if key == "d":
                    q = lax.broadcasted_iota(jnp.int32, (208, 256), 1)
                    r = lax.broadcasted_iota(jnp.int32, (208, 256), 0)
                    e = q & 15
                    pick = (r == 26 * (q >> 5) + 13 * ((q >> 4) & 1) + e) & (e < 13)
                    pick = jnp.where(pick, 1.0, 0.0).astype(BF)
                    for l in (0, 1):
                        rows = jnp.dot(pick, S["pc"][:, l].reshape(256, 512), preferred_element_type=F32)
                        S["asm"][l] = rows.reshape(26, 8, 512).astype(BF)
                    cp = pltpu.make_async_copy(S["asm"], out["d"].at[:, x, y, :, :, hc("d")], S["loc"].at[3])
                    cp.start()
                    cp.wait()
                idx = (ALL, x, ALL, z, ALL) if key == "u" else (ALL, x, y, ALL, ALL)
                to_sibling(out[key].at[(*idx, hc(key))])
    for n, ref in enumerate(twin):
        remote_copy(ref, ref, S["ss"].at[n], S["sr"].at[n], sib).wait_recv()
    for cp in pend:
        cp.wait_send()


def all_gather(u, g, d):
    sh = ag_scratch()
    any_ = pl.BlockSpec(memory_space=pl.ANY)
    outs = [jax.ShapeDtypeStruct((2, 4, 4, TILES[a], 8, 2 * WIDTH[a]), BF) for a in "ugd"]
    return pl.pallas_call(
        functools.partial(ag_kernel, list(sh)), out_shape=outs, in_specs=[any_] * 3, out_specs=[any_] * 3, scratch_shapes=list(sh.values()), name="all_gather",
        compiler_params=pltpu.CompilerParams(collective_id=1, has_side_effects=True, vmem_limit_bytes=VMEM_BYTES))(u, g, d)


T = 1024
B = 256
N = 3328 // B
NT = (((1,), (1,)), ((), ()))


def dot(a, b, dims=(((1,), (0,)), ((), ()))):
    return lax.dot_general(a, b, dims, preferred_element_type=F32)


def norm_scale(wide):
    return lax.rsqrt(jnp.mean(wide**2, -1, keepdims=True) + 1e-6)


def rowwise(n, body, step=128):
    def one(i, _):
        body(pl.ds(pl.multiple_of(i * step, step), step))
        return 0
    lax.fori_loop(0, n // step, one, 0)


def silu_back(g, u, dh):
    s = jax.nn.sigmoid(g)
    silu = g * s
    return silu, (dh * u * (s + silu * (1.0 - s))).astype(BF), (dh * silu).astype(BF)


def norm_into(h, a):
    def norm(rows):
        wide = h[rows].astype(F32)
        a[rows] = (wide * norm_scale(wide)).astype(BF)
    rowwise(T, norm)


def pipelined(chunk, first, second):
    held = None
    for m in range(0, T, chunk):
        rows = slice(m, m + chunk)
        now = first(rows)
        if held is not None:
            second(*held)
        held = rows, now
    second(*held)


def fwd0(C, tr, x, wg, wu, wd, gate, up, ht, h1, at, a, hid):
    j = pl.program_id(0)

    @pl.when(j == 0)
    def _():
        norm_into(x, a)
        at[...] = a[...].T if tr else a[...]

    @pl.when(j < N)
    def _():
        def first(rows):
            return dot(a[rows], wg[...]), dot(a[rows], wu[...])

        def second(rows, gu):
            g, u = gu
            gate[rows] = g
            up[rows] = u
            v = (g * jax.nn.sigmoid(g) * u).astype(BF)
            hid[j, rows] = v
            if tr:
                ht[:, rows] = v.T
            else:
                ht[rows] = v
        pipelined(C, first, second)

    @pl.when(j >= N)
    def _():
        def first(rows):
            return sum(dot(hid[i, rows], wd[i * B:i * B + B]) for i in range(N))

        def second(rows, y):
            n = pl.ds(pl.multiple_of((j - N) * B, B), B)
            h1[rows] = (x[rows, n].astype(F32) + y.astype(BF).astype(F32)).astype(BF)
        pipelined(C, first, second)


def layer0(x, w_gate, w_up, w_down, C=512, tr=True):
    whole = pl.BlockSpec((T, T), lambda j: (0, 0))
    cap = lambda j: jnp.minimum(j, N - 1)
    cols = pl.BlockSpec((T, B), lambda j: (0, cap(j)))
    wcols = pl.BlockSpec((None, T, B), lambda j: (0, 0, cap(j)))
    late = lambda j: jnp.maximum(j - N, 0)
    wrows = pl.BlockSpec((None, 3328, B), lambda j: (0, 0, late(j)))
    rows = pl.BlockSpec((B, T), lambda j: (cap(j), 0)) if tr else cols
    o = jax.ShapeDtypeStruct
    blk = pl.BlockSpec((None, T, B), lambda j: (cap(j), 0, 0))
    return pl.pallas_call(functools.partial(fwd0, C, tr), grid=(N + 4,), in_specs=[whole, wcols, wcols, wrows],
        out_specs=[blk, blk, rows, pl.BlockSpec((T, B), lambda j: (0, late(j))), whole],
        out_shape=[o((N, T, B), F32)] * 2 + [o((3328, T) if tr else (T, 3328), BF), o((T, T), BF), o((T, T), BF)],
        scratch_shapes=[pltpu.VMEM((T, T), BF), pltpu.VMEM((N, T, B), BF)], name="layer0",
        compiler_params=pltpu.CompilerParams(vmem_limit_bytes=VMEM_BYTES))(x, w_gate, w_up, w_down)


def both1(C, tr, h, dy, wg, wu, wd, wg2, wu2, ht, dg, du, at, dh1, a, gs, us, acc):
    j = pl.program_id(0)

    @pl.when(j == 0)
    def _():
        norm_into(h, a)
        at[...] = a[...].T if tr else a[...]

    @pl.when(j < N)
    def _():
        def first(rows):
            return dot(a[rows], wg[...]), dot(a[rows], wu[...]), dot(dy[rows], wd[...], NT)

        def second(rows, parts):
            g, u, dh = parts
            silu, dgate, dup = silu_back(g, u, dh.astype(BF).astype(F32))
            v = (silu * u).astype(BF)
            if tr:
                ht[:, rows] = v.T
            else:
                ht[rows] = v
            dg[rows] = dgate
            gs[j, rows] = dgate
            du[rows] = dup
            us[j, rows] = dup
        pipelined(C, first, second)

    @pl.when(j >= N)
    def _():
        def first(rows):
            return sum(dot(gs[i, rows], wg2[:, i * B:i * B + B], NT) + dot(us[i, rows], wu2[:, i * B:i * B + B], NT) for i in range(N))

        def second(rows, y):
            n = pl.ds(pl.multiple_of((j - N) * B, B), B)
            acc[rows, n] = y
        pipelined(C, first, second)

    @pl.when(j == N + 3)
    def _():
        def back(rows):
            wide = h[rows].astype(F32)
            scale = norm_scale(wide)
            d = acc[rows].astype(BF).astype(F32)
            d = d * scale - wide * (scale * scale * scale * jnp.mean(d * wide, -1, keepdims=True))
            dh1[rows] = (dy[rows].astype(F32) + d.astype(BF).astype(F32)).astype(BF)
        rowwise(T, back)


def layer1(h, dy, w_gate, w_up, w_down, C=512, tr=True):
    cap = lambda j: jnp.minimum(j, N - 1)
    late = lambda j: jnp.maximum(j - N, 0)
    whole = pl.BlockSpec((T, T), lambda j: (0, 0))
    cols = pl.BlockSpec((T, B), lambda j: (0, cap(j)))
    wcols = pl.BlockSpec((None, T, B), lambda j: (1, 0, cap(j)))
    wrows = pl.BlockSpec((None, B, T), lambda j: (1, cap(j), 0))
    wtall = pl.BlockSpec((None, B, 3328), lambda j: (1, late(j), 0))
    rows = pl.BlockSpec((B, T), lambda j: (cap(j), 0)) if tr else cols
    o = jax.ShapeDtypeStruct
    blk = pl.BlockSpec((None, T, B), lambda j: (cap(j), 0, 0))
    return pl.pallas_call(functools.partial(both1, C, tr), grid=(N + 4,), in_specs=[whole, whole, wcols, wcols, wrows, wtall, wtall], out_specs=[rows, cols, cols, whole, whole],
        out_shape=[o((3328, T) if tr else (T, 3328), BF)] + [o((T, 3328), BF)] * 2 + [o((T, T), BF)] * 2,
        scratch_shapes=[pltpu.VMEM((T, T), BF), pltpu.VMEM((N, T, B), BF), pltpu.VMEM((N, T, B), BF), pltpu.VMEM((T, T), F32)], name="layer1",
        compiler_params=pltpu.CompilerParams(vmem_limit_bytes=VMEM_BYTES))(h, dy, w_gate, w_up, w_down, w_gate, w_up)


def back0(C, dh1, gate, up, wd, dg, du):
    def first(rows):
        return dot(dh1[rows], wd[...], NT)

    def second(rows, dh):
        _, dg[rows], du[rows] = silu_back(gate[rows], up[rows], dh.astype(BF).astype(F32))
    pipelined(C, first, second)


def back(dh1, gate, up, w_down, C=512):
    whole = pl.BlockSpec((T, T), lambda j: (0, 0))
    blk = pl.BlockSpec((None, T, B), lambda j: (j, 0, 0))
    cols = pl.BlockSpec((T, B), lambda j: (0, j))
    wrows = pl.BlockSpec((None, B, T), lambda j: (0, j, 0))
    o = jax.ShapeDtypeStruct
    return pl.pallas_call(functools.partial(back0, C), grid=(N,), in_specs=[whole, blk, blk, wrows], out_specs=[cols, cols],
        out_shape=[o((T, 3328), BF)] * 2, name="back0",
        compiler_params=pltpu.CompilerParams(vmem_limit_bytes=VMEM_BYTES))(dh1, gate, up, w_down)


def solution(mesh):
    def step(x, dy, w_gate, w_up, w_down, *moments):
        x, dy = x[0], dy[0]
        gate0, up0, hid0, h1, a0 = layer0(x, w_gate, w_up, w_down)
        hid1, dgate1, dup1, a1, dh1 = layer1(h1, dy, w_gate, w_up, w_down)
        dgate0, dup0 = back(dh1, gate0, up0, w_down)
        m, v = moments[:3], moments[3:]
        order = lambda t: (t[1], t[0], t[2])
        pad = lambda t: (*t[:2], jnp.pad(t[2], ((0, 0), (0, 3), (0, 0))))
        acts = (a0, a1, hid0, hid1, dup0, dup1, dgate0, dgate1, dh1, dy)
        new, m, v = reduce_scatter(acts, order((w_gate, w_up, w_down)), pad(order(m)), pad(order(v)))
        u, g, d = all_gather(*new)
        w = (g.reshape(w_gate.shape), u.reshape(w_up.shape), d.reshape(w_down.shape))
        cut = lambda t: (t[1], t[0], t[2][:, :13])
        return (*w, *cut(m), *cut(v))

    data, whole, rows = P(("rep", "dp"), None, None), P(), P(None, "dp", None)
    out = P("rep", None, None)
    return jax.shard_map(step, mesh=mesh, in_specs=(data, data) + (whole,) * 3 + (rows,) * 6, out_specs=(out,) * 3 + (P("rep", "dp", None),) * 6, check_vma=False)
```

time: 2540 us -> 423 us (0.17)
  blocking collectives: 1220 us -> 0 us
  starting transfers between devices: 593 us -> 0 us
  Pallas kernels: 0 us -> 385 us
  waiting for transfers between devices: 332 us -> 0 us
  matrix products: 211 us -> 0 us
  local copies, waits for them, and re-layouts: 112 us -> 36.3 us
  other arithmetic: 32.8 us -> 0.01 us
    unnamed x2 -> x0, blocking collectives: 1140 us -> none
    unnamed x96 -> x0, starting transfers between devices: 593 us -> none
    pallas_call x0 -> x5, Pallas kernels: none -> 385 us  [the longest x1 175 us: reduce_scatter(): pl.pallas_call(functools.partial(rs_kernel, list(sh)), out_shape=outs, in...]
    reshape x3 -> x0, waiting for transfers between devices: 329 us -> none  [step(): t.reshape(-1, *t.shape[2:])]
    dot_general x15 -> x0, matrix products: 211 us -> none  [the longest x5 76.5 us: layer(): up = jnp.dot(a, w['w_up'], preferred_element_type=jnp.float32)]
    reduce_sum x1 -> x0, blocking collectives: 76.1 us -> none  [of_a_group(): jnp.sum(g * g)]
    unnamed x159 -> x29, local copies, waits for them, and re-layouts: 109 us -> 35 us
  transfers between devices with their start and end apart: 99 -> 0, of which waited for: 5 -> 0; matrix products, arithmetic and copies ran while one was open for 5% -> 0% of each run, Pallas kernels for 0% -> 0%
where the time goes in v2:
time: 423 us; the launch traced here: 422 us
  Pallas kernels  385 us (91%)
  local copies, waits for them, and re-layouts  36.3 us (9%)
    pallas_call x1, Pallas kernels, reduce_scatter(): pl.pallas_call(functools.partial(rs_kernel, list(sh)), out_shape=outs, in...  175 us
    pallas_call x1, Pallas kernels, all_gather(): pl.pallas_call(functools.partial(ag_kernel, list(sh)), out_shape=outs, in...  95.7 us
    pallas_call x1, Pallas kernels, layer1(): pl.pallas_call(functools.partial(both1, C, tr), grid=(N + 4,), in_specs=[...  51.8 us
    pallas_call x1, Pallas kernels, layer0(): pl.pallas_call(functools.partial(fwd0, C, tr), grid=(N + 4,), in_specs=[w...  36.6 us
    unnamed x29, local copies, waits for them, and re-layouts  35 us
    pallas_call x1, Pallas kernels, back(): pl.pallas_call(functools.partial(back0, C), grid=(N,), in_specs=[whole, b...  25.6 us

profile of v2, /device:TPU:1, one launch (start us, length us, event | category | flops | bytes accessed | tf_op | source)
XLA Modules:
  0.0 422.2 jit_solution(3429257473239899151)
XLA Ops:
  0.6 36.6 %layer0.1 = (f32[13,1024,256]{2,1,0:T(8,128)}, f32[13,1024,256]{2,1,0:T(8,128)}, bf16[3328,1024]{1,0:T(8,128)(2,1)}, bf16[1024,1024]{1,0:T(8,128)(2,1)}, bf16[1024,1024]{1,0:T(8,128)(2,1)}) custom-call(bf16[1024,1024]{1,0:T(8,128)(2,1)} %bitcast.20, bf16[2,1024,3328]{2,1,0:T(8,128)(2,1)} %wg2.1, bf16[2,1024,3328]{2,1,0:T(8,128)(2,1)} %wu2.1, ...), custom_call_target="tpu_custom_call" | custom-call | tf_op jit(solution)/shard_map/layer0/pallas_call | solution.py:910
  37.2 51.8 %layer1.1 = (bf16[3328,1024]{1,0:T(8,128)(2,1)}, bf16[1024,3328]{1,0:T(8,128)(2,1)}, bf16[1024,3328]{1,0:T(8,128)(2,1)}, bf16[1024,1024]{1,0:T(8,128)(2,1)}, bf16[1024,1024]{1,0:T(8,128)(2,1)}) custom-call(bf16[1024,1024]{1,0:T(8,128)(2,1)} %get-tuple-element.34.h, bf16[1024,1024]{1,0:T(8,128)(2,1)} %bitcast.18, bf16[2,1024,3328]{2,1,0:T(8,128)(2,1)} %wg2.1, ...), custom_call_target="tpu_custom_call" | custom-call | tf_op jit(solution)/shard_map/layer1/pallas_call | solution.py:976
  89.1 25.6 %back0.1 = (bf16[1024,3328]{1,0:T(8,128)(2,1)}, bf16[1024,3328]{1,0:T(8,128)(2,1)}) custom-call(bf16[1024,1024]{1,0:T(8,128)(2,1)} %get-tuple-element.38.dh1.refs_8_, f32[13,1024,256]{2,1,0:T(8,128)} %get-tuple-element.39.gate, f32[13,1024,256]{2,1,0:T(8,128)} %get-tuple-element.40.up, bf16[2,3328,1024]{2,1,0:T(8,128)(2,1)} %wd.5), custom_call_target="tpu_custom_call" | custom-call | tf_op jit(solution)/shard_map/back0/pallas_call | solution.py:997
  114.6 0.9 copy.20
  115.6 0.7 pad.7.refs_15_
  116.2 0.9 copy.21
  117.2 0.7 pad.8.refs_18_
  117.9 175.5 %reduce_scatter.1 = (bf16[2,8,1664]{2,1,0:T(8,128)(2,1)}, bf16[2,8,1664]{2,1,0:T(8,128)(2,1)}, bf16[2,2,16,512]{3,2,1,0:T(8,128)(2,1)}, f32[2,4,3328]{2,1,0:T(4,...) custom-call(bf16[1024,1024]{1,0:T(8,128)(2,1)} %get-tuple-element.33, ...), custom_call_target="tpu_custom_call" | custom-call | tf_op jit(solution)/shard_map/reduce_scatter/pallas_call | solution.py:652
  293.4 95.7 %all_gather.1 = (bf16[2,4,4,8,8,3328]{5,4,3,2,1,0:T(8,128)(2,1)}, bf16[2,4,4,8,8,3328]{5,4,3,2,1,0:T(8,128)(2,1)}, bf16[2,4,4,26,8,1024]{5,4,3,2,1,0:T(8,128)(2,1)}) custom-call(bf16[2,8,1664]{2,1,0:T(8,128)(2,1)} %get-tuple-element.45.refs_0_, bf16[2,8,1664]{2,1,0:T(8,128)(2,1)} %get-tuple-element.46.refs_1_, bf16[2,2,16,512]{3,2,1,0:T(8,128)(2,1)} %get-tuple-element.47.refs_2_), custom_call_target="tpu_custom_call" | custom-call | tf_op jit(solution)/shard_map/all_gather/pallas_call | solution.py:814
  389.1 1.6 copy.22
  390.7 1.6 copy.23
  392.4 0.0 copy-start
  392.4 0.0 slice-start
  392.4 0.0 slice-start.1
  392.4 15.1 %copy.31 = bf16[2,1024,3328]{2,1,0:T(8,128)(2,1)} copy(bf16[2,1024,3328]{2,1,0:T(8,128)(2,1)} %bitcast.17) | data formatting | bytes 27262976
  407.4 0.0 copy-done
  407.4 0.0 slice-start.2
  407.4 0.0 slice-start.3
  407.4 6.6 %copy.32 = bf16[2,1024,3328]{2,1,0:T(8,128)(2,1)} copy(bf16[2,1024,3328]{2,1,0:T(8,128)(2,1)S(1)} %bitcast.16) | data formatting | bytes 27262976
  414.0 0.0 slice-done
  414.0 0.0 slice-done.1
  414.0 0.0 slice-done.2
  414.0 0.5 slice-done.3
  414.5 5.1 %copy.33 = bf16[2,3328,1024]{2,1,0:T(8,128)(2,1)} copy(bf16[2,3328,1024]{2,1,0:T(8,128)(2,1)S(1)} %bitcast.15) | data formatting | bytes 27262976
  419.7 0.0 copy-done.4
  419.7 0.6 copy.34
  420.3 0.0 copy-done.3
  420.3 0.6 copy.35
  420.9 0.0 copy-done.2
  420.9 0.6 copy.36
  421.6 0.0 copy-done.1
  421.6 0.6 copy.37
  (5 shorter events, 0.0 us)
Async XLA Ops:
  392.4 15.1 %copy-start = (bf16[2,4,4,8,8,3328]{5,4,3,2,1,0:T(8,128)(2,1)S(1)}, bf16[2,4,4,8,8,3328]{5,4,3,2,1,0:T(8,128)(2,1)}, u32[]{:S(2)}) copy-start(bf16[2,4,4,8,8,3328]{5,4,3,2,1,0:T(8,128)(2,1)} %get-tuple-element.49) | copy-start | bytes 40894468
  392.4 21.6 %slice-start = ((s8[13631488]{0:T(1024)(128)(4,1)}), s8[4194304]{0:T(1024)(128)(4,1)S(1)}, s32[]{:S(2)}) async-start(s8[13631488]{0:T(1024)(128)(4,1)} %bitcast.13), calls=%async_computation | async-start | bytes 8388608
  392.4 21.6 %slice-start.1 = ((s8[13631488]{0:T(1024)(128)(4,1)}), s8[4194304]{0:T(1024)(128)(4,1)S(1)}, s32[]{:S(2)}) async-start(s8[13631488]{0:T(1024)(128)(4,1)} %bitcast.13), calls=%async_computation.1 | async-start | bytes 8388608
  407.4 6.6 %slice-start.2 = ((s8[13631488]{0:T(1024)(128)(4,1)}), s8[4194304]{0:T(1024)(128)(4,1)S(1)}, s32[]{:S(2)}) async-start(s8[13631488]{0:T(1024)(128)(4,1)} %bitcast.13), calls=%async_computation.2 | async-start | bytes 8388608
  407.4 7.1 %slice-start.3 = ((s8[13631488]{0:T(1024)(128)(4,1)}), s8[1048576]{0:T(1024)(128)(4,1)S(1)}, s32[]{:S(2)}) async-start(s8[13631488]{0:T(1024)(128)(4,1)} %bitcast.13), calls=%async_computation.3 | async-start | bytes 2097152
  414.5 5.1 %copy-start.4 = (f32[2,4,3328]{2,1,0:T(4,128)S(1)}, f32[2,4,3328]{2,1,0:T(4,128)}, u32[]{:S(2)}) copy-start(f32[2,4,3328]{2,1,0:T(4,128)} %get-tuple-element.78) | copy-start | bytes 319492
  414.5 5.8 %copy-start.3 = (f32[2,4,3328]{2,1,0:T(4,128)S(1)}, f32[2,4,3328]{2,1,0:T(4,128)}, u32[]{:S(2)}) copy-start(f32[2,4,3328]{2,1,0:T(4,128)} %get-tuple-element.79) | copy-start | bytes 319492
  414.5 6.4 %copy-start.2 = (f32[2,4,3328]{2,1,0:T(4,128)S(1)}, f32[2,4,3328]{2,1,0:T(4,128)}, u32[]{:S(2)}) copy-start(f32[2,4,3328]{2,1,0:T(4,128)} %get-tuple-element.81) | copy-start | bytes 319492
  414.5 7.1 %copy-start.1 = (f32[2,4,3328]{2,1,0:T(4,128)S(1)}, f32[2,4,3328]{2,1,0:T(4,128)}, u32[]{:S(2)}) copy-start(f32[2,4,3328]{2,1,0:T(4,128)} %get-tuple-element.82) | copy-start | bytes 319492

commit v3 on v2

--- a/solution.py
+++ b/solution.py
@@ -60,12 +60,172 @@
     return pltpu.make_async_remote_copy(src_ref=src, dst_ref=dst, send_sem=ss, recv_sem=rs, device_id=to, device_id_type=MESH)
 
 
-GROUPS = [(1, "d"), (1, "u"), (1, "g"), (0, "u"), (0, "d"), (0, "g")]
-OFFSETS = (2, 1, 3, 0)
+T = 1024
+B = 256
+N = 3328 // B
+NT = (((1,), (1,)), ((), ()))
+
+
+def dot(a, b, dims=(((1,), (0,)), ((), ()))):
+    return lax.dot_general(a, b, dims, preferred_element_type=F32)
+
+
+def norm_scale(wide):
+    return lax.rsqrt(jnp.mean(wide**2, -1, keepdims=True) + 1e-6)
+
+
+def rowwise(n, body, step=128):
+    def one(i, _):
+        body(pl.ds(pl.multiple_of(i * step, step), step))
+        return 0
+    lax.fori_loop(0, n // step, one, 0)
+
+
+def silu_back(g, u, dh):
+    s = jax.nn.sigmoid(g)
+    silu = g * s
+    return silu, (dh * u * (s + silu * (1.0 - s))).astype(BF), (dh * silu).astype(BF)
+
+
+def norm_into(h, a):
+    def norm(rows):
+        wide = h[rows].astype(F32)
+        a[rows] = (wide * norm_scale(wide)).astype(BF)
+    rowwise(T, norm)
+
+
+def pipelined(chunk, first, second):
+    held = None
+    for m in range(0, T, chunk):
+        rows = slice(m, m + chunk)
+        now = first(rows)
+        if held is not None:
+            second(*held)
+        held = rows, now
+    second(*held)
+
+
+def fwd0(C, tr, x, wg, wu, wd, gate, up, ht, h1, at, a, hid):
+    j = pl.program_id(0)
+
+    @pl.when(j == 0)
+    def _():
+        norm_into(x, a)
+        at[...] = a[...].T if tr else a[...]
+
+    @pl.when(j < N)
+    def _():
+        def first(rows):
+            return dot(a[rows], wg[...]), dot(a[rows], wu[...])
+
+        def second(rows, gu):
+            g, u = gu
+            gate[rows] = g
+            up[rows] = u
+            v = (g * jax.nn.sigmoid(g) * u).astype(BF)
+            hid[j, rows] = v
+            if tr:
+                ht[:, rows] = v.T
+            else:
+                ht[rows] = v
+        pipelined(C, first, second)
+
+    @pl.when(j >= N)
+    def _():
+        def first(rows):
+            return sum(dot(hid[i, rows], wd[i * B:i * B + B]) for i in range(N))
+
+        def second(rows, y):
+            n = pl.ds(pl.multiple_of((j - N) * B, B), B)
+            h1[rows] = (x[rows, n].astype(F32) + y.astype(BF).astype(F32)).astype(BF)
+        pipelined(C, first, second)
+
+
+def layer0(x, w_gate, w_up, w_down, C=512, tr=True):
+    whole = pl.BlockSpec((T, T), lambda j: (0, 0))
+    cap = lambda j: jnp.minimum(j, N - 1)
+    cols = pl.BlockSpec((T, B), lambda j: (0, cap(j)))
+    wcols = pl.BlockSpec((None, T, B), lambda j: (0, 0, cap(j)))
+    late = lambda j: jnp.maximum(j - N, 0)
+    wrows = pl.BlockSpec((None, 3328, B), lambda j: (0, 0, late(j)))
+    rows = pl.BlockSpec((B, T), lambda j: (cap(j), 0)) if tr else cols
+    o = jax.ShapeDtypeStruct
+    blk = pl.BlockSpec((None, T, B), lambda j: (cap(j), 0, 0))
+    return pl.pallas_call(functools.partial(fwd0, C, tr), grid=(N + 4,), in_specs=[whole, wcols, wcols, wrows],
+        out_specs=[blk, blk, rows, pl.BlockSpec((T, B), lambda j: (0, late(j))), whole],
+        out_shape=[o((N, T, B), F32)] * 2 + [o((3328, T) if tr else (T, 3328), BF), o((T, T), BF), o((T, T), BF)],
+        scratch_shapes=[pltpu.VMEM((T, T), BF), pltpu.VMEM((N, T, B), BF)], name="layer0",
+        compiler_params=pltpu.CompilerParams(vmem_limit_bytes=VMEM_BYTES))(x, w_gate, w_up, w_down)
+
+
+def both1(C, h, dy, wg, wu, wd, wg2, wu2, dwd, dwg, dwu, dh1, a, at, gs, us, acc):
+    j = pl.program_id(0)
+
+    @pl.when(j == 0)
+    def _():
+        norm_into(h, a)
+        at[...] = a[...].T
+
+    @pl.when(j < N)
+    def _():
+        g, u = dot(a[...], wg[...]), dot(a[...], wu[...])
+        dh = dot(dy[...], wd[...], NT).astype(BF).astype(F32)
+        silu, dgate, dup = silu_back(g, u, dh)
+        gs[j] = dgate
+        us[j] = dup
+        hid = (silu * u).astype(BF)
+        dwg[...] = dot(at[...], dgate).astype(BF)
+        dwu[...] = dot(at[...], dup).astype(BF)
+        dwd[...] = dot(hid.T, dy[...]).astype(BF)
+
+    @pl.when(j >= N)
+    def _():
+        y = sum(dot(gs[i], wg2[:, i * B:i * B + B], NT) + dot(us[i], wu2[:, i * B:i * B + B], NT) for i in range(N))
+        acc[:, pl.ds(pl.multiple_of((j - N) * B, B), B)] = y
+
+    @pl.when(j == N + 3)
+    def _():
+        def back(rows):
+            wide = h[rows].astype(F32)
+            scale = norm_scale(wide)
+            d = acc[rows].astype(BF).astype(F32)
+            d = d * scale - wide * (scale * scale * scale * jnp.mean(d * wide, -1, keepdims=True))
+            dh1[rows] = (dy[rows].astype(F32) + d.astype(BF).astype(F32)).astype(BF)
+        rowwise(T, back)
+
+
+def layer1(h, dy, w_gate, w_up, w_down, C=512):
+    cap = lambda j: jnp.minimum(j, N - 1)
+    late = lambda j: jnp.maximum(j - N, 0)
+    whole = pl.BlockSpec((T, T), lambda j: (0, 0))
+    cols = pl.BlockSpec((T, B), lambda j: (0, cap(j)))
+    wcols = pl.BlockSpec((None, T, B), lambda j: (1, 0, cap(j)))
+    wrows = pl.BlockSpec((None, B, T), lambda j: (1, cap(j), 0))
+    wtall = pl.BlockSpec((None, B, 3328), lambda j: (1, late(j), 0))
+    rows = pl.BlockSpec((B, T), lambda j: (cap(j), 0))
+    o = jax.ShapeDtypeStruct
+    return pl.pallas_call(functools.partial(both1, C), grid=(N + 4,), in_specs=[whole, whole, wcols, wcols, wrows, wtall, wtall], out_specs=[rows, cols, cols, whole],
+        out_shape=[o((3328, T), BF)] + [o((T, 3328), BF)] * 2 + [o((T, T), BF)],
+        scratch_shapes=[pltpu.VMEM((T, T), BF)] * 2 + [pltpu.VMEM((N, T, B), BF)] * 2 + [pltpu.VMEM((T, T), F32)], name="layer1",
+        compiler_params=pltpu.CompilerParams(vmem_limit_bytes=VMEM_BYTES))(h, dy, w_gate, w_up, w_down, w_gate, w_up)
+
+
+TASKS = (3, 3, 3, 4)
+
+
+def jobs_of(layer):
+    rank = {}
+    for i, u in enumerate(UNITS):
+        if u[0] == layer:
+            n = SIZE[u[4][0]]
+            h = n // 2
+            for at, off in enumerate([h] + [s * (h - k) for k in range(1, h) for s in (1, -1)] + [0]):
+                rank[i, off] = (at / n, i)
+    return sorted(rank, key=rank.get)
 
 
 def plan():
-    RATE, LAT, TASK, DRATE, DLAT = 46.0e3, 2.6, 1.15, 550.0e3, 1.7
+    RATE, LAT, TASK, DRATE, DLAT = 46.0e3, 2.6, 3.3, 500.0e3, 2.0
     free, heap, seq = {}, [], [0]
 
     def send(t, link, nbytes):
@@ -80,13 +240,14 @@
         ring[0, i] = (o[0], 4 * DEPTH[a] * 8 * cols * 2)
         ring[1, i] = (o[1], DEPTH[a] * 8 * cols * 2)
         ring[2, (l, a)] = (LASTDIM[a], TALL[a] * 8 * WIDTH[a] * 2)
-    have = {}
-    got, steps, now = {}, [], 4.0
-
-    def ready(i, off):
-        l, a, _, _, o = UNITS[i]
-        need = [(l, a, off % 4)] if o[0] == "x" else [(l, a, b) for b in range(4)]
-        return max(have[n] for n in need) if all(n in have for n in need) else None
+    arrive, got, steps, now = {}, {}, [], 2.0
+
+    def exchange(layer, t):
+        for i, off in jobs_of(layer):
+            t += ring[0, i][1] / DRATE
+            arrive[i, off] = t + DLAT
+            if off == SIZE[UNITS[i][4][0]] // 2:
+                push(arrive[i, off], ("start", 0, i, 0, 0))
 
     def run(until):
         nonlocal now
@@ -96,11 +257,9 @@
             kind, level, key, s, k = ev
             dim, nbytes = ring[level, key]
             h = SIZE[dim] // 2
-            if level == 0 and kind == "step" and k < h:
-                when = ready(key, s * (h - k))
-                if when is None or when > t:
-                    push(t + 0.5 if when is None else when, ev)
-                    continue
+            if level == 0 and kind == "step" and k < h and arrive[key, s * (h - k)] > t:
+                push(arrive[key, s * (h - k)], ev)
+                continue
             now = max(now, t)
             taken.append(ev)
             cost = 0.15 + nbytes * (4 + 2 * level) / 7.0e6
@@ -126,26 +285,17 @@
                 else:
                     push(now, ("end", 2, key, 0, 0))
         return taken
-    dfree = 0.0
-    for l, a in GROUPS:
-        own = {}
-        steps.append(((l, a), run(now)))
-        for s in range(8):
-            now += TASK
-            block, half = (s // 2, s % 2) if a == "d" else (s % 4, s // 4)
-            off = OFFSETS[block]
-            if half == 0:
-                dfree = max(dfree, now) + 4 * TILES[a] * 8 * WIDTH[a] * 2 / DRATE
-                own[off] = dfree + DLAT
-            else:
-                have[l, a, off] = max(now + 2.0, own[off])
-            if a == "d" and half == 1 and block == 0:
-                push(have[l, a, off], ("start", 0, next(i for i, u in enumerate(UNITS) if u[:2] == (l, a) and u[4][0] == "x"), 0, 0))
-        for i, u in enumerate(UNITS):
-            if u[:2] == (l, a) and not (a == "d" and u[4][0] == "x"):
-                push(ready(i, SIZE[u[4][0]] // 2), ("start", 0, i, 0, 0))
-    steps.append((None, run(float("inf"))))
+    exchange(1, now)
+    now = max(now, FIRST)
+    for n in TASKS:
+        steps.append(run(now))
+        now += n * TASK
+    exchange(0, now)
+    steps.append(run(float("inf")))
     return steps, now, free
+
+
+FIRST = 6.5
 
 
 def addsum(dst, srcs):
@@ -184,23 +334,26 @@
     sh["new_d"] = pltpu.VMEM((2, 2, 16, 512), BF)
     for i, u in enumerate(UNITS):
         h = SIZE[u[4][0]] // 2
-        if not u[0]:
-            sh["own_%d" % i] = pltpu.VMEM(block_shape(i, 0), BF)
         sh["slot0_%d" % i] = pltpu.VMEM((2, h) + block_shape(i, 0), BF)
         sh["slot1_%d" % i] = pltpu.VMEM((2, 2) + block_shape(i, 1), BF)
         for n in "rs":
             sh["%s0_%d" % (n, i)] = sem((2, h))
             sh["%s1_%d" % (n, i)] = sem((2, 2))
     sh["ownsem"] = sem((len(UNITS),))
-    sh["left"] = pltpu.VMEM((1024, 1024), BF)
-    sh["leftsem"] = sem((1,))
-    sh["right"] = pltpu.VMEM((2, 1024, 1664), BF)
-    sh["rightsem"] = sem((2,))
-    sh["res_u"] = pltpu.VMEM((2, 4, 8, 8, 1664), BF)
-    sh["res_d"] = pltpu.VMEM((2, 4, 26, 8, 512), BF)
-    sh["dr"] = sem((6, 4))
-    sh["ds"] = sem((6, 4))
-    sh["os"] = sem((6, 4))
+    sh["dh"] = pltpu.VMEM((1024, 1024), BF)
+    sh["at"] = pltpu.VMEM((1024, 1024), BF)
+    sh["gate"] = pltpu.VMEM((2, 1024, 256), F32)
+    sh["up"] = pltpu.VMEM((2, 1024, 256), F32)
+    sh["wd"] = pltpu.VMEM((2, 256, 1024), BF)
+    sh["ht"] = pltpu.VMEM((2, 256, 1024), BF)
+    sh["res_u"] = pltpu.VMEM((2, 4, 4, 8, 8, 256), BF)
+    sh["res_g"] = pltpu.VMEM((2, 4, 4, 8, 8, 256), BF)
+    sh["res_d"] = pltpu.VMEM((2, 32, 8, 1024), BF)
+    sh["insem"] = sem((4, 2))
+    sh["outsem"] = sem((3, 2))
+    sh["wholesem"] = sem((2,))
+    sh["dr"] = sem((64,))
+    sh["ds"] = sem((64,))
     sh["ar_z"] = pltpu.VMEM((16, 1, 128), F32)
     sh["ar_p"] = pltpu.VMEM((16, 1, 128), F32)
     sh["arsem"] = sem((4, 16))
@@ -212,13 +365,15 @@
 
 
 def rs_kernel(names, *refs):
-    act = {(n, l): refs[2 * j + l] for j, n in enumerate(("a", "h", "u", "g", "y")) for l in (0, 1)}
-    weights = {a: refs[10 + j] for j, a in enumerate("ugd")}
-    moments = {a: (refs[13 + j], refs[16 + j]) for j, a in enumerate("ugd")}
-    new = {a: refs[19 + j] for j, a in enumerate("ugd")}
-    new_moments = {a: (refs[22 + j], refs[25 + j]) for j, a in enumerate("ugd")}
-    mine = {a: refs[28 + j] for j, a in enumerate("ugd")}
-    S = dict(zip(names, refs[31:], strict=True))
+    given = {a: refs[j] for j, a in enumerate("ugd")}
+    acts = dict(zip(("dh", "at", "gate", "up", "ht"), refs[3:8], strict=True))
+    weights = {a: refs[8 + j] for j, a in enumerate("ugd")}
+    w_down = refs[11]
+    moments = {a: (refs[12 + j], refs[15 + j]) for j, a in enumerate("ugd")}
+    new = {a: refs[18 + j] for j, a in enumerate("ugd")}
+    new_moments = {a: (refs[21 + j], refs[24 + j]) for j, a in enumerate("ugd")}
+    made = {a: refs[27 + j] for j, a in enumerate("ugd")}
+    S = dict(zip(names, refs[30:], strict=True))
     at = coords()
     c, x = at["c"], at["x"]
     sib = device({**at, "c": 1 - c})
@@ -237,25 +392,24 @@
         w = WIDTH[a]
         return pl.ds(pl.multiple_of((c if which else 1 - c) * w, 128), w)
 
-    def left(l, a):
-        return pltpu.make_async_copy(act["y" if a == "d" else "a", l], S["left"], S["leftsem"].at[0])
-    loads = []
-    for l, a in GROUPS:
-        loads += [(l, a, n) for n in range(4 if a == "d" else 2)]
-
-    def right(n):
-        l, a, k = loads[n]
-        if a == "d":
-            b = spots["x"][OFFSETS[k]]
-            src = act["h", l].at[pl.ds(pl.multiple_of(832 * b, 832), 832)]
-            dst = S["right"].at[n % 2, pl.ds(0, 832), pl.ds(0, 1024)]
-        else:
-            src = act[a, l].at[:, halfcols(a, k)]
-            dst = S["right"].at[n % 2]
-        return pltpu.make_async_copy(src, dst, S["rightsem"].at[n % 2])
-    left(*GROUPS[0]).start()
-    right(0).start()
-    right(1).start()
+    def inputs(j, p):
+        rows = pl.ds(pl.multiple_of(j * 256, 256), 256)
+        pairs = ((acts["gate"].at[j], S["gate"]), (acts["up"].at[j], S["up"]), (w_down.at[0, rows], S["wd"]), (acts["ht"].at[rows], S["ht"]))
+        return [pltpu.make_async_copy(src, dst.at[p], S["insem"].at[n, p]) for n, (src, dst) in enumerate(pairs)]
+
+    def outputs(j, p):
+        cols = pl.ds(pl.multiple_of(j * 256, 256), 256)
+        pairs = [(S["res_" + a].at[p], made[a].at[:, :, :, :, cols], n) for n, a in enumerate("ug")]
+        for q in range(4):
+            tile = j * 32 + 8 * q
+            pairs.append((S["res_d"].at[p, pl.ds(8 * q, 8)], made["d"].at[lax.div(tile, 104), pl.ds(lax.rem(tile, 104), 8)], 2))
+        return [pltpu.make_async_copy(src, dst, S["outsem"].at[n, p]) for src, dst, n in pairs]
+
+    def outputs_done(p):
+        return [pltpu.make_async_copy(S["res_" + a].at[p], S["res_" + a].at[p], S["outsem"].at[n, p]) for n, a in enumerate("ugd")]
+    whole = [pltpu.make_async_copy(acts[n], S[n], S["wholesem"].at[k]) for k, n in enumerate(("dh", "at"))]
+    for cp in [*inputs(0, 0), *whole]:
+        cp.start()
 
     moment_copies = []
     for j, a in enumerate("ugd"):
@@ -284,6 +438,17 @@
         idx = view(a, o, at, level, v)
         return ref.at[(l, *idx, *([ALL] * (4 - len(idx))), pl.ds(col, n))]
 
+    def pairs(i, off, which, dst):
+        l, a, col, n, o = UNITS[i]
+        cols = pl.ds(pl.multiple_of((c if which else 1 - c) * WIDTH[a] + col, 128), n)
+        v = pos(i, 0, off)
+        if a == "d" and not l:
+            if o[0] == "x":
+                return [(made["d"].at[v, pl.ds(26 * q, 26), :, cols], dst.at[q]) for q in range(4)]
+            return [(made["d"].at[:, pl.ds(26 * v, 26), :, cols], dst)]
+        idx = view(a, o, at, 0, v)
+        return [((given if l else made)[a].at[(*idx, *([ALL] * (4 - len(idx))), cols)], dst)]
+
     def pos(i, level, off):
         a = UNITS[i][1]
         dim = UNITS[i][4][level] if level < 2 else LASTDIM[a]
@@ -292,42 +457,33 @@
             return spots[dim][off]
         return windows[off] if a == "d" else pl.ds(spots[dim][off], 1)
 
-    def result(gi, block, half):
-        l, a = GROUPS[gi]
-        b = spots["x"][OFFSETS[block]]
-        task = 2 * block + half if a == "d" else 4 * half + block
-        buf = S["res_d" if a == "d" else "res_u"].at[task % 2]
-        if half == 0:
-            return lambda: remote_copy(buf, S["loc_" + a].at[l, b], S["ds"].at[gi, block], S["dr"].at[gi, block], sib)
-        return lambda: pltpu.make_async_copy(buf, mine[a].at[l, b], S["os"].at[gi, block])
-
-    def offset_of(block):
-        return lax.select(block == 0, 2, lax.select(block == 1, 1, lax.select(block == 2, 3, 0)))
-
-    def task_of(a, s):
-        return (s // 2, s % 2) if a == "d" else (s % 4, s // 4)
-
-    out_waited, sib_waited = set(), set()
-
-    def wait_out(gi, block, half):
-        if (gi, block, half) not in out_waited:
-            out_waited.add((gi, block, half))
-            cp = result(gi, block, half)()
-            cp.wait() if half else cp.wait_send()
+    jobs = {k: n for n, k in enumerate(jobs_of(1) + jobs_of(0))}
+
+    def landing(i, off):
+        return region(S["loc_" + UNITS[i][1]], i, 0, pos(i, 0, off))
+
+    def exchange(layer):
+        for i, off in jobs_of(layer):
+            n = jobs[i, off]
+            for src, dst in pairs(i, off, 0, landing(i, off)):
+                remote_copy(src, dst, S["ds"].at[n], S["dr"].at[n], sib).start()
+
+    def exchanged(i, off):
+        ref = landing(i, off)
+        return remote_copy(ref, ref, S["ds"].at[jobs[i, off]], S["dr"].at[jobs[i, off]], sib)
+    exchange(1)
+    sib_waited = set()
 
     def wait_terms(i, off):
-        l, a, _, _, o = UNITS[i]
-        gi = GROUPS.index((l, a))
-        for block, b in enumerate(OFFSETS):
-            if o[0] == "x" and b != off % 4:
-                continue
-            wait_out(gi, block, 1)
-            if (gi, block) not in sib_waited:
-                sib_waited.add((gi, block))
-                result(gi, block, 0)().wait_recv()
+        off %= SIZE[UNITS[i][4][0]]
+        n = SIZE[UNITS[i][4][0]]
+        off = off - n if off > n // 2 else off
+        if (i, off) not in sib_waited:
+            sib_waited.add((i, off))
+            exchanged(i, off).wait_recv()
 
     uses = {a: [] for a in "ugd"}
-    for _, events in steps:
+    for events in steps:
         for kind, level, key, s, k in events:
             if level == 0:
                 h = SIZE[UNITS[key][4][0]] // 2
@@ -337,45 +493,34 @@
     fetched = {a: 0 for a in "ugd"}
 
     def stage(a, n):
-        i, off = uses[a][n]
-        buf = S["stage_" + a].at[n % NB, :, :, :, pl.ds(0, UNITS[i][3])]
-        return pltpu.make_async_copy(region(mine[a], i, 0, pos(i, 0, off)), buf, S["stsem_" + a].at[n % NB]), buf
-
-    complete = set()
+        i = uses[a][n][0]
+        return S["stage_" + a].at[n % NB, :, :, :, pl.ds(0, UNITS[i][3])]
+
+    layers = {1}
 
     def fetch_ahead(a):
         while fetched[a] < min(len(uses[a]), nth[a] + NB):
-            i, off = uses[a][fetched[a]]
-            if UNITS[i][:2] not in complete:
+            n = fetched[a]
+            i, off = uses[a][n]
+            if UNITS[i][0] not in layers:
                 return
-            wait_terms(i, off)
-            stage(a, fetched[a])[0].start()
+            for src, dst in pairs(i, off, 1, stage(a, n)):
+                pltpu.make_async_copy(src, dst, S["stsem_" + a].at[n % NB]).start()
             fetched[a] += 1
 
-    def fetch_now(a, n):
-        if fetched[a] == n:
-            wait_terms(*uses[a][n])
-            stage(a, n)[0].start()
-            fetched[a] += 1
-
     own_fetched = set()
 
     sent = {}
 
     def own_buffer(i):
-        return S["slot0_%d" % i].at[0, 0] if UNITS[i][0] else S["own_%d" % i]
-
-    def own(i):
-        return pltpu.make_async_copy(region(mine[UNITS[i][1]], i, 0, pos(i, 0, 0)), own_buffer(i), S["ownsem"].at[i])
+        return S["slot0_%d" % i].at[0, 0]
 
     def fetch_own(i):
-        if i in own_fetched or (UNITS[i][0] and i not in sent):
-            return
-        if UNITS[i][0]:
+        if i not in own_fetched and i in sent:
             sent[i]().wait_send()
-        own_fetched.add(i)
-        wait_terms(i, 0)
-        own(i).start()
+            own_fetched.add(i)
+            for src, dst in pairs(i, 0, 1, own_buffer(i)):
+                pltpu.make_async_copy(src, dst, S["ownsem"].at[i]).start()
 
     def operands(level, i, off):
         _, a, _, _, o = UNITS[i]
@@ -385,9 +530,9 @@
             wait_terms(i, off)
             n = nth[a]
             assert uses[a][n] == (i, off)
-            fetch_now(a, n)
-            cp, buf = stage(a, n)
-            cp.wait()
+            assert fetched[a] > n
+            buf = stage(a, n)
+            pltpu.make_async_copy(buf, buf, S["stsem_" + a].at[n % NB]).wait()
             nth[a] += 1
             return [buf, here]
         h = SIZE[o[0]] // 2
@@ -436,7 +581,7 @@
                 wait_terms(key, 0)
                 fetch_own(key)
                 assert key in own_fetched
-                own(key).wait()
+                pltpu.make_async_copy(own_buffer(key), own_buffer(key), S["ownsem"].at[key]).wait()
             dst = (lambda: S["first_" + tag]) if level == 2 else (lambda: region(S["loc_" + a], key, level, pos(key, level, h)))
             if level < 2:
                 addsum(dst(), operands(level, key, h))
@@ -479,7 +624,7 @@
                         hm = half(m, w, level, a)
                         addsum(hm, ([hm] if w == d else []) + [half(r, w, level, a) for r in ops])
         send(lambda: slot.at[d, k - 1], d, k)
-        if (level, d, k) == (0, 0, 1) and l:
+        if (level, d, k) == (0, 0, 1):
             sent[key] = pend.pop()
         if level == 0:
             fetch_ahead(a)
@@ -490,75 +635,52 @@
             ops = [cut(o, uc) for o in operands(2, i, 0)] + [cut(S["slot2_%d%s" % (l, a)].at[d, h - 1], sc) for d in (0, 1)]
             addsum(cut(S["red_" + a].at[l], sc), ops)
 
-    filled = {}
-    holds = ("y", 1)
-    left(*GROUPS[0]).wait()
-    for gi, (l, a) in enumerate(GROUPS):
-        wants = ("y" if a == "d" else "a", l)
-        if wants != holds:
-            left(l, a).start()
-            left(l, a).wait()
-            holds = wants
-        first_load = sum(4 if g[1] == "d" else 2 for g in GROUPS[:gi])
-
-        for k in (0, 1):
-            if (a == "d", k) in filled:
-                wait_out(*filled[a == "d", k])
-        for ev in steps[gi][1]:
+    for a in "ugd":
+        fetch_ahead(a)
+    first = 0
+    for n, events in zip(TASKS, steps, strict=False):
+        for ev in events:
             event(ev)
-        res = S["res_d" if a == "d" else "res_u"]
-
-        def away(s, block, half_, gi=gi, l=l, a=a, res=res):
-            b = lax.rem(x + offset_of(block), 4)
-            buf = res.at[lax.rem(s, 2)]
-            return (remote_copy(buf, S["loc_" + a].at[l, b], S["ds"].at[gi, block], S["dr"].at[gi, block], sib),
-                    pltpu.make_async_copy(buf, mine[a].at[l, b], S["os"].at[gi, block]))
-
-        def loop(s, _, l=l, a=a, first_load=first_load, res=res, away=away):
-            block, half_ = (lax.div(s, 2), lax.rem(s, 2)) if a == "d" else (lax.rem(s, 4), lax.div(s, 4))
-            n = lax.rem(block, 2) if a == "d" else half_
-
-            @pl.when((half_ if a == "d" else block) == 0)
+        if not first:
+            for cp in whole:
+                cp.wait()
+
+        def task(j, _):
+            p = lax.rem(j, 2)
+            for cp in inputs(j, p):
+                cp.wait()
+
+            @pl.when(j < 12)
             def _():
-                src, buf = (act["h", l].at[pl.ds(0, 832)], S["right"].at[n, pl.ds(0, 832), pl.ds(0, 1024)]) if a == "d" else (act[a, l].at[:, pl.ds(0, 1664)], S["right"].at[n])
-                pltpu.make_async_copy(src, buf, S["rightsem"].at[n]).wait()
-            before = (lax.div(s - 2, 2), half_) if a == "d" else (lax.rem(s - 2, 4), lax.div(s - 2, 4))
-            send, keep = away(s, *before)
-
-            @pl.when((s >= 2) & (before[1] == 0))
+                for cp in inputs(j + 1, 1 - p):
+                    cp.start()
+
+            @pl.when(j >= 2)
             def _():
-                send.wait_send()
-
-            @pl.when((s >= 2) & (before[1] == 1))
-            def _():
-                keep.wait()
-            if a == "d":
-                cols = pl.ds(pl.multiple_of(lax.select(half_ == 0, 1 - c, c) * 512, 512), 512)
-                t = jnp.dot(S["right"][n, pl.ds(0, 832), pl.ds(0, 1024)], S["left"][:, cols], preferred_element_type=F32)
-                res[lax.rem(s, 2)] = t.reshape(4, 26, 8, 512).astype(BF)
-            else:
-                rows = pl.ds(pl.multiple_of(lax.rem(x + offset_of(block), 4) * 256, 256), 256)
-                t = jnp.dot(S["left"][rows], S["right"][half_], preferred_element_type=F32)
-                res[lax.rem(s, 2)] = t.reshape(4, 8, 8, 1664).astype(BF)
-            send, keep = away(s, block, half_)
-            pl.when(half_ == 0)(send.start)
-            pl.when(half_ == 1)(keep.start)
-            for k in range(4 if a == "d" else 2):
-                if first_load + k + 2 < len(loads):
-                    pl.when(s == (2 * k + 1 if a == "d" else 4 * k + 3))(right(first_load + k + 2).start)
+                for cp in outputs_done(p):
+                    cp.wait()
+            dh = dot(S["dh"][...], S["wd"][p], NT).astype(BF).astype(F32)
+            _, dgate, dup = silu_back(S["gate"][p], S["up"][p], dh)
+            S["res_u"][p] = dot(S["at"][...], dup).reshape(4, 4, 8, 8, 256).astype(BF)
+            S["res_g"][p] = dot(S["at"][...], dgate).reshape(4, 4, 8, 8, 256).astype(BF)
+            S["res_d"][p] = dot(S["ht"][p], S["dh"][...]).reshape(32, 8, 1024).astype(BF)
+            for cp in outputs(j, p):
+                cp.start()
             return 0
-        lax.fori_loop(0, 8, loop, 0)
-        for k in range(6):
-            out_waited.add((gi, *task_of(a, k)))
-        for k in (0, 1):
-            filled[a == "d", k] = gi, *task_of(a, 6 + k)
-        complete.add((l, a))
+        lax.fori_loop(first, first + n, task, 0)
+        first += n
+    for p in (1, 0):
+        for cp in outputs_done(p):
+            cp.wait()
+    exchange(0)
+    layers.add(0)
+    for a in "ugd":
         fetch_ahead(a)
-    for ev in steps[-1][1]:
+    for ev in steps[-1]:
         event(ev)
-    for gi, (l, a) in enumerate(GROUPS):
-        for k in range(8):
-            wait_out(gi, *task_of(a, k))
+    for i, off in jobs:
+        exchanged(i, off).wait_send()
+        wait_terms(i, off)
 
     total = jnp.zeros((8, 128), F32)
     for a in "ugd":
@@ -643,14 +765,15 @@
         make().wait_send()
 
 
-def reduce_scatter(acts, weights, m, v):
-    args = list(acts) + [w.reshape(2, 4, 4, -1, 8, w.shape[-1]) for w in weights] + [*m, *v]
+def reduce_scatter(grads, acts, weights, w_down, m, v):
+    args = [g.reshape(4, 4, -1, 8, g.shape[-1]) for g in grads] + list(acts)
+    args += [w.reshape(2, 4, 4, -1, 8, w.shape[-1]) for w in weights] + [w_down, *m, *v]
     sh = rs_scratch()
     any_ = pl.BlockSpec(memory_space=pl.ANY)
     outs = [jax.ShapeDtypeStruct(s, BF) for s in ((2, 8, 1664), (2, 8, 1664), (2, 2, 16, 512))] + [jax.ShapeDtypeStruct(t.shape, F32) for t in (*m, *v)]
-    outs += [jax.ShapeDtypeStruct((2, 4, 4, TILES[a], 8, WIDTH[a]), BF) for a in "ugd"]
+    outs += [jax.ShapeDtypeStruct(s, BF) for s in ((4, 4, 8, 8, 3328), (4, 4, 8, 8, 3328), (4, 104, 8, 1024))]
     outs = pl.pallas_call(
-        functools.partial(rs_kernel, list(sh)), out_shape=outs, in_specs=[any_] * 19, out_specs=[any_] * 12, scratch_shapes=list(sh.values()), name="reduce_scatter",
+        functools.partial(rs_kernel, list(sh)), out_shape=outs, in_specs=[any_] * 18, out_specs=[any_] * 12, scratch_shapes=list(sh.values()), name="reduce_scatter",
         compiler_params=pltpu.CompilerParams(collective_id=0, has_side_effects=True, vmem_limit_bytes=VMEM_BYTES))(*args)
     return outs[:3], outs[3:6], outs[6:9]
 
@@ -816,200 +939,16 @@
         compiler_params=pltpu.CompilerParams(collective_id=1, has_side_effects=True, vmem_limit_bytes=VMEM_BYTES))(u, g, d)
 
 
-T = 1024
-B = 256
-N = 3328 // B
-NT = (((1,), (1,)), ((), ()))
-
-
-def dot(a, b, dims=(((1,), (0,)), ((), ()))):
-    return lax.dot_general(a, b, dims, preferred_element_type=F32)
-
-
-def norm_scale(wide):
-    return lax.rsqrt(jnp.mean(wide**2, -1, keepdims=True) + 1e-6)
-
-
-def rowwise(n, body, step=128):
-    def one(i, _):
-        body(pl.ds(pl.multiple_of(i * step, step), step))
-        return 0
-    lax.fori_loop(0, n // step, one, 0)
-
-
-def silu_back(g, u, dh):
-    s = jax.nn.sigmoid(g)
-    silu = g * s
-    return silu, (dh * u * (s + silu * (1.0 - s))).astype(BF), (dh * silu).astype(BF)
-
-
-def norm_into(h, a):
-    def norm(rows):
-        wide = h[rows].astype(F32)
-        a[rows] = (wide * norm_scale(wide)).astype(BF)
-    rowwise(T, norm)
-
-
-def pipelined(chunk, first, second):
-    held = None
-    for m in range(0, T, chunk):
-        rows = slice(m, m + chunk)
-        now = first(rows)
-        if held is not None:
-            second(*held)
-        held = rows, now
-    second(*held)
-
-
-def fwd0(C, tr, x, wg, wu, wd, gate, up, ht, h1, at, a, hid):
-    j = pl.program_id(0)
-
-    @pl.when(j == 0)
-    def _():
-        norm_into(x, a)
-        at[...] = a[...].T if tr else a[...]
-
-    @pl.when(j < N)
-    def _():
-        def first(rows):
-            return dot(a[rows], wg[...]), dot(a[rows], wu[...])
-
-        def second(rows, gu):
-            g, u = gu
-            gate[rows] = g
-            up[rows] = u
-            v = (g * jax.nn.sigmoid(g) * u).astype(BF)
-            hid[j, rows] = v
-            if tr:
-                ht[:, rows] = v.T
-            else:
-                ht[rows] = v
-        pipelined(C, first, second)
-
-    @pl.when(j >= N)
-    def _():
-        def first(rows):
-            return sum(dot(hid[i, rows], wd[i * B:i * B + B]) for i in range(N))
-
-        def second(rows, y):
-            n = pl.ds(pl.multiple_of((j - N) * B, B), B)
-            h1[rows] = (x[rows, n].astype(F32) + y.astype(BF).astype(F32)).astype(BF)
-        pipelined(C, first, second)
-
-
-def layer0(x, w_gate, w_up, w_down, C=512, tr=True):
-    whole = pl.BlockSpec((T, T), lambda j: (0, 0))
-    cap = lambda j: jnp.minimum(j, N - 1)
-    cols = pl.BlockSpec((T, B), lambda j: (0, cap(j)))
-    wcols = pl.BlockSpec((None, T, B), lambda j: (0, 0, cap(j)))
-    late = lambda j: jnp.maximum(j - N, 0)
-    wrows = pl.BlockSpec((None, 3328, B), lambda j: (0, 0, late(j)))
-    rows = pl.BlockSpec((B, T), lambda j: (cap(j), 0)) if tr else cols
-    o = jax.ShapeDtypeStruct
-    blk = pl.BlockSpec((None, T, B), lambda j: (cap(j), 0, 0))
-    return pl.pallas_call(functools.partial(fwd0, C, tr), grid=(N + 4,), in_specs=[whole, wcols, wcols, wrows],
-        out_specs=[blk, blk, rows, pl.BlockSpec((T, B), lambda j: (0, late(j))), whole],
-        out_shape=[o((N, T, B), F32)] * 2 + [o((3328, T) if tr else (T, 3328), BF), o((T, T), BF), o((T, T), BF)],
-        scratch_shapes=[pltpu.VMEM((T, T), BF), pltpu.VMEM((N, T, B), BF)], name="layer0",
-        compiler_params=pltpu.CompilerParams(vmem_limit_bytes=VMEM_BYTES))(x, w_gate, w_up, w_down)
-
-
-def both1(C, tr, h, dy, wg, wu, wd, wg2, wu2, ht, dg, du, at, dh1, a, gs, us, acc):
-    j = pl.program_id(0)
-
-    @pl.when(j == 0)
-    def _():
-        norm_into(h, a)
-        at[...] = a[...].T if tr else a[...]
-
-    @pl.when(j < N)
-    def _():
-        def first(rows):
-            return dot(a[rows], wg[...]), dot(a[rows], wu[...]), dot(dy[rows], wd[...], NT)
-
-        def second(rows, parts):
-            g, u, dh = parts
-            silu, dgate, dup = silu_back(g, u, dh.astype(BF).astype(F32))
-            v = (silu * u).astype(BF)
-            if tr:
-                ht[:, rows] = v.T
-            else:
-                ht[rows] = v
-            dg[rows] = dgate
-            gs[j, rows] = dgate
-            du[rows] = dup
-            us[j, rows] = dup
-        pipelined(C, first, second)
-
-    @pl.when(j >= N)
-    def _():
-        def first(rows):
-            return sum(dot(gs[i, rows], wg2[:, i * B:i * B + B], NT) + dot(us[i, rows], wu2[:, i * B:i * B + B], NT) for i in range(N))
-
-        def second(rows, y):
-            n = pl.ds(pl.multiple_of((j - N) * B, B), B)
-            acc[rows, n] = y
-        pipelined(C, first, second)
-
-    @pl.when(j == N + 3)
-    def _():
-        def back(rows):
-            wide = h[rows].astype(F32)
-            scale = norm_scale(wide)
-            d = acc[rows].astype(BF).astype(F32)
-            d = d * scale - wide * (scale * scale * scale * jnp.mean(d * wide, -1, keepdims=True))
-            dh1[rows] = (dy[rows].astype(F32) + d.astype(BF).astype(F32)).astype(BF)
-        rowwise(T, back)
-
-
-def layer1(h, dy, w_gate, w_up, w_down, C=512, tr=True):
-    cap = lambda j: jnp.minimum(j, N - 1)
-    late = lambda j: jnp.maximum(j - N, 0)
-    whole = pl.BlockSpec((T, T), lambda j: (0, 0))
-    cols = pl.BlockSpec((T, B), lambda j: (0, cap(j)))
-    wcols = pl.BlockSpec((None, T, B), lambda j: (1, 0, cap(j)))
-    wrows = pl.BlockSpec((None, B, T), lambda j: (1, cap(j), 0))
-    wtall = pl.BlockSpec((None, B, 3328), lambda j: (1, late(j), 0))
-    rows = pl.BlockSpec((B, T), lambda j: (cap(j), 0)) if tr else cols
-    o = jax.ShapeDtypeStruct
-    blk = pl.BlockSpec((None, T, B), lambda j: (cap(j), 0, 0))
-    return pl.pallas_call(functools.partial(both1, C, tr), grid=(N + 4,), in_specs=[whole, whole, wcols, wcols, wrows, wtall, wtall], out_specs=[rows, cols, cols, whole, whole],
-        out_shape=[o((3328, T) if tr else (T, 3328), BF)] + [o((T, 3328), BF)] * 2 + [o((T, T), BF)] * 2,
-        scratch_shapes=[pltpu.VMEM((T, T), BF), pltpu.VMEM((N, T, B), BF), pltpu.VMEM((N, T, B), BF), pltpu.VMEM((T, T), F32)], name="layer1",
-        compiler_params=pltpu.CompilerParams(vmem_limit_bytes=VMEM_BYTES))(h, dy, w_gate, w_up, w_down, w_gate, w_up)
-
-
-def back0(C, dh1, gate, up, wd, dg, du):
-    def first(rows):
-        return dot(dh1[rows], wd[...], NT)
-
-    def second(rows, dh):
-        _, dg[rows], du[rows] = silu_back(gate[rows], up[rows], dh.astype(BF).astype(F32))
-    pipelined(C, first, second)
-
-
-def back(dh1, gate, up, w_down, C=512):
-    whole = pl.BlockSpec((T, T), lambda j: (0, 0))
-    blk = pl.BlockSpec((None, T, B), lambda j: (j, 0, 0))
-    cols = pl.BlockSpec((T, B), lambda j: (0, j))
-    wrows = pl.BlockSpec((None, B, T), lambda j: (0, j, 0))
-    o = jax.ShapeDtypeStruct
-    return pl.pallas_call(functools.partial(back0, C), grid=(N,), in_specs=[whole, blk, blk, wrows], out_specs=[cols, cols],
-        out_shape=[o((T, 3328), BF)] * 2, name="back0",
-        compiler_params=pltpu.CompilerParams(vmem_limit_bytes=VMEM_BYTES))(dh1, gate, up, w_down)
-
-
 def solution(mesh):
     def step(x, dy, w_gate, w_up, w_down, *moments):
         x, dy = x[0], dy[0]
         gate0, up0, hid0, h1, a0 = layer0(x, w_gate, w_up, w_down)
-        hid1, dgate1, dup1, a1, dh1 = layer1(h1, dy, w_gate, w_up, w_down)
-        dgate0, dup0 = back(dh1, gate0, up0, w_down)
+        down1, gate1, up1, dh1 = layer1(h1, dy, w_gate, w_up, w_down)
         m, v = moments[:3], moments[3:]
         order = lambda t: (t[1], t[0], t[2])
         pad = lambda t: (*t[:2], jnp.pad(t[2], ((0, 0), (0, 3), (0, 0))))
-        acts = (a0, a1, hid0, hid1, dup0, dup1, dgate0, dgate1, dh1, dy)
-        new, m, v = reduce_scatter(acts, order((w_gate, w_up, w_down)), pad(order(m)), pad(order(v)))
+        acts = (dh1, a0, gate0, up0, hid0)
+        new, m, v = reduce_scatter((up1, gate1, down1), acts, order((w_gate, w_up, w_down)), w_down, pad(order(m)), pad(order(v)))
         u, g, d = all_gather(*new)
         w = (g.reshape(w_gate.shape), u.reshape(w_up.shape), d.reshape(w_down.shape))
         cut = lambda t: (t[1], t[0], t[2][:, :13])

time: 423 us -> 402 us (0.950)
  Pallas kernels: 385 us -> 364 us
    pallas_call x1, Pallas kernels: 175 us -> 147 us  [reduce_scatter(): pl.pallas_call(functools.partial(rs_kernel, list(sh)), out_shape=outs, in...]
    pallas_call x2 -> x1, Pallas kernels: 77.4 us -> 84.6 us  [layer1(): pl.pallas_call(functools.partial(both1, C), grid=(N + 4,), in_specs=[whol...]
where the time goes in v3:
time: 402 us; the launch traced here: 401 us
  Pallas kernels  364 us (91%)
  local copies, waits for them, and re-layouts  36.3 us (9%)
    pallas_call x1, Pallas kernels, reduce_scatter(): pl.pallas_call(functools.partial(rs_kernel, list(sh)), out_shape=outs, in...  147 us
    pallas_call x1, Pallas kernels, all_gather(): pl.pallas_call(functools.partial(ag_kernel, list(sh)), out_shape=outs, in...  95.8 us
    pallas_call x1, Pallas kernels, layer1(): pl.pallas_call(functools.partial(both1, C), grid=(N + 4,), in_specs=[whol...  84.6 us
    pallas_call x1, Pallas kernels, layer0(): pl.pallas_call(functools.partial(fwd0, C, tr), grid=(N + 4,), in_specs=[w...  36.5 us
    unnamed x29, local copies, waits for them, and re-layouts  34.9 us

profile of v3, /device:TPU:1, one launch (start us, length us, event | category | flops | bytes accessed | tf_op | source)
XLA Modules:
  0.0 400.9 jit_solution(6425157389752089921)
XLA Ops:
  0.6 0.9 copy.20
  1.6 0.7 pad.7.refs_14_
  2.3 0.9 copy.21
  3.2 0.7 pad.8.refs_17_
  3.9 36.5 %layer0.1 = (f32[13,1024,256]{2,1,0:T(8,128)}, f32[13,1024,256]{2,1,0:T(8,128)}, bf16[3328,1024]{1,0:T(8,128)(2,1)}, bf16[1024,1024]{1,0:T(8,128)(2,1)}, bf16[1024,1024]{1,0:T(8,128)(2,1)}) custom-call(bf16[1024,1024]{1,0:T(8,128)(2,1)} %bitcast.25, bf16[2,1024,3328]{2,1,0:T(8,128)(2,1)} %wg2.1, bf16[2,1024,3328]{2,1,0:T(8,128)(2,1)} %wu2.1, ...), custom_call_target="tpu_custom_call" | custom-call | tf_op jit(solution)/shard_map/layer0/pallas_call | solution.py:154
  40.4 84.6 %layer1.1 = (bf16[3328,1024]{1,0:T(8,128)(2,1)}, bf16[1024,3328]{1,0:T(8,128)(2,1)}, bf16[1024,3328]{1,0:T(8,128)(2,1)}, bf16[1024,1024]{1,0:T(8,128)(2,1)}) custom-call(bf16[1024,1024]{1,0:T(8,128)(2,1)} %get-tuple-element.30.h, bf16[1024,1024]{1,0:T(8,128)(2,1)} %bitcast.24, bf16[2,1024,3328]{2,1,0:T(8,128)(2,1)} %wg2.1, bf16[2,1024,3328]{2,1,0:T(8,128)(2,1)} %wu2.1, ...), custom_call_target="tpu_custom_call" | custom-call | tf_op jit(solution)/shard_map/layer1/pallas_call | solution.py:207
  125.0 147.0 %reduce_scatter.1 = (bf16[2,8,1664]{2,1,0:T(8,128)(2,1)}, bf16[2,8,1664]{2,1,0:T(8,128)(2,1)}, bf16[2,2,16,512]{3,2,1,0:T(8,128)(2,1)}, f32[2,4,3328]{2,1,0:T(4,...) custom-call(bf16[4,4,8,8,3328]{4,3,2,1,0:T(8,128)(2,1)} %bitcast.23,, ...), custom_call_target="tpu_custom_call" | custom-call | tf_op jit(solution)/shard_map/reduce_scatter/pallas_call | solution.py:775
  272.0 1.6 copy.22
  273.7 1.6 copy.23
  275.3 95.8 %all_gather.1 = (bf16[2,4,4,8,8,3328]{5,4,3,2,1,0:T(8,128)(2,1)}, bf16[2,4,4,8,8,3328]{5,4,3,2,1,0:T(8,128)(2,1)}, bf16[2,4,4,26,8,1024]{5,4,3,2,1,0:T(8,128)(2,1)}) custom-call(bf16[2,8,1664]{2,1,0:T(8,128)(2,1)} %get-tuple-element.39.refs_0_, bf16[2,8,1664]{2,1,0:T(8,128)(2,1)} %get-tuple-element.40.refs_1_, bf16[2,2,16,512]{3,2,1,0:T(8,128)(2,1)} %get-tuple-element.41.refs_2_), custom_call_target="tpu_custom_call" | custom-call | tf_op jit(solution)/shard_map/all_gather/pallas_call | solution.py:937
  371.1 0.0 copy-start
  371.2 0.0 slice-start
  371.2 0.0 slice-start.1
  371.2 15.1 %copy.31 = bf16[2,1024,3328]{2,1,0:T(8,128)(2,1)} copy(bf16[2,1024,3328]{2,1,0:T(8,128)(2,1)} %bitcast.20) | data formatting | bytes 27262976
  386.2 0.0 copy-done
  386.2 0.0 slice-start.2
  386.2 0.0 slice-start.3
  386.2 6.5 %copy.32 = bf16[2,1024,3328]{2,1,0:T(8,128)(2,1)} copy(bf16[2,1024,3328]{2,1,0:T(8,128)(2,1)S(1)} %bitcast.19) | data formatting | bytes 27262976
  392.8 0.0 slice-done
  392.8 0.0 slice-done.1
  392.8 0.0 slice-done.2
  392.8 0.4 slice-done.3
  393.2 0.0 copy-start.4
  393.2 5.1 %copy.33 = bf16[2,3328,1024]{2,1,0:T(8,128)(2,1)} copy(bf16[2,3328,1024]{2,1,0:T(8,128)(2,1)S(1)} %bitcast.18) | data formatting | bytes 27262976
  398.4 0.0 copy-done.4
  398.4 0.6 copy.34
  399.0 0.0 copy-done.3
  399.0 0.6 copy.35
  399.7 0.0 copy-done.2
  399.7 0.6 copy.36
  400.3 0.0 copy-done.1
  400.3 0.6 copy.37
  (4 shorter events, 0.0 us)
Async XLA Ops:
  371.1 15.1 %copy-start = (bf16[2,4,4,8,8,3328]{5,4,3,2,1,0:T(8,128)(2,1)S(1)}, bf16[2,4,4,8,8,3328]{5,4,3,2,1,0:T(8,128)(2,1)}, u32[]{:S(2)}) copy-start(bf16[2,4,4,8,8,3328]{5,4,3,2,1,0:T(8,128)(2,1)} %get-tuple-element.43) | copy-start | bytes 40894468
  371.2 21.6 %slice-start = ((s8[13631488]{0:T(1024)(128)(4,1)}), s8[4194304]{0:T(1024)(128)(4,1)S(1)}, s32[]{:S(2)}) async-start(s8[13631488]{0:T(1024)(128)(4,1)} %bitcast.16), calls=%async_computation | async-start | bytes 8388608
  371.2 21.6 %slice-start.1 = ((s8[13631488]{0:T(1024)(128)(4,1)}), s8[4194304]{0:T(1024)(128)(4,1)S(1)}, s32[]{:S(2)}) async-start(s8[13631488]{0:T(1024)(128)(4,1)} %bitcast.16), calls=%async_computation.1 | async-start | bytes 8388608
  386.2 6.6 %slice-start.2 = ((s8[13631488]{0:T(1024)(128)(4,1)}), s8[4194304]{0:T(1024)(128)(4,1)S(1)}, s32[]{:S(2)}) async-start(s8[13631488]{0:T(1024)(128)(4,1)} %bitcast.16), calls=%async_computation.2 | async-start | bytes 8388608
  386.2 7.0 %slice-start.3 = ((s8[13631488]{0:T(1024)(128)(4,1)}), s8[1048576]{0:T(1024)(128)(4,1)S(1)}, s32[]{:S(2)}) async-start(s8[13631488]{0:T(1024)(128)(4,1)} %bitcast.16), calls=%async_computation.3 | async-start | bytes 2097152
  393.2 5.1 %copy-start.4 = (f32[2,4,3328]{2,1,0:T(4,128)S(1)}, f32[2,4,3328]{2,1,0:T(4,128)}, u32[]{:S(2)}) copy-start(f32[2,4,3328]{2,1,0:T(4,128)} %get-tuple-element.72) | copy-start | bytes 319492
  393.2 5.8 %copy-start.3 = (f32[2,4,3328]{2,1,0:T(4,128)S(1)}, f32[2,4,3328]{2,1,0:T(4,128)}, u32[]{:S(2)}) copy-start(f32[2,4,3328]{2,1,0:T(4,128)} %get-tuple-element.73) | copy-start | bytes 319492
  393.2 6.4 %copy-start.2 = (f32[2,4,3328]{2,1,0:T(4,128)S(1)}, f32[2,4,3328]{2,1,0:T(4,128)}, u32[]{:S(2)}) copy-start(f32[2,4,3328]{2,1,0:T(4,128)} %get-tuple-element.75) | copy-start | bytes 319492
  393.2 7.1 %copy-start.1 = (f32[2,4,3328]{2,1,0:T(4,128)S(1)}, f32[2,4,3328]{2,1,0:T(4,128)}, u32[]{:S(2)}) copy-start(f32[2,4,3328]{2,1,0:T(4,128)} %get-tuple-element.76) | copy-start | bytes 319492

commit v4 on v3

--- a/solution.py
+++ b/solution.py
@@ -12,6 +12,7 @@
 BF, F32 = jnp.bfloat16, jnp.float32
 SIZE = {"x": 4, "y": 4, "z": 8}
 VMEM_BYTES = 67043328
+AG_VMEM = 4 * 2**20
 ALL = slice(None)
 
 
@@ -158,7 +159,7 @@
         compiler_params=pltpu.CompilerParams(vmem_limit_bytes=VMEM_BYTES))(x, w_gate, w_up, w_down)
 
 
-def both1(C, h, dy, wg, wu, wd, wg2, wu2, dwd, dwg, dwu, dh1, a, at, gs, us, acc):
+def both1(h, dy, wg, wu, wd, wg2, wu2, dwd, dwg, dwu, dh1, a, at, gs, us, hta, htb, acc):
     j = pl.program_id(0)
 
     @pl.when(j == 0)
@@ -166,17 +167,34 @@
         norm_into(h, a)
         at[...] = a[...].T
 
-    @pl.when(j < N)
-    def _():
-        g, u = dot(a[...], wg[...]), dot(a[...], wu[...])
-        dh = dot(dy[...], wd[...], NT).astype(BF).astype(F32)
-        silu, dgate, dup = silu_back(g, u, dh)
+    def now():
+        return dot(a[...], wg[...]), dot(a[...], wu[...]), dot(dy[...], wd[...], NT)
+
+    def before(ht):
+        dwd[...] = dot(ht[...], dy[...]).astype(BF)
+        dwg[...] = dot(at[...], gs[j - 1]).astype(BF)
+        dwu[...] = dot(at[...], us[j - 1]).astype(BF)
+
+    def then(g, u, dh, ht):
+        silu, dgate, dup = silu_back(g, u, dh.astype(BF).astype(F32))
         gs[j] = dgate
         us[j] = dup
-        hid = (silu * u).astype(BF)
-        dwg[...] = dot(at[...], dgate).astype(BF)
-        dwu[...] = dot(at[...], dup).astype(BF)
-        dwd[...] = dot(hid.T, dy[...]).astype(BF)
+        ht[...] = (silu * u).astype(BF).T
+
+    @pl.when(j == 0)
+    def _():
+        then(*now(), hta)
+
+    for p, (mine, last) in enumerate(((hta, htb), (htb, hta))):
+        @pl.when((j > 0) & (j < N) & (lax.rem(j, 2) == p))
+        def _():
+            x = now()
+            before(last)
+            then(*x, mine)
+
+    @pl.when(j == N)
+    def _():
+        before(hta)
 
     @pl.when(j >= N)
     def _():
@@ -194,19 +212,20 @@
         rowwise(T, back)
 
 
-def layer1(h, dy, w_gate, w_up, w_down, C=512):
+def layer1(h, dy, w_gate, w_up, w_down):
     cap = lambda j: jnp.minimum(j, N - 1)
+    prev = lambda j: jnp.clip(j - 1, 0, N - 1)
     late = lambda j: jnp.maximum(j - N, 0)
     whole = pl.BlockSpec((T, T), lambda j: (0, 0))
-    cols = pl.BlockSpec((T, B), lambda j: (0, cap(j)))
+    cols = pl.BlockSpec((T, B), lambda j: (0, prev(j)))
     wcols = pl.BlockSpec((None, T, B), lambda j: (1, 0, cap(j)))
     wrows = pl.BlockSpec((None, B, T), lambda j: (1, cap(j), 0))
     wtall = pl.BlockSpec((None, B, 3328), lambda j: (1, late(j), 0))
-    rows = pl.BlockSpec((B, T), lambda j: (cap(j), 0))
+    rows = pl.BlockSpec((B, T), lambda j: (prev(j), 0))
     o = jax.ShapeDtypeStruct
-    return pl.pallas_call(functools.partial(both1, C), grid=(N + 4,), in_specs=[whole, whole, wcols, wcols, wrows, wtall, wtall], out_specs=[rows, cols, cols, whole],
+    return pl.pallas_call(both1, grid=(N + 4,), in_specs=[whole, whole, wcols, wcols, wrows, wtall, wtall], out_specs=[rows, cols, cols, whole],
         out_shape=[o((3328, T), BF)] + [o((T, 3328), BF)] * 2 + [o((T, T), BF)],
-        scratch_shapes=[pltpu.VMEM((T, T), BF)] * 2 + [pltpu.VMEM((N, T, B), BF)] * 2 + [pltpu.VMEM((T, T), F32)], name="layer1",
+        scratch_shapes=[pltpu.VMEM((T, T), BF)] * 2 + [pltpu.VMEM((N, T, B), BF)] * 2 + [pltpu.VMEM((B, T), BF)] * 2 + [pltpu.VMEM((T, T), F32)], name="layer1",
         compiler_params=pltpu.CompilerParams(vmem_limit_bytes=VMEM_BYTES))(h, dy, w_gate, w_up, w_down, w_gate, w_up)
 
 
@@ -225,7 +244,7 @@
 
 
 def plan():
-    RATE, LAT, TASK, DRATE, DLAT = 46.0e3, 2.6, 3.3, 500.0e3, 2.0
+    RATE, LAT, TASK, DRATE, DLAT = 46.0e3, 3.0, 2.7, 600.0e3, 2.0
     free, heap, seq = {}, [], [0]
 
     def send(t, link, nbytes):
@@ -295,7 +314,7 @@
     return steps, now, free
 
 
-FIRST = 6.5
+FIRST = 3.0
 
 
 def addsum(dst, srcs):
@@ -659,11 +678,11 @@
             def _():
                 for cp in outputs_done(p):
                     cp.wait()
-            dh = dot(S["dh"][...], S["wd"][p], NT).astype(BF).astype(F32)
-            _, dgate, dup = silu_back(S["gate"][p], S["up"][p], dh)
+            dh = dot(S["dh"][...], S["wd"][p], NT)
+            S["res_d"][p] = dot(S["ht"][p], S["dh"][...]).reshape(32, 8, 1024).astype(BF)
+            _, dgate, dup = silu_back(S["gate"][p], S["up"][p], dh.astype(BF).astype(F32))
             S["res_u"][p] = dot(S["at"][...], dup).reshape(4, 4, 8, 8, 256).astype(BF)
             S["res_g"][p] = dot(S["at"][...], dgate).reshape(4, 4, 8, 8, 256).astype(BF)
-            S["res_d"][p] = dot(S["ht"][p], S["dh"][...]).reshape(32, 8, 1024).astype(BF)
             for cp in outputs(j, p):
                 cp.start()
             return 0
@@ -936,7 +955,7 @@
     outs = [jax.ShapeDtypeStruct((2, 4, 4, TILES[a], 8, 2 * WIDTH[a]), BF) for a in "ugd"]
     return pl.pallas_call(
         functools.partial(ag_kernel, list(sh)), out_shape=outs, in_specs=[any_] * 3, out_specs=[any_] * 3, scratch_shapes=list(sh.values()), name="all_gather",
-        compiler_params=pltpu.CompilerParams(collective_id=1, has_side_effects=True, vmem_limit_bytes=VMEM_BYTES))(u, g, d)
+        compiler_params=pltpu.CompilerParams(collective_id=1, has_side_effects=True, vmem_limit_bytes=AG_VMEM))(u, g, d)
 
 
 def solution(mesh):

time: 402 us -> 366 us (0.910)
  Pallas kernels: 364 us -> 337 us
  local copies, waits for them, and re-layouts: 36.3 us -> 26.9 us
    pallas_call x1, Pallas kernels: 147 us -> 134 us  [reduce_scatter(): pl.pallas_call(functools.partial(rs_kernel, list(sh)), out_shape=outs, in...]
    pallas_call x1, Pallas kernels: 84.6 us -> 72.8 us  [layer1(): pl.pallas_call(both1, grid=(N + 4,), in_specs=[whole, whole, wcols, wcols...]
    unnamed x29 -> x25, local copies, waits for them, and re-layouts: 34.9 us -> 25.5 us
where the time goes in v4:
time: 366 us; the launch traced here: 364 us
  Pallas kernels  337 us (92%)
  local copies, waits for them, and re-layouts  26.9 us (7%)
    pallas_call x1, Pallas kernels, reduce_scatter(): pl.pallas_call(functools.partial(rs_kernel, list(sh)), out_shape=outs, in...  134 us
    pallas_call x1, Pallas kernels, all_gather(): pl.pallas_call(functools.partial(ag_kernel, list(sh)), out_shape=outs, in...  93.3 us
    pallas_call x1, Pallas kernels, layer1(): pl.pallas_call(both1, grid=(N + 4,), in_specs=[whole, whole, wcols, wcols...  72.8 us
    pallas_call x1, Pallas kernels, layer0(): pl.pallas_call(functools.partial(fwd0, C, tr), grid=(N + 4,), in_specs=[w...  36.5 us
    unnamed x25, local copies, waits for them, and re-layouts  25.5 us

profile of v4, /device:TPU:1, one launch (start us, length us, event | category | flops | bytes accessed | tf_op | source)
XLA Modules:
  0.0 364.3 jit_solution(15718384208835264292)
XLA Ops:
  0.6 0.9 copy.20
  1.6 0.7 pad.7.refs_14_
  2.2 0.9 copy.21
  3.2 0.7 pad.8.refs_17_
  3.8 36.5 %layer0.1 = (f32[13,1024,256]{2,1,0:T(8,128)}, f32[13,1024,256]{2,1,0:T(8,128)}, bf16[3328,1024]{1,0:T(8,128)(2,1)}, bf16[1024,1024]{1,0:T(8,128)(2,1)}, bf16[1024,1024]{1,0:T(8,128)(2,1)}) custom-call(bf16[1024,1024]{1,0:T(8,128)(2,1)} %bitcast.23, bf16[2,1024,3328]{2,1,0:T(8,128)(2,1)} %wg2.1, bf16[2,1024,3328]{2,1,0:T(8,128)(2,1)} %wu2.1, ...), custom_call_target="tpu_custom_call" | custom-call | tf_op jit(solution)/shard_map/layer0/pallas_call | solution.py:155
  40.4 72.8 %layer1.1 = (bf16[3328,1024]{1,0:T(8,128)(2,1)}, bf16[1024,3328]{1,0:T(8,128)(2,1)}, bf16[1024,3328]{1,0:T(8,128)(2,1)}, bf16[1024,1024]{1,0:T(8,128)(2,1)}) custom-call(bf16[1024,1024]{1,0:T(8,128)(2,1)} %get-tuple-element.30.h, bf16[1024,1024]{1,0:T(8,128)(2,1)} %bitcast.22, bf16[2,1024,3328]{2,1,0:T(8,128)(2,1)} %wg2.1, bf16[2,1024,3328]{2,1,0:T(8,128)(2,1)} %wu2.1, ...), custom_call_target="tpu_custom_call" | custom-call | tf_op jit(solution)/shard_map/layer1/pallas_call | solution.py:226
  113.2 134.1 %reduce_scatter.1 = (bf16[2,8,1664]{2,1,0:T(8,128)(2,1)}, bf16[2,8,1664]{2,1,0:T(8,128)(2,1)}, bf16[2,2,16,512]{3,2,1,0:T(8,128)(2,1)}, f32[2,4,3328]{2,1,0:T(4,...) custom-call(bf16[4,4,8,8,3328]{4,3,2,1,0:T(8,128)(2,1)} %bitcast.21,, ...), custom_call_target="tpu_custom_call" | custom-call | tf_op jit(solution)/shard_map/reduce_scatter/pallas_call | solution.py:794
  247.3 1.6 copy.22
  248.9 1.6 copy.23
  250.6 0.0 copy-start
  250.6 0.8 copy-done
  251.4 0.0 copy-start.1
  251.4 0.8 copy-done.1
  252.2 0.0 copy-start.2
  252.2 0.8 copy-done.2
  253.0 93.3 %all_gather.1 = (bf16[2,4,4,8,8,3328]{5,4,3,2,1,0:T(8,128)(2,1)S(1)}, bf16[2,4,4,8,8,3328]{5,4,3,2,1,0:T(8,128)(2,1)S(1)}, bf16[2,4,4,26,8,1024]{5,4,3,2,1,0:T(8,128)(2,1)S(1)}) custom-call(bf16[2,8,1664]{2,1,0:T(8,128)(2,1)S(1)} %copy-done.1, bf16[2,8,1664]{2,1,0:T(8,128)(2,1)S(1)} %copy-done.2, bf16[2,2,16,512]{3,2,1,0:T(8,128)(2,1)S(1)} %copy-done), custom_call_target="tpu_custom_call" | custom-call | tf_op jit(solution)/shard_map/all_gather/pallas_call | solution.py:956
  346.3 5.1 %copy.31 = bf16[2,1024,3328]{2,1,0:T(8,128)(2,1)} copy(bf16[2,1024,3328]{2,1,0:T(8,128)(2,1)S(1)} %bitcast.15) | data formatting | bytes 27262976
  351.4 5.1 %copy.32 = bf16[2,1024,3328]{2,1,0:T(8,128)(2,1)} copy(bf16[2,1024,3328]{2,1,0:T(8,128)(2,1)S(1)} %bitcast.14) | data formatting | bytes 27262976
  356.6 0.0 copy-start.6
  356.6 0.0 copy-start.5
  356.6 0.0 copy-start.4
  356.6 0.0 copy-start.3
  356.6 5.1 %copy.33 = bf16[2,3328,1024]{2,1,0:T(8,128)(2,1)} copy(bf16[2,3328,1024]{2,1,0:T(8,128)(2,1)S(1)} %bitcast.13) | data formatting | bytes 27262976
  361.7 0.0 copy-done.6
  361.7 0.6 copy.34
  362.4 0.0 copy-done.5
  362.4 0.6 copy.35
  363.0 0.0 copy-done.4
  363.0 0.6 copy.36
  363.6 0.0 copy-done.3
  363.6 0.6 copy.37
Async XLA Ops:
  250.6 0.8 copy-start
  251.4 0.8 copy-start.1
  252.2 0.8 copy-start.2
  356.6 5.1 %copy-start.6 = (f32[2,4,3328]{2,1,0:T(4,128)S(1)}, f32[2,4,3328]{2,1,0:T(4,128)}, u32[]{:S(2)}) copy-start(f32[2,4,3328]{2,1,0:T(4,128)} %get-tuple-element.72) | copy-start | bytes 319492
  356.6 5.8 %copy-start.5 = (f32[2,4,3328]{2,1,0:T(4,128)S(1)}, f32[2,4,3328]{2,1,0:T(4,128)}, u32[]{:S(2)}) copy-start(f32[2,4,3328]{2,1,0:T(4,128)} %get-tuple-element.73) | copy-start | bytes 319492
  356.6 6.4 %copy-start.4 = (f32[2,4,3328]{2,1,0:T(4,128)S(1)}, f32[2,4,3328]{2,1,0:T(4,128)}, u32[]{:S(2)}) copy-start(f32[2,4,3328]{2,1,0:T(4,128)} %get-tuple-element.75) | copy-start | bytes 319492
  356.6 7.1 %copy-start.3 = (f32[2,4,3328]{2,1,0:T(4,128)S(1)}, f32[2,4,3328]{2,1,0:T(4,128)}, u32[]{:S(2)}) copy-start(f32[2,4,3328]{2,1,0:T(4,128)} %get-tuple-element.76) | copy-start | bytes 319492

commit v5 on v4

--- a/solution.py
+++ b/solution.py
@@ -39,7 +39,7 @@
 WIDTH = {"u": 1664, "g": 1664, "d": 512}
 TALL = {"u": 1, "g": 1, "d": 4}
 LASTDIM = {"u": "y", "g": "z", "d": "z"}
-ROWS = {"u": 4, "g": 4, "d": 16}
+MOMENTS = {"u": (2, 4), "g": (2, 4), "d": (13, 2)}
 COUNT = 2 * 3 * 1024 * 3328
 NB = 2
 
@@ -229,7 +229,7 @@
         compiler_params=pltpu.CompilerParams(vmem_limit_bytes=VMEM_BYTES))(h, dy, w_gate, w_up, w_down, w_gate, w_up)
 
 
-TASKS = (3, 3, 3, 4)
+TASKS = (2, 3, 4, 4)
 
 
 def jobs_of(layer):
@@ -314,7 +314,7 @@
     return steps, now, free
 
 
-FIRST = 3.0
+FIRST = 1.0
 
 
 def addsum(dst, srcs):
@@ -342,7 +342,7 @@
         sh["stage_" + a] = pltpu.VMEM((NB, 4, DEPTH[a], 8, max(u[3] for u in UNITS if u[1] == a)), BF)
         sh["stsem_" + a] = sem((NB,))
         sh["red_" + a] = pltpu.VMEM((2, TALL[a], 8, WIDTH[a]), BF)
-        sh["mv_" + a] = pltpu.VMEM((2, 2, 2, ROWS[a], WIDTH[a]), F32)
+        sh["mv_" + a] = pltpu.VMEM((2, 2, *MOMENTS[a], WIDTH[a]), F32)
         sh["w_" + a] = pltpu.VMEM((2, TALL[a], 8, WIDTH[a]), BF)
         h = SIZE[LASTDIM[a]] // 2
         for l in (0, 1):
@@ -351,6 +351,7 @@
             for n in "rs":
                 sh["%s2_%d%s" % (n, l, a)] = sem((2, h))
     sh["new_d"] = pltpu.VMEM((2, 2, 16, 512), BF)
+    sh["wide_d"] = pltpu.VMEM((2, 2, 16, 512), F32)
     for i, u in enumerate(UNITS):
         h = SIZE[u[4][0]] // 2
         sh["slot0_%d" % i] = pltpu.VMEM((2, h) + block_shape(i, 0), BF)
@@ -756,14 +757,16 @@
     column = lax.broadcasted_iota(jnp.int32, (32, 32), 1)
     pick = (column == 2 * zz + 13 * (row >> 4) + (row & 15)) & ((row & 15) < 13)
     pick = jnp.where(pick, 1.0, 0.0).astype(BF)
+    S["wide_d"][...] = jnp.zeros((2, 2, 16, 512), F32)
     for l in (0, 1):
         gd, wd = (jnp.dot(pick, S[n][l].reshape(32, 512), preferred_element_type=F32) for n in ("red_d", "w_d"))
         for s in (0, 1):
-            rows = slice(16 * s, 16 * s + 16)
-            n, m, v = adamw(wd[rows], S["mv_d"][0, s, l], S["mv_d"][1, s, l], gd[rows])
-            S["new_d"][l, s] = n
-            S["mv_d"][0, s, l] = m
-            S["mv_d"][1, s, l] = v
+            rows = slice(16 * s, 16 * s + 13)
+            n, m, v = adamw(wd[rows], S["mv_d"][0, s, :, l], S["mv_d"][1, s, :, l], gd[rows])
+            S["wide_d"][l, s, 0:13] = n.astype(F32)
+            S["new_d"][l, s] = S["wide_d"][l, s].astype(BF)
+            S["mv_d"][0, s, :, l] = m
+            S["mv_d"][1, s, :, l] = v
     ends = []
     for j, a in enumerate("ugd"):
         cp = pltpu.make_async_copy(S["new_d"] if a == "d" else S["w_" + a].at[:, 0], new[a], S["newsem"].at[j])
@@ -954,8 +957,24 @@
     any_ = pl.BlockSpec(memory_space=pl.ANY)
     outs = [jax.ShapeDtypeStruct((2, 4, 4, TILES[a], 8, 2 * WIDTH[a]), BF) for a in "ugd"]
     return pl.pallas_call(
-        functools.partial(ag_kernel, list(sh)), out_shape=outs, in_specs=[any_] * 3, out_specs=[any_] * 3, scratch_shapes=list(sh.values()), name="all_gather",
+        functools.partial(ag_kernel, list(sh)), out_shape=outs, in_specs=[pl.BlockSpec(memory_space=pltpu.HBM)] * 3, out_specs=[any_] * 3, scratch_shapes=list(sh.values()), name="all_gather",
         compiler_params=pltpu.CompilerParams(collective_id=1, has_side_effects=True, vmem_limit_bytes=AG_VMEM))(u, g, d)
+
+
+def settle_kernel(*refs):
+    ins, outs, sem = refs[:3], refs[3:6], refs[6]
+    copies = [pltpu.make_async_copy(ins[n].at[l, x], outs[n].at[l, x], sem.at[n, l, x]) for l in (0, 1) for x in range(4) for n in range(3)]
+    for cp in copies:
+        cp.start()
+    for cp in copies:
+        cp.wait()
+
+
+def settle(*gathered):
+    any_ = pl.BlockSpec(memory_space=pl.ANY)
+    return pl.pallas_call(
+        settle_kernel, out_shape=[jax.ShapeDtypeStruct(t.shape, t.dtype) for t in gathered], in_specs=[any_] * 3, out_specs=[pl.BlockSpec(memory_space=pltpu.HBM)] * 3,
+        scratch_shapes=[pltpu.SemaphoreType.DMA((3, 2, 4))], name="settle", compiler_params=pltpu.CompilerParams(vmem_limit_bytes=2**20))(*gathered)
 
 
 def solution(mesh):
@@ -965,13 +984,12 @@
         down1, gate1, up1, dh1 = layer1(h1, dy, w_gate, w_up, w_down)
         m, v = moments[:3], moments[3:]
         order = lambda t: (t[1], t[0], t[2])
-        pad = lambda t: (*t[:2], jnp.pad(t[2], ((0, 0), (0, 3), (0, 0))))
+        turned = lambda t: (*t[:2], t[2].transpose(1, 0, 2))
         acts = (dh1, a0, gate0, up0, hid0)
-        new, m, v = reduce_scatter((up1, gate1, down1), acts, order((w_gate, w_up, w_down)), w_down, pad(order(m)), pad(order(v)))
-        u, g, d = all_gather(*new)
+        new, m, v = reduce_scatter((up1, gate1, down1), acts, order((w_gate, w_up, w_down)), w_down, turned(order(m)), turned(order(v)))
+        u, g, d = settle(*all_gather(*new))
         w = (g.reshape(w_gate.shape), u.reshape(w_up.shape), d.reshape(w_down.shape))
-        cut = lambda t: (t[1], t[0], t[2][:, :13])
-        return (*w, *cut(m), *cut(v))
+        return (*w, *order(turned(m)), *order(turned(v)))
 
     data, whole, rows = P(("rep", "dp"), None, None), P(), P(None, "dp", None)
     out = P("rep", None, None)

time: 366 us -> 356 us (0.973)
  local copies, waits for them, and re-layouts: 26.9 us -> 6.34 us
  Pallas kernels: 337 us -> 348 us
    unnamed x25 -> x24, local copies, waits for them, and re-layouts: 25.5 us -> 6.34 us
    pallas_call x0 -> x1, Pallas kernels: none -> 13.3 us  [settle(): pl.pallas_call(settle_kernel, out_shape=[jax.ShapeDtypeStruct(t.shape, t....]
where the time goes in v5:
time: 356 us; the launch traced here: 355 us
  Pallas kernels  348 us (98%)
  local copies, waits for them, and re-layouts  6.34 us (2%)
    pallas_call x1, Pallas kernels, reduce_scatter(): pl.pallas_call(functools.partial(rs_kernel, list(sh)), out_shape=outs, in...  133 us
    pallas_call x1, Pallas kernels, all_gather(): pl.pallas_call(functools.partial(ag_kernel, list(sh)), out_shape=outs, in...  92.4 us
    pallas_call x1, Pallas kernels, layer1(): pl.pallas_call(both1, grid=(N + 4,), in_specs=[whole, whole, wcols, wcols...  72.9 us
    pallas_call x1, Pallas kernels, layer0(): pl.pallas_call(functools.partial(fwd0, C, tr), grid=(N + 4,), in_specs=[w...  36.5 us
    pallas_call x1, Pallas kernels, settle(): pl.pallas_call(settle_kernel, out_shape=[jax.ShapeDtypeStruct(t.shape, t....  13.3 us

profile of v5, /device:TPU:1, one launch (start us, length us, event | category | flops | bytes accessed | tf_op | source)
XLA Modules:
  0.0 355.1 jit_solution(629152523785322329)
XLA Ops:
  0.6 36.5 %layer0.1 = (f32[13,1024,256]{2,1,0:T(8,128)}, f32[13,1024,256]{2,1,0:T(8,128)}, bf16[3328,1024]{1,0:T(8,128)(2,1)}, bf16[1024,1024]{1,0:T(8,128)(2,1)}, bf16[1024,1024]{1,0:T(8,128)(2,1)}) custom-call(bf16[1024,1024]{1,0:T(8,128)(2,1)} %bitcast.22, bf16[2,1024,3328]{2,1,0:T(8,128)(2,1)} %wg2.1, bf16[2,1024,3328]{2,1,0:T(8,128)(2,1)} %wu2.1, ...), custom_call_target="tpu_custom_call" | custom-call | tf_op jit(solution)/shard_map/layer0/pallas_call | solution.py:155
  37.2 72.9 %layer1.1 = (bf16[3328,1024]{1,0:T(8,128)(2,1)}, bf16[1024,3328]{1,0:T(8,128)(2,1)}, bf16[1024,3328]{1,0:T(8,128)(2,1)}, bf16[1024,1024]{1,0:T(8,128)(2,1)}) custom-call(bf16[1024,1024]{1,0:T(8,128)(2,1)} %get-tuple-element.33.h, bf16[1024,1024]{1,0:T(8,128)(2,1)} %bitcast.21, bf16[2,1024,3328]{2,1,0:T(8,128)(2,1)} %wg2.1, bf16[2,1024,3328]{2,1,0:T(8,128)(2,1)} %wu2.1, ...), custom_call_target="tpu_custom_call" | custom-call | tf_op jit(solution)/shard_map/layer1/pallas_call | solution.py:226
  110.1 132.8 %reduce_scatter.1 = (bf16[2,8,1664]{2,1,0:T(8,128)(2,1)}, bf16[2,8,1664]{2,1,0:T(8,128)(2,1)}, bf16[2,2,16,512]{3,2,1,0:T(8,128)(2,1)}, f32[2,4,3328]{2,1,0:T(4,...) custom-call(bf16[4,4,8,8,3328]{4,3,2,1,0:T(8,128)(2,1)} %bitcast.20,, ...), custom_call_target="tpu_custom_call" | custom-call | tf_op jit(solution)/shard_map/reduce_scatter/pallas_call | solution.py:797
  242.9 0.0 copy-start
  243.0 0.8 copy-done
  243.8 0.0 copy-start.1
  243.8 0.8 copy-done.1
  244.6 0.0 copy-start.2
  244.6 0.8 copy-done.2
  245.4 92.4 %all_gather.1 = (bf16[2,4,4,8,8,3328]{5,4,3,2,1,0:T(8,128)(2,1)S(1)}, bf16[2,4,4,8,8,3328]{5,4,3,2,1,0:T(8,128)(2,1)S(1)}, bf16[2,4,4,26,8,1024]{5,4,3,2,1,0:T(8,128)(2,1)S(1)}) custom-call(bf16[2,8,1664]{2,1,0:T(8,128)(2,1)S(1)} %copy-done.1, bf16[2,8,1664]{2,1,0:T(8,128)(2,1)S(1)} %copy-done.2, bf16[2,2,16,512]{3,2,1,0:T(8,128)(2,1)S(1)} %copy-done), custom_call_target="tpu_custom_call" | custom-call | tf_op jit(solution)/shard_map/all_gather/pallas_call | solution.py:959
  337.8 0.0 copy-start.8
  337.8 0.0 copy-start.7
  337.8 0.0 copy-start.6
  337.8 0.0 copy-start.5
  337.8 0.0 copy-start.4
  337.8 0.0 copy-start.3
  337.8 13.3 %settle.1 = (bf16[2,4,4,8,8,3328]{5,4,3,2,1,0:T(8,128)(2,1)}, bf16[2,4,4,8,8,3328]{5,4,3,2,1,0:T(8,128)(2,1)}, bf16[2,4,4,26,8,1024]{5,4,3,2,1,0:T(8,128)(2,1)}) custom-call(bf16[2,4,4,8,8,3328]{5,4,3,2,1,0:T(8,128)(2,1)S(1)} %get-tuple-element.45.refs_0_, bf16[2,4,4,8,8,3328]{5,4,3,2,1,0:T(8,128)(2,1)S(1)} %get-tuple-element.46.refs_1_, ...), custom_call_target="tpu_custom_call" | custom-call | tf_op jit(solution)/shard_map/settle/pallas_call | solution.py:975
  351.2 0.0 copy-done.8
  351.2 0.6 copy.26
  351.8 0.0 copy-done.7
  351.8 0.6 copy.27
  352.5 0.0 copy-done.6
  352.5 0.6 copy.28
  353.1 0.0 copy-done.5
  353.1 0.6 copy.29
  353.8 0.0 copy-done.4
  353.8 0.6 copy.30
  354.4 0.0 copy-done.3
  354.4 0.6 copy.31
Async XLA Ops:
  242.9 0.8 copy-start
  243.8 0.8 copy-start.1
  244.6 0.8 copy-start.2
  337.8 13.4 %copy-start.8 = (f32[2,4,3328]{2,1,0:T(4,128)S(1)}, f32[2,4,3328]{2,1,0:T(4,128)}, u32[]{:S(2)}) copy-start(f32[2,4,3328]{2,1,0:T(4,128)} %get-tuple-element.69) | copy-start | bytes 319492
  337.8 14.0 %copy-start.7 = (f32[2,4,3328]{2,1,0:T(4,128)S(1)}, f32[2,4,3328]{2,1,0:T(4,128)}, u32[]{:S(2)}) copy-start(f32[2,4,3328]{2,1,0:T(4,128)} %get-tuple-element.70) | copy-start | bytes 319492
  337.8 14.7 %copy-start.6 = (f32[13,2,1024]{2,1,0:T(2,128)S(1)}, f32[13,2,1024]{2,1,0:T(2,128)}, u32[]{:S(2)}) copy-start(f32[13,2,1024]{2,1,0:T(2,128)} %get-tuple-element.53) | copy-start | bytes 319492
  337.8 15.3 %copy-start.5 = (f32[2,4,3328]{2,1,0:T(4,128)S(1)}, f32[2,4,3328]{2,1,0:T(4,128)}, u32[]{:S(2)}) copy-start(f32[2,4,3328]{2,1,0:T(4,128)} %get-tuple-element.72) | copy-start | bytes 319492
  337.8 15.9 %copy-start.4 = (f32[2,4,3328]{2,1,0:T(4,128)S(1)}, f32[2,4,3328]{2,1,0:T(4,128)}, u32[]{:S(2)}) copy-start(f32[2,4,3328]{2,1,0:T(4,128)} %get-tuple-element.73) | copy-start | bytes 319492
  337.8 16.6 %copy-start.3 = (f32[13,2,1024]{2,1,0:T(2,128)S(1)}, f32[13,2,1024]{2,1,0:T(2,128)}, u32[]{:S(2)}) copy-start(f32[13,2,1024]{2,1,0:T(2,128)} %get-tuple-element.56) | copy-start | bytes 319492

commit v6 on v5

--- a/solution.py
+++ b/solution.py
@@ -390,10 +390,10 @@
     weights = {a: refs[8 + j] for j, a in enumerate("ugd")}
     w_down = refs[11]
     moments = {a: (refs[12 + j], refs[15 + j]) for j, a in enumerate("ugd")}
-    new = {a: refs[18 + j] for j, a in enumerate("ugd")}
-    new_moments = {a: (refs[21 + j], refs[24 + j]) for j, a in enumerate("ugd")}
-    made = {a: refs[27 + j] for j, a in enumerate("ugd")}
-    S = dict(zip(names, refs[30:], strict=True))
+    new = {"u": refs[18].at[0], "g": refs[18].at[1], "d": refs[19]}
+    new_moments = {a: (refs[20 + j], refs[23 + j]) for j, a in enumerate("ugd")}
+    made = {a: refs[26 + j] for j, a in enumerate("ugd")}
+    S = dict(zip(names, refs[29:], strict=True))
     at = coords()
     c, x = at["c"], at["x"]
     sib = device({**at, "c": 1 - c})
@@ -448,11 +448,6 @@
         cp.start()
         pend.append(make)
         return cp
-    for j, a in enumerate("ugd"):
-        for q in (0, 1):
-            moment_copies.append(remote(lambda j=j, a=a, q=q: remote_copy(
-                moments[a][q].at[:, :, halfcols(a, 0)], S["mv_" + a].at[q, c], S["mvsem"].at[j, q, 0], S["mvsem"].at[j, q, 1], sib)))
-
     def region(ref, i, level, v):
         l, a, col, n, o = UNITS[i]
         idx = view(a, o, at, level, v)
@@ -492,6 +487,11 @@
         ref = landing(i, off)
         return remote_copy(ref, ref, S["ds"].at[jobs[i, off]], S["dr"].at[jobs[i, off]], sib)
     exchange(1)
+    for j, a in enumerate("ugd"):
+        for q in (0, 1):
+            moment_copies.append(remote(lambda j=j, a=a, q=q: remote_copy(
+                moments[a][q].at[:, :, halfcols(a, 0)], S["mv_" + a].at[q, c], S["mvsem"].at[j, q, 0], S["mvsem"].at[j, q, 1], sib)))
+
     sib_waited = set()
 
     def wait_terms(i, off):
@@ -792,12 +792,12 @@
     args += [w.reshape(2, 4, 4, -1, 8, w.shape[-1]) for w in weights] + [w_down, *m, *v]
     sh = rs_scratch()
     any_ = pl.BlockSpec(memory_space=pl.ANY)
-    outs = [jax.ShapeDtypeStruct(s, BF) for s in ((2, 8, 1664), (2, 8, 1664), (2, 2, 16, 512))] + [jax.ShapeDtypeStruct(t.shape, F32) for t in (*m, *v)]
+    outs = [jax.ShapeDtypeStruct(s, BF) for s in ((2, 2, 8, 1664), (2, 2, 16, 512))] + [jax.ShapeDtypeStruct(t.shape, F32) for t in (*m, *v)]
     outs += [jax.ShapeDtypeStruct(s, BF) for s in ((4, 4, 8, 8, 3328), (4, 4, 8, 8, 3328), (4, 104, 8, 1024))]
     outs = pl.pallas_call(
-        functools.partial(rs_kernel, list(sh)), out_shape=outs, in_specs=[any_] * 18, out_specs=[any_] * 12, scratch_shapes=list(sh.values()), name="reduce_scatter",
+        functools.partial(rs_kernel, list(sh)), out_shape=outs, in_specs=[any_] * 18, out_specs=[any_] * 11, scratch_shapes=list(sh.values()), name="reduce_scatter",
         compiler_params=pltpu.CompilerParams(collective_id=0, has_side_effects=True, vmem_limit_bytes=VMEM_BYTES))(*args)
-    return outs[:3], outs[3:6], outs[6:9]
+    return outs[:2], outs[2:5], outs[5:8]
 
 
 def plan_ag():
@@ -856,9 +856,9 @@
 
 
 def ag_kernel(names, *refs):
-    own = {a: refs[j] for j, a in enumerate("ugd")}
-    out = {a: refs[3 + j] for j, a in enumerate("ugd")}
-    S = dict(zip(names, refs[6:], strict=True))
+    own = {"u": refs[0].at[0], "g": refs[0].at[1], "d": refs[1]}
+    out = {a: refs[2 + j] for j, a in enumerate("ugd")}
+    S = dict(zip(names, refs[5:], strict=True))
     at = coords()
     c, x, y, z = at["c"], at["x"], at["y"], at["z"]
     sib = device({**at, "c": 1 - c})
@@ -952,13 +952,13 @@
         cp.wait_send()
 
 
-def all_gather(u, g, d):
+def all_gather(ug, d):
     sh = ag_scratch()
     any_ = pl.BlockSpec(memory_space=pl.ANY)
     outs = [jax.ShapeDtypeStruct((2, 4, 4, TILES[a], 8, 2 * WIDTH[a]), BF) for a in "ugd"]
     return pl.pallas_call(
-        functools.partial(ag_kernel, list(sh)), out_shape=outs, in_specs=[pl.BlockSpec(memory_space=pltpu.HBM)] * 3, out_specs=[any_] * 3, scratch_shapes=list(sh.values()), name="all_gather",
-        compiler_params=pltpu.CompilerParams(collective_id=1, has_side_effects=True, vmem_limit_bytes=AG_VMEM))(u, g, d)
+        functools.partial(ag_kernel, list(sh)), out_shape=outs, in_specs=[any_] * 2, out_specs=[any_] * 3, scratch_shapes=list(sh.values()), name="all_gather",
+        compiler_params=pltpu.CompilerParams(collective_id=1, has_side_effects=True, vmem_limit_bytes=AG_VMEM))(ug, d)
 
 
 def settle_kernel(*refs):

time: 356 us -> 355 us (level)
  no operation moved by 1% of the time
where the time goes in v6:
time: 355 us; the launch traced here: 354 us
  Pallas kernels  348 us (98%)
  local copies, waits for them, and re-layouts  5.61 us (2%)
    pallas_call x1, Pallas kernels, reduce_scatter(): pl.pallas_call(functools.partial(rs_kernel, list(sh)), out_shape=outs, in...  133 us
    pallas_call x1, Pallas kernels, all_gather(): pl.pallas_call(functools.partial(ag_kernel, list(sh)), out_shape=outs, in...  92.3 us
    pallas_call x1, Pallas kernels, layer1(): pl.pallas_call(both1, grid=(N + 4,), in_specs=[whole, whole, wcols, wcols...  72.9 us
    pallas_call x1, Pallas kernels, layer0(): pl.pallas_call(functools.partial(fwd0, C, tr), grid=(N + 4,), in_specs=[w...  36.6 us
    pallas_call x1, Pallas kernels, settle(): pl.pallas_call(settle_kernel, out_shape=[jax.ShapeDtypeStruct(t.shape, t....  13.3 us

profile of v6, /device:TPU:1, one launch (start us, length us, event | category | flops | bytes accessed | tf_op | source)
XLA Modules:
  0.0 354.2 jit_solution(8564535661738843369)
XLA Ops:
  0.6 36.6 %layer0.1 = (f32[13,1024,256]{2,1,0:T(8,128)}, f32[13,1024,256]{2,1,0:T(8,128)}, bf16[3328,1024]{1,0:T(8,128)(2,1)}, bf16[1024,1024]{1,0:T(8,128)(2,1)}, bf16[1024,1024]{1,0:T(8,128)(2,1)}) custom-call(bf16[1024,1024]{1,0:T(8,128)(2,1)} %bitcast.22, bf16[2,1024,3328]{2,1,0:T(8,128)(2,1)} %wg2.1, bf16[2,1024,3328]{2,1,0:T(8,128)(2,1)} %wu2.1, ...), custom_call_target="tpu_custom_call" | custom-call | tf_op jit(solution)/shard_map/layer0/pallas_call | solution.py:155
  37.2 72.9 %layer1.1 = (bf16[3328,1024]{1,0:T(8,128)(2,1)}, bf16[1024,3328]{1,0:T(8,128)(2,1)}, bf16[1024,3328]{1,0:T(8,128)(2,1)}, bf16[1024,1024]{1,0:T(8,128)(2,1)}) custom-call(bf16[1024,1024]{1,0:T(8,128)(2,1)} %get-tuple-element.32.h, bf16[1024,1024]{1,0:T(8,128)(2,1)} %bitcast.21, bf16[2,1024,3328]{2,1,0:T(8,128)(2,1)} %wg2.1, bf16[2,1024,3328]{2,1,0:T(8,128)(2,1)} %wu2.1, ...), custom_call_target="tpu_custom_call" | custom-call | tf_op jit(solution)/shard_map/layer1/pallas_call | solution.py:226
  110.1 132.8 %reduce_scatter.1 = (bf16[2,2,8,1664]{3,2,1,0:T(8,128)(2,1)}, bf16[2,2,16,512]{3,2,1,0:T(8,128)(2,1)}, f32[2,4,3328]{2,1,0:T(4,128)}, f32[2,4,3328]{2,1,0:T(4,12...) custom-call(bf16[4,4,8,8,3328]{4,3,2,1,0:T(8,128)(2,1)} %bitcast.20,, ...), custom_call_target="tpu_custom_call" | custom-call | tf_op jit(solution)/shard_map/reduce_scatter/pallas_call | solution.py:797
  242.9 0.0 copy-start
  242.9 0.9 copy-done
  243.8 0.0 copy-start.1
  243.8 0.8 copy-done.1
  244.6 92.3 %all_gather.1 = (bf16[2,4,4,8,8,3328]{5,4,3,2,1,0:T(8,128)(2,1)S(1)}, bf16[2,4,4,8,8,3328]{5,4,3,2,1,0:T(8,128)(2,1)S(1)}, bf16[2,4,4,26,8,1024]{5,4,3,2,1,0:T(8,128)(2,1)S(1)}) custom-call(bf16[2,2,8,1664]{3,2,1,0:T(8,128)(2,1)S(1)} %copy-done, bf16[2,2,16,512]{3,2,1,0:T(8,128)(2,1)S(1)} %copy-done.1), custom_call_target="tpu_custom_call" | custom-call | tf_op jit(solution)/shard_map/all_gather/pallas_call | solution.py:959
  336.9 0.0 copy-start.7
  337.0 0.0 copy-start.6
  337.0 0.0 copy-start.5
  337.0 0.0 copy-start.4
  337.0 0.0 copy-start.3
  337.0 0.0 copy-start.2
  337.0 13.3 %settle.1 = (bf16[2,4,4,8,8,3328]{5,4,3,2,1,0:T(8,128)(2,1)}, bf16[2,4,4,8,8,3328]{5,4,3,2,1,0:T(8,128)(2,1)}, bf16[2,4,4,26,8,1024]{5,4,3,2,1,0:T(8,128)(2,1)}) custom-call(bf16[2,4,4,8,8,3328]{5,4,3,2,1,0:T(8,128)(2,1)S(1)} %get-tuple-element.43.refs_0_, bf16[2,4,4,8,8,3328]{5,4,3,2,1,0:T(8,128)(2,1)S(1)} %get-tuple-element.44.refs_1_, ...), custom_call_target="tpu_custom_call" | custom-call | tf_op jit(solution)/shard_map/settle/pallas_call | solution.py:975
  350.3 0.0 copy-done.7
  350.3 0.6 copy.26
  351.0 0.0 copy-done.6
  351.0 0.6 copy.27
  351.6 0.0 copy-done.5
  351.6 0.6 copy.28
  352.3 0.0 copy-done.4
  352.3 0.6 copy.29
  352.9 0.0 copy-done.3
  352.9 0.6 copy.30
  353.6 0.0 copy-done.2
  353.6 0.6 copy.31
Async XLA Ops:
  242.9 0.9 copy-start
  243.8 0.8 copy-start.1
  336.9 13.4 %copy-start.7 = (f32[2,4,3328]{2,1,0:T(4,128)S(1)}, f32[2,4,3328]{2,1,0:T(4,128)}, u32[]{:S(2)}) copy-start(f32[2,4,3328]{2,1,0:T(4,128)} %get-tuple-element.67) | copy-start | bytes 319492
  337.0 14.0 %copy-start.6 = (f32[2,4,3328]{2,1,0:T(4,128)S(1)}, f32[2,4,3328]{2,1,0:T(4,128)}, u32[]{:S(2)}) copy-start(f32[2,4,3328]{2,1,0:T(4,128)} %get-tuple-element.68) | copy-start | bytes 319492
  337.0 14.7 %copy-start.5 = (f32[13,2,1024]{2,1,0:T(2,128)S(1)}, f32[13,2,1024]{2,1,0:T(2,128)}, u32[]{:S(2)}) copy-start(f32[13,2,1024]{2,1,0:T(2,128)} %get-tuple-element.51) | copy-start | bytes 319492
  337.0 15.3 %copy-start.4 = (f32[2,4,3328]{2,1,0:T(4,128)S(1)}, f32[2,4,3328]{2,1,0:T(4,128)}, u32[]{:S(2)}) copy-start(f32[2,4,3328]{2,1,0:T(4,128)} %get-tuple-element.70) | copy-start | bytes 319492
  337.0 15.9 %copy-start.3 = (f32[2,4,3328]{2,1,0:T(4,128)S(1)}, f32[2,4,3328]{2,1,0:T(4,128)}, u32[]{:S(2)}) copy-start(f32[2,4,3328]{2,1,0:T(4,128)} %get-tuple-element.71) | copy-start | bytes 319492
  337.0 16.6 %copy-start.2 = (f32[13,2,1024]{2,1,0:T(2,128)S(1)}, f32[13,2,1024]{2,1,0:T(2,128)}, u32[]{:S(2)}) copy-start(f32[13,2,1024]{2,1,0:T(2,128)} %get-tuple-element.54) | copy-start | bytes 319492
